TPU v7x, 256 devices: a whole 4x4x8 slice. The times are simulated.
256 devices in a mesh: dp: 64 (over z, y_lo, x), tensor: 4 (over y_hi, core).
Axes of the slice: x: 4, y: 4 (y_hi: 2, y_lo: 2; y = y_hi * 2 + y_lo), z: 8, core: 2. Of those that a mesh axis runs over, the one named last changes fastest.
Arguments:
- out_first: bfloat16 [64, 197, 1024], P('dp', None, 'tensor'), may hold values from -6 to 6
- out_second: bfloat16 [64, 197, 1024], P('dp', None, 'tensor'), may hold values from -6 to 6
- grad_first: bfloat16 [64, 197, 1024], P('dp', None, 'tensor'), may hold values from -6 to 6
- grad_second: bfloat16 [64, 197, 1024], P('dp', None, 'tensor'), may hold values from -16 to 16
- gain_attn: float32 [1024], replicated, may hold values from 0.25 to 1.75
- gain_mlp: float32 [1024], replicated, may hold values from 0.25 to 1.75
- qkv_weight: bfloat16 [1024, 3, 1024], P(None, None, 'tensor'), may hold values from -1 to 1
- proj_weight: bfloat16 [1024, 1024], P(None, 'tensor'), may hold values from -0.1875 to 0.1875
- inner_weight: bfloat16 [1024, 4096], P(None, 'tensor'), may hold values from -0.1875 to 0.1875
- inner_bias: float32 [4096], P('tensor'), may hold values from -3 to 3
- outer_weight: bfloat16 [1024, 4096], P(None, 'tensor'), may hold values from -0.09375 to 0.09375
Outputs:
- input_first: bfloat16 [64, 197, 1024], P('dp', None, 'tensor')
- input_second: bfloat16 [64, 197, 1024], P('dp', None, 'tensor')
- back_first: bfloat16 [64, 197, 1024], P('dp', None, 'tensor')
- back_second: bfloat16 [64, 197, 1024], P('dp', None, 'tensor')
- grad_qkv: float32 [1024, 3, 1024], P('dp', None, 'tensor')
- grad_proj: float32 [1024, 1024], P('dp', 'tensor')
- grad_inner: float32 [1024, 4096], P('dp', 'tensor')
- grad_bias: float32 [4096], P('tensor')
- grad_outer: float32 [1024, 4096], P('dp', 'tensor')
- grad_gain_attn: float32 [1024], P('tensor')
- grad_gain_mlp: float32 [1024], P('tensor')
All inputs are finite; a program needn't handle non-finite values.
Results may differ from a plain program's by a relative error of at most 0.016.
Values may be sent and summed in bfloat16 or wider, within the bound.
No kernel may reach another device: no remote copies, remote signals or barrier semaphores. Data moves between devices by JAX's collectives and lax.ppermute only.
A program may use at most 64 MiB of HBM per device.

v0:
```python
import jax
import jax.numpy as jnp
from jax import lax
from jax.sharding import Mesh
from jax.sharding import PartitionSpec as P

D = 1024
HEADS = 16
DP = ("dp_0", "dp_1", "dp_2")


epsilon = 1e-06


def split_up(x, dim, devices):
    dims = x.shape
    pieces = x.reshape(*dims[:dim], devices, dims[dim] // devices, *dims[dim + 1 :])
    return jnp.moveaxis(pieces, dim, 0)


def summed_on_arrival(x, axis, dim):
    pieces = split_up(x, dim, lax.axis_size(axis))
    arrived = lax.all_to_all(pieces, axis, split_axis=0, concat_axis=0, tiled=True)
    return arrived.astype(jnp.float32).sum(axis=0)


def sent_to_all(x, axis):
    copies = jnp.broadcast_to(x, (lax.axis_size(axis), *x.shape))
    return lax.all_to_all(copies, axis, split_axis=0, concat_axis=0, tiled=True)


def of_everyone(x, axis):
    everything = sent_to_all(x, axis)
    return jnp.sum(everything, axis=0)


def packed_total(arrays, axis):
    flat, at, finished = (jnp.concatenate([a.reshape(-1) for a in arrays]), 0, [])
    subtotal = of_everyone(flat, axis)
    for a in arrays:
        finished.append(subtotal[at : at + a.size].reshape(a.shape))
        at += a.size
    return tuple(finished)


def side_by_side(arrays, axis, dim, along):
    widths = [a.shape[along] for a in arrays]
    both = jnp.concatenate(arrays, axis=along)
    whole = lax.all_gather(both, axis, axis=dim, tiled=True)
    return tuple(jnp.split(whole, [sum(widths[:k]) for k in range(1, len(widths))], axis=along))


def summed_on_arrival_2(x, axis, dim):
    devices = lax.axis_size(axis)
    pieces = lax.all_to_all(split_up(x, dim, devices), axis, 0, 0, tiled=True)
    return jnp.sum(pieces, axis=0)


def sum_in_order(pieces, axes, order):
    inside = pieces.shape[1:]
    pieces = pieces.reshape(*(lax.axis_size(a) for a in axes), *inside)
    pieces = jnp.moveaxis(pieces, order, range(len(axes))).reshape(-1, *inside)
    for k in order:
        pieces = lax.psum_scatter(pieces, axes[k], scatter_dimension=0, tiled=True)
    return pieces[0]


def scatter_axes(x, axes, order, dim):
    devices = lax.axis_size(axes)
    return sum_in_order(split_up(x, dim, devices), axes, order)


def normalize(values):
    centre = values - jnp.mean(values, -1, keepdims=True)
    spread = lax.rsqrt(jnp.mean(centre * centre, -1, keepdims=True) + epsilon)
    return (centre * spread, spread)


def weight_term(left_rows, right_rows):
    return lax.dot_general(
        left_rows, right_rows, (((0,), (0,)), ((), ())), preferred_element_type=jnp.float32
    )


def norm_backward(grad_part, normed, spread, gain, offset, local_width):
    full_width = normed.shape[1]
    own_part = summed_on_arrival(grad_part.astype(jnp.bfloat16), "tensor", 1)
    own_normed = lax.dynamic_slice_in_dim(normed, offset, local_width, 1)
    own_gain = lax.dynamic_slice_in_dim(gain, offset, local_width, 0)
    scaled = own_part * own_gain
    totals = packed_total((jnp.sum(scaled, 1), jnp.sum(scaled * own_normed, 1)), "tensor")
    first_mean = totals[0][:, None] / full_width
    second_mean = totals[1][:, None] / full_width
    back_rows = spread * (scaled - first_mean - own_normed * second_mean)
    return (back_rows, jnp.sum(own_part * own_normed, 0))


def on_device(
    out_first,
    out_second,
    grad_first,
    grad_second,
    gain_attn,
    gain_mlp,
    qkv_weight,
    proj_weight,
    inner_weight,
    inner_bias,
    outer_weight,
):
    images, length, local_width = out_first.shape
    full_width = local_width * lax.axis_size("tensor")
    rows_all = images * length
    head_dim = D // HEADS
    local_heads = local_width // head_dim
    factor = head_dim ** (-0.5)
    shard_rows = full_width // lax.axis_size(DP)
    offset = lax.axis_index("tensor") * local_width
    hidden_width = inner_weight.shape[1]
    whole_first, whole_lower = side_by_side((out_first, grad_second), "tensor", 2, 0)
    first_rows = whole_first.reshape(rows_all, full_width).astype(jnp.float32)
    lower_grad = whole_lower.reshape(rows_all, full_width)
    normed_mlp, spread_mlp = normalize(first_rows)
    input_mlp = (normed_mlp * gain_mlp).astype(jnp.bfloat16)
    hidden = jnp.dot(input_mlp, inner_weight, preferred_element_type=jnp.float32) + inner_bias
    active = jax.nn.gelu(hidden).astype(jnp.bfloat16)
    mlp_part = summed_on_arrival_2(
        jnp.dot(active, outer_weight.T, preferred_element_type=jnp.float32), "tensor", 1
    )
    input_second = (
        out_second.reshape(rows_all, local_width).astype(jnp.float32) - mlp_part
    ).astype(jnp.bfloat16)
    grad_active = jnp.dot(lower_grad, outer_weight, preferred_element_type=jnp.float32)
    grad_hidden = jax.vjp(jax.nn.gelu, hidden)[1](grad_active)[0].astype(jnp.bfloat16)
    bias_part = jnp.sum(grad_hidden.astype(jnp.float32), 0)
    grad_norm_mlp = jnp.dot(grad_hidden, inner_weight.T, preferred_element_type=jnp.float32)
    back_mlp, gain_mlp_part = norm_backward(
        grad_norm_mlp, normed_mlp, spread_mlp, gain_mlp, offset, local_width
    )
    back_first = (grad_first.reshape(rows_all, local_width).astype(jnp.float32) + back_mlp).astype(
        jnp.bfloat16
    )
    whole_second, whole_back = side_by_side(
        (
            input_second.reshape(images, length, local_width),
            back_first.reshape(images, length, local_width),
        ),
        "tensor",
        2,
        0,
    )
    normed_attn, spread_attn = normalize(
        whole_second.reshape(rows_all, full_width).astype(jnp.float32)
    )
    input_attn = (normed_attn * gain_attn).astype(jnp.bfloat16)
    back_rows_all = whole_back.reshape(rows_all, full_width)
    qkv_rows = jnp.einsum(
        "td,dcj->tcj", input_attn, qkv_weight, preferred_element_type=jnp.float32
    ).astype(jnp.bfloat16)
    shaped = qkv_rows.reshape(images, length, 3, local_heads, head_dim)
    queries = shaped[:, :, 0]
    key_rows = shaped[:, :, 1]
    value_rows = shaped[:, :, 2]
    grad_heads = (
        jnp.dot(back_rows_all, proj_weight, preferred_element_type=jnp.float32)
        .astype(jnp.bfloat16)
        .reshape(images, length, local_heads, head_dim)
    )
    scores = (
        jnp.einsum("bqhe,bkhe->bhqk", queries, key_rows, preferred_element_type=jnp.float32)
        * factor
    )
    attn_probs = jax.nn.softmax(scores, -1)
    probs_low = attn_probs.astype(jnp.bfloat16)
    heads_out = jnp.einsum(
        "bhqk,bkhe->bqhe", probs_low, value_rows, preferred_element_type=jnp.float32
    ).astype(jnp.bfloat16)
    grad_probs = jnp.einsum(
        "bqhe,bkhe->bhqk", grad_heads, value_rows, preferred_element_type=jnp.float32
    )
    grad_value = jnp.einsum(
        "bhqk,bqhe->bkhe", probs_low, grad_heads, preferred_element_type=jnp.float32
    ).astype(jnp.bfloat16)
    row_dot = jnp.sum(grad_probs * attn_probs, -1, keepdims=True)
    grad_scores = (attn_probs * (grad_probs - row_dot)).astype(jnp.bfloat16)
    grad_query = (
        jnp.einsum("bhqk,bkhe->bqhe", grad_scores, key_rows, preferred_element_type=jnp.float32)
        * factor
    ).astype(jnp.bfloat16)
    grad_key = (
        jnp.einsum("bhqk,bqhe->bkhe", grad_scores, queries, preferred_element_type=jnp.float32)
        * factor
    ).astype(jnp.bfloat16)
    grad_rows = jnp.stack([grad_query, grad_key, grad_value], 2).reshape(rows_all, 3 * local_width)
    attn_rows = heads_out.reshape(rows_all, local_width)
    attn_part = summed_on_arrival(
        jnp.dot(attn_rows, proj_weight.T, preferred_element_type=jnp.float32).astype(jnp.bfloat16),
        "tensor",
        1,
    )
    input_first = (out_first.reshape(rows_all, local_width).astype(jnp.float32) - attn_part).astype(
        jnp.bfloat16
    )
    flat_qkv = qkv_weight.reshape(full_width, 3 * local_width)
    grad_norm_attn = jnp.dot(grad_rows, flat_qkv.T, preferred_element_type=jnp.float32)
    back_attn, gain_attn_part = norm_backward(
        grad_norm_attn, normed_attn, spread_attn, gain_attn, offset, local_width
    )
    back_second = (
        grad_second.reshape(rows_all, local_width).astype(jnp.float32) + back_attn
    ).astype(jnp.bfloat16)
    joined = scatter_axes(
        jnp.concatenate(
            [
                weight_term(input_attn, grad_rows),
                weight_term(back_rows_all, attn_rows),
                weight_term(input_mlp, grad_hidden),
                weight_term(lower_grad, active),
            ],
            1,
        ).astype(jnp.bfloat16),
        DP,
        (0, 2, 1),
        0,
    ).astype(jnp.float32)
    grad_qkv = joined[:, : 3 * local_width]
    grad_proj = joined[:, 3 * local_width : 4 * local_width]
    grad_inner = joined[:, 4 * local_width : 4 * local_width + hidden_width]
    grad_outer = joined[:, 4 * local_width + hidden_width :]
    summed_small = packed_total((gain_attn_part, gain_mlp_part, bias_part), DP)
    shape_out = (images, length, local_width)
    return (
        input_first.reshape(shape_out),
        input_second.reshape(shape_out),
        back_first.reshape(shape_out),
        back_second.reshape(shape_out),
        grad_qkv.reshape(shard_rows, 3, local_width),
        grad_proj,
        grad_inner,
        summed_small[2],
        grad_outer,
        summed_small[0],
        summed_small[1],
    )


def solution(mesh):
    split = Mesh(
        mesh.devices.reshape(8, 2, 4, mesh.shape["tensor"]), ("dp_0", "dp_1", "dp_2", "tensor")
    )
    return jax.shard_map(
        on_device,
        mesh=split,
        in_specs=(
            P(DP, None, "tensor"),
            P(DP, None, "tensor"),
            P(DP, None, "tensor"),
            P(DP, None, "tensor"),
            P(),
            P(),
            P(None, None, "tensor"),
            P(None, "tensor"),
            P(None, "tensor"),
            P("tensor"),
            P(None, "tensor"),
        ),
        out_specs=(
            P(DP, None, "tensor"),
            P(DP, None, "tensor"),
            P(DP, None, "tensor"),
            P(DP, None, "tensor"),
            P(DP, None, "tensor"),
            P(DP, "tensor"),
            P(DP, "tensor"),
            P("tensor"),
            P(DP, "tensor"),
            P("tensor"),
            P("tensor"),
        ),
        check_vma=False,
    )
```

profile of v0, /device:TPU:1, one launch (start us, length us, event | category | flops | bytes accessed | tf_op | source)
XLA Modules:
  0.0 252.3 jit_solution(8271185419312058462)
XLA Ops:
  7.2 1.1 pad_maximum_fusion.1
  8.3 12.0 %all_gather.6 = bf16[2,197,1024]{2,1,0:T(8,128)(2,1)S(1)} all-gather(bf16[2,197,256]{2,1,0:T(8,128)(2,1)S(1)} %pad_maximum_fusion.1), channel_id=1, replica_groups=mesh['dp_0'=8,'dp_1'=2,'dp_2'=4,'tensor'=4] {'tensor'}, dimensions={2}, use_global_device_ids=true | all-gather | bytes 1008640 | tf_op jit(solution)/shard_map/all_gather | solution.py:49
  21.5 1.6 convert_reduce_fusion.2
  25.7 1.8 copy.158
  27.5 4.2 %all-to-all-start.1 = ((bf16[4,197,256]{2,1,0:T(8,128)(2,1)}), bf16[4,197,256]{2,1,0:T(8,128)(2,1)}, u32[]{:S(2)}, u32[]{:S(2)}) async-start(bf16[4,197,256]{2,1,0:T(8,128)(2,1)} %bitcast.199), calls=%async_computation.1 | async-start | bytes 819200 | tf_op jit(solution)/shard_map/all_to_all | solution.py:23
  31.7 1.3 fusion.45
  33.4 2.9 %fusion.51 = f32[197,1024]{1,0:T(8,128)} fusion(bf16[1024,1024]{1,0:T(8,128)(2,1)S(1)} %copy-done, f32[197,1024]{1,0:T(8,128)} %copy-done.21), kind=kOutput, calls=%fused_computation.116 | convolution fusion | flops 414954496 | bytes 3710976 | tf_op jit(solution)/shard_map/dot_general | solution.py:128
  36.3 3.7 %all-to-all-done.1 = bf16[4,197,256]{2,1,0:T(8,128)(2,1)} async-done(((bf16[4,197,256]{2,1,0:T(8,128)(2,1)}), bf16[4,197,256]{2,1,0:T(8,128)(2,1)}, u32[]{:S(2)}, u32[]{:S(2)}) %all-to-all-start.1) | async-done | bytes 403488 | tf_op jit(solution)/shard_map/all_to_all | solution.py:23
  41.7 1.7 multiply_reduce_fusion.1
  44.1 4.2 %all-to-all-start.2 = ((f32[4,1,394]{2,1,0:T(1,128)}), f32[4,1,394]{2,1,0:T(1,128)S(1)}, u32[]{:S(2)}, u32[]{:S(2)}) async-start(f32[4,1,394]{2,1,0:T(1,128)} %broadcast_in_dim.6), calls=%async_computation.2 | async-start | bytes 16384 | tf_op jit(solution)/shard_map/all_to_all | solution.py:29
  48.3 3.3 %convolution_convert_fusion = bf16[8,2,4,16,1024]{4,3,2,1,0:T(8,128)(2,1)} fusion(bf16[8,2,4,16,197]{4,3,2,1,0:T(8,128)(2,1)S(1)} %bitcast.216, f32[197,1024]{1,0:T(8,128)} %copy-done.21), kind=kOutput, calls=%fused_computation.2 | convolution fusion | flops 416003072 | bytes 3307520 | tf_op jit(solution)/shard_map/dot_general | solution.py:80
  51.6 1.5 reshape.232
  54.2 1.2 copy.121
  55.4 4.8 %all-to-all-start = ((f32[4,197,256]{2,1,0:T(8,128)}), f32[4,197,256]{2,1,0:T(8,128)S(1)}, u32[]{:S(2)}, u32[]{:S(2)}) async-start(f32[4,197,256]{2,1,0:T(8,128)} %bitcast.196), calls=%async_computation | async-start | bytes 1638400 | tf_op jit(solution)/shard_map/all_to_all | solution.py:55
  60.2 3.0 %convolution_convert_fusion.1 = bf16[8,2,4,16,1024]{4,3,2,1,0:T(8,128)(2,1)} fusion(bf16[8,2,4,16,197]{4,3,2,1,0:T(8,128)(2,1)S(1)} %bitcast.207, bf16[197,1024]{1,0:T(8,128)(2,1)} %copy-done.5), kind=kOutput, calls=%fused_computation.3 | convolution fusion | flops 414187520 | bytes 2904064 | tf_op jit(solution)/shard_map/dot_general | solution.py:80
  63.4 1.3 fusion.47
  64.6 8.1 %all-to-all-done = f32[4,197,256]{2,1,0:T(8,128)S(1)} async-done(((f32[4,197,256]{2,1,0:T(8,128)}), f32[4,197,256]{2,1,0:T(8,128)S(1)}, u32[]{:S(2)}, u32[]{:S(2)}) %all-to-all-start) | async-done | bytes 806944 | tf_op jit(solution)/shard_map/all_to_all | solution.py:55
  73.5 10.6 %all_gather.7 = bf16[2,197,1024]{2,1,0:T(8,128)(2,1)S(1)} all-gather(bf16[2,197,256]{2,1,0:T(8,128)(2,1)S(1)} %pad_maximum_fusion.2), channel_id=1, replica_groups=mesh['dp_0'=8,'dp_1'=2,'dp_2'=4,'tensor'=4] {'tensor'}, dimensions={2}, use_global_device_ids=true | all-gather | bytes 1008640 | tf_op jit(solution)/shard_map/all_gather | solution.py:49
  84.5 1.3 convolution_convert_fusion.7
  85.8 1.1 copy.106
  87.0 1.4 fusion.56
  88.3 1.2 convolution_convert_fusion.9
  89.6 1.3 convolution_convert_fusion.10
  91.0 1.3 fusion.5
  92.3 1.5 multiply_reduce_fusion
  97.5 1.2 copy.119
  98.7 2.0 copy.117
  100.7 1.4 convolution_convert_fusion.3
  102.1 1.1 pad_maximum_fusion
  103.9 2.6 %maximum_bitcast_fusion = bf16[8,4,2,16,3072]{4,3,1,2,0:T(8,128)(2,1)S(1)} fusion(bf16[8,2,4,16,1024]{4,3,2,1,0:T(8,128)(2,1)} %convolution_convert_fusion, bf16[8,2,4,16,1024]{4,3,2,1,0:T(8,128)(2,1)S(1)} %copy-done.1, bf16[8,2,4,16,256]{4,3,2,1,0:T(8,128)(2,1)S(1)} %convolution_convert_fusion.3, bf16[8,2,4,16,768]{4,3,2,1,0:T(8,128)(2,1)S(1)} %convolution_convert_fusion.2), kind=kLoop, calls=%fused_computation.1 | loop fusion | flops 25165824 | bytes 12582912 | tf_op jit(solution)/shard_map/transpose | solution.py:62
  106.5 3.1 %copy.123 = bf16[8,4,2,16,3072]{4,3,2,1,0:T(8,128)(2,1)} copy(bf16[8,4,2,16,3072]{4,3,1,2,0:T(8,128)(2,1)S(1)} %maximum_bitcast_fusion) | data formatting | bytes 12582912 | tf_op jit(solution)/shard_map/transpose | solution.py:62
  109.6 2.6 %copy.113 = bf16[1024,3,256]{0,2,1:T(8,128)(2,1)} copy(bf16[1024,3,256]{2,0,1:T(8,128)(2,1)} %param.17) | data formatting | bytes 3145728 | tf_op args[6]
  112.3 2.7 %convolution_convert_fusion.4 = bf16[197,1024]{1,0:T(8,128)(2,1)} fusion(bf16[197,768]{0,1:T(8,128)(2,1)S(1)} %bitcast.204, bf16[1024,768]{0,1:T(8,128)(2,1)} %bitcast.202), kind=kOutput, calls=%fused_computation.10 | convolution fusion | flops 310055936 | bytes 2278912 | tf_op jit(solution)/shard_map/dot_general | solution.py:205
  115.0 1.2 reshape.246
  117.0 3.6 %all-to-all-start.4 = ((bf16[4,197,256]{2,1,0:T(8,128)(2,1)}), bf16[4,197,256]{2,1,0:T(8,128)(2,1)S(1)}, u32[]{:S(2)}, u32[]{:S(2)}) async-start(bf16[4,197,256]{2,1,0:T(8,128)(2,1)} %bitcast.208), calls=%async_computation.4 | async-start | bytes 819200 | tf_op jit(solution)/shard_map/all_to_all | solution.py:23
  120.6 64.8 %reduce-scatter.4.cloned.1.call-done = bf16[8,16,3072]{2,1,0:T(8,128)(2,1)} async-done(((bf16[64,16,3072]{2,1,0:T(8,128)(2,1)}), bf16[8,16,3072]{2,1,0:T(8,128)(2,1)}) %reduce-scatter.4.cloned.1.call-update) | async-done | bytes 786448 | tf_op jit(solution)/shard_map/reduce_scatter | solution.py:64
  185.5 2.2 convolution_convert_fusion.6
  187.7 2.0 reshape.241
  189.6 1.8 copy.157
  191.5 1.1 fusion.20
  192.6 5.1 %all-to-all-start.3 = ((bf16[4,197,256]{2,1,0:T(8,128)(2,1)}), bf16[4,197,256]{2,1,0:T(8,128)(2,1)S(1)}, u32[]{:S(2)}, u32[]{:S(2)}) async-start(bf16[4,197,256]{2,1,0:T(8,128)(2,1)} %bitcast.209), calls=%async_computation.3 | async-start | bytes 819200 | tf_op jit(solution)/shard_map/all_to_all | solution.py:23
  199.0 6.9 %all-to-all-done.3 = bf16[4,197,256]{2,1,0:T(8,128)(2,1)S(1)} async-done(((bf16[4,197,256]{2,1,0:T(8,128)(2,1)}), bf16[4,197,256]{2,1,0:T(8,128)(2,1)S(1)}, u32[]{:S(2)}, u32[]{:S(2)}) %all-to-all-start.3) | async-done | bytes 403488 | tf_op jit(solution)/shard_map/all_to_all | solution.py:23
  206.5 4.2 %all-to-all-start.5 = ((f32[4,1,394]{2,1,0:T(1,128)}), f32[4,1,394]{2,1,0:T(1,128)S(1)}, u32[]{:S(2)}, u32[]{:S(2)}) async-start(f32[4,1,394]{2,1,0:T(1,128)} %broadcast_in_dim.7), calls=%async_computation.5 | async-start | bytes 16384 | tf_op jit(solution)/shard_map/all_to_all | solution.py:29
  210.7 4.6 %all-to-all-done.5 = f32[4,1,394]{2,1,0:T(1,128)S(1)} async-done(((f32[4,1,394]{2,1,0:T(1,128)}), f32[4,1,394]{2,1,0:T(1,128)S(1)}, u32[]{:S(2)}, u32[]{:S(2)}) %all-to-all-start.5) | async-done | bytes 6336 | tf_op jit(solution)/shard_map/all_to_all | solution.py:29
  216.2 7.6 %all-to-all-start.6 = ((f32[64,1,1536]{2,1,0:T(1,128)}), f32[64,1,1536]{2,1,0:T(1,128)S(1)}, u32[]{:S(2)}, u32[]{:S(2)}) async-start(f32[64,1,1536]{2,1,0:T(1,128)} %broadcast_in_dim.8), calls=%async_computation.9 | async-start | bytes 786432 | tf_op jit(solution)/shard_map/all_to_all | solution.py:29
  224.7 1.7 fusion.48
  226.4 11.0 %all-to-all-done.6 = f32[64,1,1536]{2,1,0:T(1,128)S(1)} async-done(((f32[64,1,1536]{2,1,0:T(1,128)}), f32[64,1,1536]{2,1,0:T(1,128)S(1)}, u32[]{:S(2)}, u32[]{:S(2)}) %all-to-all-start.6) | async-done | bytes 393248 | tf_op jit(solution)/shard_map/all_to_all | solution.py:29
  238.8 4.2 %reduce-scatter.8.cloned.1.call-done = bf16[1,16,3072]{2,1,0:T(8,128)(2,1)} async-done(((bf16[2,16,3072]{2,1,0:T(8,128)(2,1)}), bf16[1,16,3072]{2,1,0:T(8,128)(2,1)}) %reduce-scatter.8.cloned.1.call-update) | async-done | bytes 98320 | tf_op jit(solution)/shard_map/reduce_scatter | solution.py:64
  (103 shorter events, 22.1 us)
Async XLA Ops:
  7.2 14.3 %copy-start = (bf16[1024,1024]{1,0:T(8,128)(2,1)S(1)}, bf16[1024,1024]{1,0:T(8,128)(2,1)}, u32[]{:S(2)}) copy-start(bf16[1024,1024]{1,0:T(8,128)(2,1)} %param.21) | copy-start | bytes 6291460
  7.2 13.6 %copy-start.15 = (f32[1024]{0:T(1024)S(1)}, f32[1024]{0:T(1024)}, u32[]{:S(2)}) copy-start(f32[1024]{0:T(1024)} %param.16) | copy-start | bytes 12292
  7.2 13.6 %copy-start.3 = (bf16[1024,1024]{1,0:T(8,128)(2,1)S(1)}, bf16[1024,1024]{1,0:T(8,128)(2,1)}, u32[]{:S(2)}) copy-start(bf16[1024,1024]{1,0:T(8,128)(2,1)} %param.19) | copy-start | bytes 6291460
  7.2 13.6 %copy-start.20 = (f32[1024]{0:T(1024)S(1)}, f32[1024]{0:T(1024)}, u32[]{:S(2)}) copy-start(f32[1024]{0:T(1024)} %param.20) | copy-start | bytes 12292
  21.5 1.6 copy-start.21
  23.1 0.8 copy-start.5
  27.5 12.5 %all-to-all-start.1 = ((bf16[4,197,256]{2,1,0:T(8,128)(2,1)}), bf16[4,197,256]{2,1,0:T(8,128)(2,1)}, u32[]{:S(2)}, u32[]{:S(2)}) async-start(bf16[4,197,256]{2,1,0:T(8,128)(2,1)} %bitcast.199), calls=%async_computation.1 | async-start | bytes 819200 | tf_op jit(solution)/shard_map/all_to_all | solution.py:23
  33.2 7.9 %copy-start.14 = (f32[256]{0:T(256)}, f32[256]{0:T(256)S(1)}, u32[]{:S(2)}) copy-start(f32[256]{0:T(256)S(1)} %dynamic_slice.12) | copy-start | bytes 3076
  41.1 0.7 copy-start.4
  44.1 11.3 %all-to-all-start.2 = ((f32[4,1,394]{2,1,0:T(1,128)}), f32[4,1,394]{2,1,0:T(1,128)S(1)}, u32[]{:S(2)}, u32[]{:S(2)}) async-start(f32[4,1,394]{2,1,0:T(1,128)} %broadcast_in_dim.6), calls=%async_computation.2 | async-start | bytes 16384 | tf_op jit(solution)/shard_map/all_to_all | solution.py:29
  55.4 17.3 %all-to-all-start = ((f32[4,197,256]{2,1,0:T(8,128)}), f32[4,197,256]{2,1,0:T(8,128)S(1)}, u32[]{:S(2)}, u32[]{:S(2)}) async-start(f32[4,197,256]{2,1,0:T(8,128)} %bitcast.196), calls=%async_computation | async-start | bytes 1638400 | tf_op jit(solution)/shard_map/all_to_all | solution.py:55
  60.2 125.3 %reduce-scatter.4.cloned.1.call-start = ((), (), s32[]{:S(2)}) async-start(), calls=%async_computation.10 | async-start | bytes 7077888 | tf_op jit(solution)/shard_map/reduce_scatter | solution.py:64
  60.2 12.6 %copy-start.13 = (bf16[1,197,256]{2,1,0:T(8,128)(2,1)S(1)}, bf16[1,197,256]{2,1,0:T(8,128)(2,1)}, u32[]{:S(2)}) copy-start(bf16[1,197,256]{2,1,0:T(8,128)(2,1)} %param.12) | copy-start | bytes 302596
  63.4 21.1 %copy-start.16 = (f32[1024]{0:T(1024)S(1)}, f32[1024]{0:T(1024)}, u32[]{:S(2)}) copy-start(f32[1024]{0:T(1024)} %param.15) | copy-start | bytes 12292
  64.6 19.9 %copy-start.12 = (bf16[1,197,256]{2,1,0:T(8,128)(2,1)}, bf16[1,197,256]{2,1,0:T(8,128)(2,1)S(1)}, u32[]{:S(2)}) copy-start(bf16[1,197,256]{2,1,0:T(8,128)(2,1)S(1)} %fusion.47) | copy-start | bytes 302596
  72.8 11.7 %copy-start.6 = (bf16[1024,3,256]{2,0,1:T(8,128)(2,1)S(1)}, bf16[1024,3,256]{2,0,1:T(8,128)(2,1)}, u32[]{:S(2)}) copy-start(bf16[1024,3,256]{2,0,1:T(8,128)(2,1)} %param.17) | copy-start | bytes 4718596
  72.8 0.6 copy-start.10
  92.2 1.6 copy-start.7
  93.8 2.7 %copy-start.17 = (f32[1024]{0:T(1024)S(1)}, f32[1024]{0:T(1024)}, u32[]{:S(2)}) copy-start(f32[1024]{0:T(1024)} %param.15) | copy-start | bytes 12292
  100.7 2.5 %copy-start.2 = (bf16[1024,197]{1,0:T(8,128)(2,1)S(1)}, bf16[1024,197]{1,0:T(8,128)(2,1)}, u32[]{:S(2)}) copy-start(bf16[1024,197]{1,0:T(8,128)(2,1)} %copy.117) | copy-start | bytes 1210372
  100.7 3.2 %copy-start.1 = (bf16[8,2,4,16,1024]{4,3,2,1,0:T(8,128)(2,1)S(1)}, bf16[8,2,4,16,1024]{4,3,2,1,0:T(8,128)(2,1)}, u32[]{:S(2)}) copy-start(bf16[8,2,4,16,1024]{4,3,2,1,0:T(8,128)(2,1)} %convolution_convert_fusion.1) | copy-start | bytes 6291460
  115.0 70.5 %copy-start.8 = (bf16[4,64,197]{2,1,0:T(8,128)(2,1)S(1)}, bf16[4,64,197]{2,1,0:T(8,128)(2,1)}, u32[]{:S(2)}) copy-start(bf16[4,64,197]{2,1,0:T(8,128)(2,1)} %convolution_convert_fusion.9) | copy-start | bytes 302596
  117.0 75.5 %all-to-all-start.4 = ((bf16[4,197,256]{2,1,0:T(8,128)(2,1)}), bf16[4,197,256]{2,1,0:T(8,128)(2,1)S(1)}, u32[]{:S(2)}, u32[]{:S(2)}) async-start(bf16[4,197,256]{2,1,0:T(8,128)(2,1)} %bitcast.208), calls=%async_computation.4 | async-start | bytes 819200 | tf_op jit(solution)/shard_map/all_to_all | solution.py:23
  120.6 104.0 %reduce-scatter.6.cloned.1.call-start = ((), (), s32[]{:S(2)}) async-start(), calls=%async_computation.11 | async-start | bytes 983040 | tf_op jit(solution)/shard_map/reduce_scatter | solution.py:64
  189.6 21.0 %copy-start.18 = (f32[256]{0:T(256)S(1)}, f32[256]{0:T(256)}, u32[]{:S(2)}) copy-start(f32[256]{0:T(256)} %get-tuple-element.57) | copy-start | bytes 3076
  189.6 21.0 %copy-start.19 = (f32[1024]{0:T(1024)S(1)}, f32[1024]{0:T(1024)}, u32[]{:S(2)}) copy-start(f32[1024]{0:T(1024)} %get-tuple-element.75) | copy-start | bytes 12292
  192.6 31.3 %copy-start.9 = (bf16[1,197,256]{2,1,0:T(8,128)(2,1)S(1)}, bf16[1,197,256]{2,1,0:T(8,128)(2,1)}, u32[]{:S(2)}) copy-start(bf16[1,197,256]{2,1,0:T(8,128)(2,1)} %param.11) | copy-start | bytes 302596
  192.6 32.1 %copy-start.11 = (bf16[1,197,256]{2,1,0:T(8,128)(2,1)S(1)}, bf16[1,197,256]{2,1,0:T(8,128)(2,1)}, u32[]{:S(2)}) copy-start(bf16[1,197,256]{2,1,0:T(8,128)(2,1)} %param.14) | copy-start | bytes 302596
  192.6 13.3 %all-to-all-start.3 = ((bf16[4,197,256]{2,1,0:T(8,128)(2,1)}), bf16[4,197,256]{2,1,0:T(8,128)(2,1)S(1)}, u32[]{:S(2)}, u32[]{:S(2)}) async-start(bf16[4,197,256]{2,1,0:T(8,128)(2,1)} %bitcast.209), calls=%async_computation.3 | async-start | bytes 819200 | tf_op jit(solution)/shard_map/all_to_all | solution.py:23
  206.5 8.8 %all-to-all-start.5 = ((f32[4,1,394]{2,1,0:T(1,128)}), f32[4,1,394]{2,1,0:T(1,128)S(1)}, u32[]{:S(2)}, u32[]{:S(2)}) async-start(f32[4,1,394]{2,1,0:T(1,128)} %broadcast_in_dim.7), calls=%async_computation.5 | async-start | bytes 16384 | tf_op jit(solution)/shard_map/all_to_all | solution.py:29
  216.2 21.2 %all-to-all-start.6 = ((f32[64,1,1536]{2,1,0:T(1,128)}), f32[64,1,1536]{2,1,0:T(1,128)S(1)}, u32[]{:S(2)}, u32[]{:S(2)}) async-start(f32[64,1,1536]{2,1,0:T(1,128)} %broadcast_in_dim.8), calls=%async_computation.9 | async-start | bytes 786432 | tf_op jit(solution)/shard_map/all_to_all | solution.py:29
  223.8 19.2 %reduce-scatter.8.cloned.1.call-start = ((), (), s32[]{:S(2)}) async-start(), calls=%async_computation.12 | async-start | bytes 294912 | tf_op jit(solution)/shard_map/reduce_scatter | solution.py:64
Sparse Core Ops, SparseCore 0:
  109.8 75.6 reduce-scatter.3
  188.0 21.6 reduce-scatter.5
  227.1 15.8 reduce-scatter.7
where the time goes:
time: 254 us; the launch traced here: 252 us
  waiting for transfers between devices  103 us (41%)
  starting transfers between devices  33.8 us (13%)
  local copies, waits for them, and re-layouts  31.1 us (12%)
  matrix products  29.1 us (11%)
  blocking collectives  22.6 us (9%)
  other arithmetic  18.4 us (7%)
  between operations  14.2 us (6%)
    reduce_scatter x3, waiting for transfers between devices, sum_in_order(): pieces = lax.psum_scatter(pieces, axes[k], scatter_dimension=0, tiled=True)  69 us
    all_gather x2, blocking collectives, side_by_side(): whole = lax.all_gather(both, axis, axis=dim, tiled=True)  22.6 us
    all_to_all x3, starting transfers between devices, sent_to_all(): return lax.all_to_all(copies, axis, split_axis=0, concat_axis=0, tiled=True)  15.9 us
    all_to_all x3, waiting for transfers between devices, sent_to_all(): return lax.all_to_all(copies, axis, split_axis=0, concat_axis=0, tiled=True)  15.6 us
    all_to_all x3, starting transfers between devices, summed_on_arrival(): lax.all_to_all(pieces, axis, split_axis=0, concat_axis=0, tiled=True)  13 us
    reshape x8, local copies, waits for them, and re-layouts, split_up(): x.reshape(*dims[:dim], devices, dims[dim] // devices, *dims[dim + 1:])  11.2 us
    all_to_all x3, waiting for transfers between devices, summed_on_arrival(): lax.all_to_all(pieces, axis, split_axis=0, concat_axis=0, tiled=True)  10.6 us
    dot_general x4, matrix products, weight_term(): lax.dot_general(left_rows, right_rows, (((0,), (0,)), ((), ())), preferre...  8.37 us
  transfers between devices with their start and end apart: 10, of which 7 were waited for; matrix products, arithmetic and copies ran while one was open for 15% of the time, Pallas kernels for 0%

commit v1 on v0

v1 whole, which is shorter than its diff:
```python
import jax
import jax.numpy as jnp
from jax import lax
from jax.experimental import pallas as pl
from jax.experimental.pallas import tpu as pltpu
from jax.sharding import Mesh
from jax.sharding import PartitionSpec as P

D = 1024
HEADS = 16
AXES = ("z", "ylo", "x", "yhi", "core")
DP = ("z", "ylo", "x")
TENSOR = ("yhi", "core")
SWAP = [(0, 1), (1, 0)]
BF = jnp.bfloat16
F32 = jnp.float32
SEQ = 197
ROWS = 208
WIDTH = 256
HALF = 512
HEAD_DIM = 64
FACTOR = HEAD_DIM ** (-0.5)

epsilon = 1e-06


def swap(x, axis):
    return lax.ppermute(x, axis, SWAP)


def pick(index, zero, one):
    return jnp.where(index == 0, zero, one)


def normalize(values):
    centre = values - jnp.mean(values, -1, keepdims=True)
    spread = lax.rsqrt(jnp.mean(centre * centre, -1, keepdims=True) + epsilon)
    return (centre * spread, spread)


def norm_back(grad_in, normed, spread, gain):
    scaled = grad_in * gain
    first_mean = jnp.mean(scaled, -1, keepdims=True)
    second_mean = jnp.mean(scaled * normed, -1, keepdims=True)
    return spread * (scaled - first_mean - normed * second_mean)


def dot(a, b):
    return jnp.dot(a, b, preferred_element_type=F32)


def dot_t(a, b):
    return lax.dot_general(a, b, (((1,), (1,)), ((), ())), preferred_element_type=F32)


def t_dot(a, b):
    return lax.dot_general(a, b, (((0,), (0,)), ((), ())), preferred_element_type=F32)


def gelu_both(h):
    c = (2.0 / jnp.pi) ** 0.5
    square = h * h
    bent = jnp.tanh(c * h * (1.0 + 0.044715 * square))
    half = 0.5 * (1.0 + bent)
    slope = half + 0.5 * h * (1.0 - bent * bent) * (c * (1.0 + 3.0 * 0.044715 * square))
    return h * half, slope


def at_rows():
    return lax.broadcasted_iota(jnp.int32, (ROWS, 1), 0)


def columns(start, width):
    return pl.ds(pl.multiple_of(start, 128), width)


VMEM = pl.BlockSpec(memory_space=pltpu.VMEM)
SMEM = pl.BlockSpec(memory_space=pltpu.SMEM)


def call(kernel, outs, scratch, flops, *args):
    return pl.pallas_call(
        kernel,
        out_shape=[jax.ShapeDtypeStruct(s, d) for s, d in outs],
        in_specs=[SMEM] + [VMEM] * (len(args) - 1),
        out_specs=[VMEM] * len(outs),
        scratch_shapes=scratch,
        cost_estimate=pl.CostEstimate(flops=flops, bytes_accessed=4 << 20, transcendentals=0),
        compiler_params=pltpu.CompilerParams(vmem_limit_bytes=48 << 20),
    )(*args)


def mlp_kernel(
    at, f0, f1, f2, f3, l0, l1, l2, l3, second, upper, gain, inner, bias, outer,
    keep, away, left_in, left_out, right_in, right_out, bias_part, whole, part,
):
    tensor, core = at[0], at[1]
    half = columns(core * HALF, HALF)
    rest = columns((1 - core) * HALF, HALF)
    real = at_rows() < SEQ

    def gathered(blocks):
        whole[192:ROWS, :] = jnp.zeros((ROWS - 192, D), F32)
        for k, b in enumerate(blocks):
            whole[0:SEQ, columns((tensor ^ k) * WIDTH, WIDTH)] = b[...].astype(F32)
        return whole[...]

    def shared(values, k):
        part[...] = values
        keep[:, k * HALF : (k + 1) * HALF] = part[:, half]
        away[:, k * HALF : (k + 1) * HALF] = part[:, rest].astype(BF)

    normed, spread = normalize(gathered((f0, f1, f2, f3)))
    given = (normed * gain[...]).astype(BF)
    left_in[...] = given
    hidden = dot(given, inner[...]) + bias[...]
    active, slope = gelu_both(hidden)
    active = active.astype(BF)
    right_out[...] = active
    part[...] = -dot_t(active, outer[...])
    mine = columns(tensor * WIDTH, WIDTH)
    part[0:SEQ, mine] = part[0:SEQ, mine] + second[...].astype(F32)
    keep[:, 0:HALF] = part[:, half]
    away[:, 0:HALF] = part[:, rest].astype(BF)

    lower = gathered((l0, l1, l2, l3)).astype(BF)
    left_out[...] = lower
    grad_hidden = (dot(lower, outer[...]) * slope).astype(BF)
    right_in[...] = grad_hidden
    bias_part[...] = jnp.sum(grad_hidden.astype(F32), 0, keepdims=True)
    grad_norm = dot_t(grad_hidden, inner[...])
    gain_part = jnp.sum(grad_norm * normed, 0, keepdims=True)
    back = norm_back(grad_norm, normed, spread, gain[...])
    part[...] = jnp.where(at_rows() == SEQ, gain_part, back)
    part[0:SEQ, mine] = part[0:SEQ, mine] + upper[...].astype(F32)
    keep[:, HALF:D] = part[:, half]
    away[:, HALF:D] = part[:, rest].astype(BF)


def attention_kernel(
    at, done, theirs, gain, qkv, proj,
    left_in, left_out, rows_out, normed_out, spread_out, second_out, back_out, gain_out, whole,
):
    tensor, core = at[0], at[1]
    mine = columns(tensor * WIDTH, WIDTH)
    half = columns(core * HALF, HALF)
    rest = columns((1 - core) * HALF, HALF)
    real = at_rows() < SEQ

    whole[:, half] = done[:, 0:HALF].astype(F32)
    whole[:, rest] = theirs[:, 0:HALF].astype(F32)
    second_out[...] = whole[0:SEQ, mine].astype(BF)
    normed, spread = normalize(jnp.where(real, whole[...], 0.0))
    normed_out[...] = normed
    spread_out[...] = spread
    given = (normed * gain[...]).astype(BF)
    left_in[...] = given
    whole[:, half] = done[:, HALF:D].astype(F32)
    whole[:, rest] = theirs[:, HALF:D].astype(F32)
    back_out[...] = whole[0:SEQ, mine].astype(BF)
    gain_out[...] = whole[192:200, mine]
    back = jnp.where(real, whole[...], 0.0).astype(BF)
    left_out[...] = back

    rows = dot(given, qkv[...]).astype(BF)
    grads = dot(back, proj[...]).astype(BF)
    valid = lax.broadcasted_iota(jnp.int32, (1, ROWS), 1) < SEQ
    query_parts, key_parts, value_parts, out_parts = [], [], [], []
    for h in range(4):
        s = slice(h * HEAD_DIM, (h + 1) * HEAD_DIM)
        q = rows[:, 0:WIDTH][:, s]
        k = rows[:, WIDTH : 2 * WIDTH][:, s]
        v = rows[:, 2 * WIDTH :][:, s]
        g = grads[:, s]
        scores = jnp.where(valid, dot_t(q, k) * FACTOR, -1e30)
        raised = jnp.exp(scores - jnp.max(scores, -1, keepdims=True))
        probs = raised / jnp.sum(raised, -1, keepdims=True)
        low = probs.astype(BF)
        out_parts.append(dot(low, v))
        grad_probs = dot_t(g, v)
        value_parts.append(t_dot(low, g))
        row_dot = jnp.sum(grad_probs * probs, -1, keepdims=True)
        grad_scores = (probs * (grad_probs - row_dot)).astype(BF)
        query_parts.append(dot(grad_scores, k) * FACTOR)
        key_parts.append(t_dot(grad_scores, q) * FACTOR)
    for n, parts in enumerate((query_parts, key_parts, value_parts, out_parts)):
        rows_out[:, n * WIDTH : (n + 1) * WIDTH] = jnp.concatenate(parts, 1).astype(BF)


def close_kernel(at, rows, normed, spread, gain, qkv, proj, keep, away, part):
    core = at[1]

    def quarters(first_column):
        for k in range(2):
            to = slice(first_column + k * WIDTH, first_column + (k + 1) * WIDTH)
            keep[:, to] = part[:, columns((2 * k + core) * WIDTH, WIDTH)]
            away[:, to] = part[:, columns((2 * k + 1 - core) * WIDTH, WIDTH)].astype(BF)

    grad_norm = dot_t(rows[:, 0 : 3 * WIDTH], qkv[...])
    gain_part = jnp.sum(grad_norm * normed[...], 0, keepdims=True)
    back = norm_back(grad_norm, normed[...], spread[...], gain[...])
    part[...] = jnp.where(at_rows() == SEQ, gain_part, back)
    quarters(HALF)
    part[...] = dot_t(rows[:, 3 * WIDTH :], proj[...])
    quarters(0)


def products_kernel(widths, extra, at, *refs):
    n = len(widths)
    lefts, rights = refs[:n], refs[n : 2 * n]
    small = refs[2 * n] if extra else None
    outs = refs[2 * n + extra : 2 * n + extra + 4]
    turned, chosen = refs[-2:]
    x = at[2]
    column = 0
    for left, right, width in zip(lefts, rights, widths):
        turned[...] = left[...].astype(F32).T.astype(BF)
        for k in range(4):
            owner = (x + k) % 4
            for b in range(16):
                chosen[b * 16 : (b + 1) * 16, :] = turned[
                    pl.ds(pl.multiple_of(b * 64 + owner * 16, 16), 16), :
                ]
            outs[k][:, column : column + width] = dot(chosen[...], right[...]).astype(BF)
        column += width
    if extra:
        block = jnp.concatenate([small[...], jnp.zeros((24, 128), F32)], 0).astype(BF)
        for k in range(4):
            for b in range(8):
                outs[k][b * 32 : (b + 1) * 32, column:] = block


def products(at, lefts, rights, widths, small=None):
    total = sum(widths) + (128 if small is not None else 0)
    args = (at, *lefts, *rights) + ((small,) if small is not None else ())

    def kernel(*refs):
        products_kernel(widths, int(small is not None), *refs)

    return call(
        kernel,
        [((256, total), BF)] * 4,
        [pltpu.VMEM((D, ROWS), BF), pltpu.VMEM((256, ROWS), BF)],
        2 * D * ROWS * total,
        *args,
    )


def around(axis_size, step):
    return [(i, (i + step) % axis_size) for i in range(axis_size)]


def over_x(pieces):
    came = [lax.ppermute(pieces[k], "x", around(4, k)) for k in (1, 2, 3)]
    return sum((c.astype(F32) for c in came), pieces[0].astype(F32))


def over_z(total):
    came = lax.all_to_all(total.astype(BF).reshape(8, 32, -1), "z", 0, 0, tiled=True)
    return jnp.sum(came.astype(F32), 0)


def over_ylo(rows, ylo, main):
    keep = pick(ylo, rows[:16, :main], rows[16:, :main])
    away = pick(ylo, rows[16:, :main], rows[:16, :main])
    small = rows[:16, main:]
    came = swap(jnp.concatenate([away, small], 1).astype(BF), "ylo").astype(F32)
    return keep + came[:, :main], small + came[:, main:]


def on_device(
    out_first,
    out_second,
    grad_first,
    grad_second,
    gain_attn,
    gain_mlp,
    qkv_weight,
    proj_weight,
    inner_weight,
    inner_bias,
    outer_weight,
):
    yhi, core, ylo, x = (lax.axis_index(a) for a in ("yhi", "core", "ylo", "x"))
    at = jnp.stack([yhi * 2 + core, core, x, ylo]).astype(jnp.int32)
    first, second, upper, lower = (
        a.reshape(SEQ, WIDTH) for a in (out_first, out_second, grad_first, grad_second)
    )
    gain_m, gain_a = gain_mlp.reshape(1, D), gain_attn.reshape(1, D)
    flat_qkv = qkv_weight.reshape(D, 3 * WIDTH)
    block = (ROWS, D)

    def gather(own):
        by_core, by_yhi = swap(own, "core"), swap(own, "yhi")
        return own, by_core, by_yhi, swap(by_yhi, "core")

    keep, away, left_in, left_out, right_in, right_out, bias_part = call(
        mlp_kernel,
        [(block, F32), (block, BF), (block, BF), (block, BF), (block, BF), (block, BF), ((1, D), F32)],
        [pltpu.VMEM(block, F32), pltpu.VMEM(block, F32)],
        8 * ROWS * D * D,
        at,
        *gather(first),
        *gather(lower),
        second,
        upper,
        gain_m,
        inner_weight,
        inner_bias.reshape(1, D),
        outer_weight,
    )
    come = swap(away, "core")
    pair = (keep + come.astype(F32)).astype(BF)
    other = swap(pair, "yhi")
    done = (pair.astype(F32) + other.astype(F32)).astype(BF)
    theirs = swap(done, "core")

    mlp_pieces = products(
        at, (left_in, left_out), (right_in, right_out), (D, D), bias_part.reshape(8, 128)
    )
    mlp_rows, mlp_small = over_ylo(over_z(over_x(mlp_pieces)), ylo, 2 * D)

    attn_in, attn_back, rows, normed, spread, input_second, back_first, gain_rows = call(
        attention_kernel,
        [
            (block, BF),
            (block, BF),
            (block, BF),
            (block, F32),
            ((ROWS, 1), F32),
            ((SEQ, WIDTH), BF),
            ((SEQ, WIDTH), BF),
            ((8, WIDTH), F32),
        ],
        [pltpu.VMEM(block, F32)],
        4 * ROWS * D * D,
        at,
        done,
        theirs,
        gain_a,
        flat_qkv,
        proj_weight,
    )
    attn_pieces = products(
        at, (attn_in, attn_back), (rows[:, : 3 * WIDTH], rows[:, 3 * WIDTH :]), (3 * WIDTH, WIDTH)
    )
    keep, away = call(
        close_kernel,
        [(block, F32), (block, BF)],
        [pltpu.VMEM(block, F32)],
        2 * ROWS * D * D,
        at,
        rows,
        normed,
        spread,
        gain_a,
        flat_qkv,
        proj_weight,
    )
    pair = keep + swap(away, "core").astype(F32)
    mine = jnp.concatenate([pick(yhi, pair[:, a : a + WIDTH], pair[:, a + WIDTH : a + HALF]) for a in (0, HALF)], 1)
    sent = jnp.concatenate([pick(yhi, pair[:, a + WIDTH : a + HALF], pair[:, a : a + WIDTH]) for a in (0, HALF)], 1)
    closed = mine + swap(sent.astype(BF), "yhi").astype(F32)
    input_first = (first.astype(F32) - closed[:SEQ, :WIDTH]).astype(BF)
    back_second = (lower.astype(F32) + closed[:SEQ, WIDTH:]).astype(BF)

    gains = jnp.concatenate([closed[SEQ, WIDTH:].reshape(2, 128), gain_rows[5].reshape(2, 128)], 0)
    gains = over_x([gains] * 4)
    gain_block = jnp.tile(jnp.concatenate([gains, jnp.zeros((28, 128), F32)], 0), (8, 1))
    attn_rows, attn_small = over_ylo(
        over_z(jnp.concatenate([over_x(attn_pieces), gain_block], 1)), ylo, D
    )

    shape_out = (1, SEQ, WIDTH)
    return (
        input_first.reshape(shape_out),
        input_second.reshape(shape_out),
        back_first.reshape(shape_out),
        back_second.reshape(shape_out),
        attn_rows[:, : 3 * WIDTH].reshape(16, 3, WIDTH),
        attn_rows[:, 3 * WIDTH :],
        mlp_rows[:, :D],
        mlp_small[:8].reshape(D),
        mlp_rows[:, D:],
        attn_small[0:2].reshape(WIDTH),
        attn_small[2:4].reshape(WIDTH),
    )


def solution(mesh):
    split = Mesh(mesh.devices.reshape(8, 2, 4, 2, 2), AXES)
    rows = P(DP, None, TENSOR)
    return jax.shard_map(
        on_device,
        mesh=split,
        in_specs=(
            rows,
            rows,
            rows,
            rows,
            P(),
            P(),
            P(None, None, TENSOR),
            P(None, TENSOR),
            P(None, TENSOR),
            P(TENSOR),
            P(None, TENSOR),
        ),
        out_specs=(
            rows,
            rows,
            rows,
            rows,
            rows,
            P(DP, TENSOR),
            P(DP, TENSOR),
            P(TENSOR),
            P(DP, TENSOR),
            P(TENSOR),
            P(TENSOR),
        ),
        check_vma=False,
    )
```

time: 254 us -> 204 us (0.80)
  matrix products: 29.1 us -> 0 us
  blocking collectives: 22.6 us -> 0 us
  Pallas kernels: 0 us -> 16.7 us
  waiting for transfers between devices: 103 us -> 117 us
  between operations: 14.2 us -> 1.03 us
  local copies, waits for them, and re-layouts: 31.1 us -> 18.3 us
  other arithmetic: 18.4 us -> 7.98 us
  starting transfers between devices: 33.8 us -> 40 us
    ppermute x0 -> x22, waiting for transfers between devices: none -> 79.5 us  [the longest x9 58.4 us: over_x(): came = [lax.ppermute(pieces[k], 'x', around(4, k)) for k in (1, 2, 3)]]
    reduce_scatter x3 -> x0, waiting for transfers between devices: 69 us -> none  [sum_in_order(): pieces = lax.psum_scatter(pieces, axes[k], scatter_dimension=0, tiled=True)]
    ppermute x0 -> x22, starting transfers between devices: none -> 28.1 us  [the longest x13 18 us: swap(): return lax.ppermute(x, axis, SWAP)]
    dot_general x17 -> x0, matrix products: 27.7 us -> none  [the longest x4 8.37 us: weight_term(): lax.dot_general(left_rows, right_rows, (((0,), (0,)), ((), ())), preferre...]
    all_gather x2 -> x0, blocking collectives: 22.6 us -> none  [side_by_side(): whole = lax.all_gather(both, axis, axis=dim, tiled=True)]
    all_to_all x7 -> x2, starting transfers between devices: 33.7 us -> 11.9 us  [over_z(): lax.all_to_all(total.astype(BF).reshape(8, 32, -1), 'z', 0, 0, tiled=True)]
    pallas_call x0 -> x5, Pallas kernels: none -> 16.7 us  [call(): pl.pallas_call(kernel, out_shape=[jax.ShapeDtypeStruct(s, d) for s, d in...]
    unnamed x45 -> x47, local copies, waits for them, and re-layouts: 4.75 us -> 14 us
  transfers between devices with their start and end apart: 10 -> 24, of which waited for: 7 -> 12; matrix products, arithmetic and copies ran while one was open for 15% -> 7% of each run, Pallas kernels for 0% -> 3%
where the time goes in v1:
time: 204 us; the launch traced here: 201 us
  waiting for transfers between devices  117 us (57%)
  starting transfers between devices  40 us (20%)
  local copies, waits for them, and re-layouts  18.3 us (9%)
  Pallas kernels  16.7 us (8%)
  other arithmetic  7.98 us (4%)
    ppermute x9, waiting for transfers between devices, over_x(): came = [lax.ppermute(pieces[k], 'x', around(4, k)) for k in (1, 2, 3)]  58.4 us
    all_to_all x2, waiting for transfers between devices, over_z(): lax.all_to_all(total.astype(BF).reshape(8, 32, -1), 'z', 0, 0, tiled=True)  37.4 us
    ppermute x13, waiting for transfers between devices, swap(): return lax.ppermute(x, axis, SWAP)  21 us
    ppermute x13, starting transfers between devices, swap(): return lax.ppermute(x, axis, SWAP)  18 us
    pallas_call x5, Pallas kernels, call(): pl.pallas_call(kernel, out_shape=[jax.ShapeDtypeStruct(s, d) for s, d in...  16.7 us
    unnamed x47, local copies, waits for them, and re-layouts  14 us
    all_to_all x2, starting transfers between devices, over_z(): lax.all_to_all(total.astype(BF).reshape(8, 32, -1), 'z', 0, 0, tiled=True)  11.9 us
    ppermute x9, starting transfers between devices, over_x(): came = [lax.ppermute(pieces[k], 'x', around(4, k)) for k in (1, 2, 3)]  10.1 us
  transfers between devices with their start and end apart: 24, of which 12 were waited for; matrix products, arithmetic and copies ran while one was open for 7% of the time, Pallas kernels for 3%

profile of v1, /device:TPU:1, one launch (start us, length us, event | category | flops | bytes accessed | tf_op | source)
XLA Modules:
  0.0 200.8 jit_solution(271092259593946173)
XLA Ops:
  0.6 3.8 %collective-permute-start.1 = (bf16[197,256]{1,0:T(8,128)(2,1)}, bf16[197,256]{1,0:T(8,128)(2,1)S(1)}, u32[]{:S(2)}, u32[]{:S(2)}) collective-permute-start(bf16[197,256]{1,0:T(8,128)(2,1)} %bitcast.35), channel_id=1, source_target_pairs={{0,2},{2,0},{1,3},{3,1},{4,6},{6,4},{5,7},{7,5},{8,10},{10,8},{9,1... | collective-permute-start | bytes 302600 | tf_op jit(solution)/shard_map/ppermute | solution.py:28
  4.6 2.9 %collective-permute-start = (bf16[197,256]{1,0:T(8,128)(2,1)}, bf16[197,256]{1,0:T(8,128)(2,1)S(1)}, u32[]{:S(2)}, u32[]{:S(2)}) collective-permute-start(bf16[197,256]{1,0:T(8,128)(2,1)} %bitcast.36), channel_id=1, source_target_pairs={{0,1},{1,0},{2,3},{3,2},{4,5},{5,4},{6,7},{7,6},{8,9},{9,8},{10,11... | collective-permute-start | bytes 302600 | tf_op jit(solution)/shard_map/ppermute | solution.py:28
  7.5 3.9 %collective-permute-start.2 = (bf16[197,256]{1,0:T(8,128)(2,1)S(1)}, bf16[197,256]{1,0:T(8,128)(2,1)S(1)}, u32[]{:S(2)}, u32[]{:S(2)}) collective-permute-start(bf16[197,256]{1,0:T(8,128)(2,1)S(1)} %collective-permute-done.1.f2), channel_id=1, source_target_pairs={{0,1},{1,0},{2,3},{3,2},{4,5},{5,4},{6,7},{7,6},{8,9},{9,8},{10,11... | collective-permute-start | bytes 302600 | tf_op jit(solution)/shard_map/ppermute | solution.py:28
  11.3 1.2 collective-permute-start.5
  12.6 0.9 collective-permute-done.5.l3
  13.5 0.9 copy-done.1
  14.3 0.9 copy-done.3
  15.2 1.6 copy-done.6
  16.8 0.9 copy-done.7
  17.7 0.9 copy-done.8
  18.6 0.7 copy-done.9
  19.3 0.7 copy-done.10
  20.0 4.8 %shard_map.194 = (f32[208,1024]{1,0:T(8,128)S(1)}, bf16[208,1024]{1,0:T(8,128)(2,1)S(1)}, bf16[208,1024]{1,0:T(8,128)(2,1)S(1)}, bf16[208,1024]{1,0:T(8,128)(2,1...) custom-call(s32[4]{0:T(128)S(1)} %pad_add_fusion.at.refs_0_, ...), custom_call_target="tpu_custom_call" | custom-call | flops 1744830464 | bytes 4194304 | tf_op jit(solution)/shard_map/pallas_call | solution.py:82
  25.3 1.4 collective-permute-done.6
  26.8 1.3 collective-permute-start.7
  28.1 11.3 %collective-permute-done.7 = bf16[208,1024]{1,0:T(8,128)(2,1)S(1)} collective-permute-done((bf16[208,1024]{1,0:T(8,128)(2,1)S(1)}, bf16[208,1024]{1,0:T(8,128)(2,1)S(1)}, u32[]{:S(2)}, u32[]{:S(2)}) %collective-permute-start.7) | collective-permute-done | bytes 426016 | tf_op jit(solution)/shard_map/ppermute | solution.py:28
  39.6 1.5 collective-permute-start.8
  41.1 2.6 %copy.23 = bf16[1024,3,256]{0,2,1:T(8,128)(2,1)} copy(bf16[1024,3,256]{2,0,1:T(8,128)(2,1)} %param.17) | data formatting | bytes 3145728 | tf_op args[6]
  43.7 1.8 copy.24.qkv
  45.5 4.2 %shard_map.195 = (bf16[208,1024]{1,0:T(8,128)(2,1)S(1)}, bf16[208,1024]{1,0:T(8,128)(2,1)S(1)}, bf16[208,1024]{1,0:T(8,128)(2,1)S(1)}, f32[208,1024]{1,0:T(8,128...) custom-call(s32[4]{0:T(128)S(1)} %pad_add_fusion.at.refs_0_, ...), custom_call_target="tpu_custom_call" | custom-call | flops 872415232 | bytes 4194304 | tf_op jit(solution)/shard_map/pallas_call | solution.py:82
  49.7 0.8 copy-done.13
  50.5 2.4 %shard_map.196 = (f32[208,1024]{1,0:T(8,128)S(1)}, bf16[208,1024]{1,0:T(8,128)(2,1)}) custom-call(s32[4]{0:T(128)S(1)} %pad_add_fusion.at.refs_0_, bf16[208,1024]{1,0:T(8,128)(2,1)S(1)} %get-tuple-element.38.rows, f32[208,1024]{1,0:T(8,128)S(1)} %get-tuple-element.39.normed, f32[208,1]{1,0:T(8,128)S(1)} %get-tuple-element.40.spread, f32[1,1024]{1,0:T(1,128)S(1)} %bitcast.42, ...), custom_call_target="tpu_custom_call" | custom-call | flops 436207616 | bytes 4194304 | tf_op jit(solution)/shard_map/pallas_call | solution.py:82
  52.9 1.0 copy-done.16
  54.0 1.0 copy-done.18
  55.0 1.0 copy-done.20
  56.0 1.0 copy-done.22
  57.0 3.7 %shard_map.198 = (bf16[256,2176]{1,0:T(8,128)(2,1)S(1)}, bf16[256,2176]{1,0:T(8,128)(2,1)}, bf16[256,2176]{1,0:T(8,128)(2,1)}, bf16[256,2176]{1,0:T(8,128)(2,1)}) custom-call(s32[4]{0:T(128)S(1)} %pad_add_fusion.at.refs_0_, bf16[208,1024]{1,0:T(8,128)(2,1)S(1)} %copy-done.16, bf16[208,1024]{1,0:T(8,128)(2,1)S(1)} %copy-done.18, ...), custom_call_target="tpu_custom_call" | custom-call | flops 926941184 | bytes 4194304 | tf_op jit(solution)/shard_map/pallas_call | solution.py:82
  61.3 1.5 shard_map.197
  62.8 1.3 collective-permute-start.11
  64.1 2.1 %collective-permute-start.12 = (bf16[256,1024]{1,0:T(8,128)(2,1)S(1)}, bf16[256,1024]{1,0:T(8,128)(2,1)S(1)}, u32[]{:S(2)}, u32[]{:S(2)}) collective-permute-start(bf16[256,1024]{1,0:T(8,128)(2,1)S(1)} %get-tuple-element.49), channel_id=1, source_target_pairs={{0,8},{4,12},{8,0},{12,4},{1,9},{5,13},{9,1},{13,5},{2,10},{6,14},... | collective-permute-start | bytes 1572872 | tf_op jit(solution)/shard_map/ppermute | solution.py:254
  66.2 1.2 collective-permute-start.13
  67.4 1.1 convert_add_fusion
  68.6 2.0 collective-permute-start.10
  70.6 4.8 %collective-permute-done.10 = bf16[208,512]{1,0:T(8,128)(2,1)S(1)} collective-permute-done((bf16[208,512]{1,0:T(8,128)(2,1)S(1)}, bf16[208,512]{1,0:T(8,128)(2,1)S(1)}, u32[]{:S(2)}, u32[]{:S(2)}) %collective-permute-start.10) | collective-permute-done | bytes 213024 | tf_op jit(solution)/shard_map/ppermute | solution.py:28
  75.9 23.0 %collective-permute-done.11 = bf16[256,1024]{1,0:T(8,128)(2,1)S(1)} collective-permute-done((bf16[256,1024]{1,0:T(8,128)(2,1)S(1)}, bf16[256,1024]{1,0:T(8,128)(2,1)S(1)}, u32[]{:S(2)}, u32[]{:S(2)}) %collective-permute-start.11) | collective-permute-done | bytes 524320 | tf_op jit(solution)/shard_map/ppermute | solution.py:254
  99.6 10.8 %collective-permute-done.12 = bf16[256,1024]{1,0:T(8,128)(2,1)S(1)} collective-permute-done((bf16[256,1024]{1,0:T(8,128)(2,1)S(1)}, bf16[256,1024]{1,0:T(8,128)(2,1)S(1)}, u32[]{:S(2)}, u32[]{:S(2)}) %collective-permute-start.12) | collective-permute-done | bytes 524320 | tf_op jit(solution)/shard_map/ppermute | solution.py:254
  111.0 23.5 %collective-permute-done.15 = f32[4,128]{1,0:T(4,128)S(1)} collective-permute-done((f32[4,128]{1,0:T(4,128)S(1)}, f32[4,128]{1,0:T(4,128)S(1)}, u32[]{:S(2)}, u32[]{:S(2)}) %collective-permute-start.15) | collective-permute-done | bytes 2080 | tf_op jit(solution)/shard_map/ppermute | solution.py:254
  134.5 3.3 %collective-permute-start.14 = (f32[4,128]{1,0:T(4,128)S(1)}, f32[4,128]{1,0:T(4,128)S(1)}, u32[]{:S(2)}, u32[]{:S(2)}) collective-permute-start(f32[4,128]{1,0:T(4,128)S(1)} %pad_maximum_fusion.4), channel_id=1, source_target_pairs={{0,4},{4,8},{8,12},{12,0},{1,5},{5,9},{9,13},{13,1},{2,6},{6,10},{... | collective-permute-start | bytes 6152 | tf_op jit(solution)/shard_map/ppermute | solution.py:254
  138.2 1.1 collective-permute-done.14
  139.3 0.9 pad_maximum_fusion
  140.2 8.2 %all-to-all-start = ((bf16[8,32,1152]{2,1,0:T(8,128)(2,1)}), bf16[8,32,1152]{2,1,0:T(8,128)(2,1)S(1)}, u32[]{:S(2)}, u32[]{:S(2)}) async-start(bf16[8,32,1152]{2,1,0:T(8,128)(2,1)} %pad_maximum_fusion), calls=%async_computation | async-start | bytes 1179648 | tf_op jit(solution)/shard_map/all_to_all | solution.py:259
  148.4 3.5 %add_convert_fusion = bf16[256,2176]{1,0:T(8,128)(2,1)} fusion(bf16[256,2176]{1,0:T(8,128)(2,1)} %collective-permute-done.20, bf16[256,2176]{1,0:T(8,128)(2,1)} %collective-permute-done.19, bf16[256,2176]{1,0:T(8,128)(2,1)} %collective-permute-done.18, bf16[256,2176]{1,0:T(8,128)(2,1)S(1)} %get-tuple-element.57), kind=kLoop, calls=%fused_computation.1 | loop fusion | flops 4456448 | bytes 5570560 | tf_op jit(solution)/shard_map/convert_element_type | solution.py:259
  151.9 12.7 %all-to-all-done = bf16[8,32,1152]{2,1,0:T(8,128)(2,1)S(1)} async-done(((bf16[8,32,1152]{2,1,0:T(8,128)(2,1)}), bf16[8,32,1152]{2,1,0:T(8,128)(2,1)S(1)}, u32[]{:S(2)}, u32[]{:S(2)}) %all-to-all-start) | async-done | bytes 589856 | tf_op jit(solution)/shard_map/all_to_all | solution.py:259
  164.6 3.7 %all-to-all-start.1 = ((bf16[8,32,2176]{2,1,0:T(8,128)(2,1)}), bf16[8,32,2176]{2,1,0:T(8,128)(2,1)S(1)}, u32[]{:S(2)}, u32[]{:S(2)}) async-start(bf16[8,32,2176]{2,1,0:T(8,128)(2,1)} %bitcast.20), calls=%async_computation.1 | async-start | bytes 2228224 | tf_op jit(solution)/shard_map/all_to_all | solution.py:259
  168.9 0.7 fusion.3
  169.6 1.7 collective-permute-done.17
  171.3 24.7 %all-to-all-done.1 = bf16[8,32,2176]{2,1,0:T(8,128)(2,1)S(1)} async-done(((bf16[8,32,2176]{2,1,0:T(8,128)(2,1)}), bf16[8,32,2176]{2,1,0:T(8,128)(2,1)S(1)}, u32[]{:S(2)}, u32[]{:S(2)}) %all-to-all-start.1) | async-done | bytes 1114144 | tf_op jit(solution)/shard_map/all_to_all | solution.py:259
  198.6 0.9 collective-permute-done.21
  (94 shorter events, 8.2 us)
Async XLA Ops:
  0.6 6.8 %collective-permute-start.1 = (bf16[197,256]{1,0:T(8,128)(2,1)}, bf16[197,256]{1,0:T(8,128)(2,1)S(1)}, u32[]{:S(2)}, u32[]{:S(2)}) collective-permute-start(bf16[197,256]{1,0:T(8,128)(2,1)} %bitcast.35), channel_id=1, source_target_pairs={{0,2},{2,0},{1,3},{3,1},{4,6},{6,4},{5,7},{7,5},{8,10},{10,8},{9,1... | collective-permute-start | bytes 302600 | tf_op jit(solution)/shard_map/ppermute | solution.py:28
  4.5 6.9 %collective-permute-start.4 = (bf16[197,256]{1,0:T(8,128)(2,1)}, bf16[197,256]{1,0:T(8,128)(2,1)S(1)}, u32[]{:S(2)}, u32[]{:S(2)}) collective-permute-start(bf16[197,256]{1,0:T(8,128)(2,1)} %bitcast.38), channel_id=1, source_target_pairs={{0,2},{2,0},{1,3},{3,1},{4,6},{6,4},{5,7},{7,5},{8,10},{10,8},{9,1... | collective-permute-start | bytes 302600 | tf_op jit(solution)/shard_map/ppermute | solution.py:28
  4.6 8.0 %collective-permute-start = (bf16[197,256]{1,0:T(8,128)(2,1)}, bf16[197,256]{1,0:T(8,128)(2,1)S(1)}, u32[]{:S(2)}, u32[]{:S(2)}) collective-permute-start(bf16[197,256]{1,0:T(8,128)(2,1)} %bitcast.36), channel_id=1, source_target_pairs={{0,1},{1,0},{2,3},{3,2},{4,5},{5,4},{6,7},{7,6},{8,9},{9,8},{10,11... | collective-permute-start | bytes 302600 | tf_op jit(solution)/shard_map/ppermute | solution.py:28
  7.5 5.1 %collective-permute-start.3 = (bf16[197,256]{1,0:T(8,128)(2,1)}, bf16[197,256]{1,0:T(8,128)(2,1)S(1)}, u32[]{:S(2)}, u32[]{:S(2)}) collective-permute-start(bf16[197,256]{1,0:T(8,128)(2,1)} %bitcast.39), channel_id=1, source_target_pairs={{0,1},{1,0},{2,3},{3,2},{4,5},{5,4},{6,7},{7,6},{8,9},{9,8},{10,11... | collective-permute-start | bytes 302600 | tf_op jit(solution)/shard_map/ppermute | solution.py:28
  7.5 5.1 %collective-permute-start.2 = (bf16[197,256]{1,0:T(8,128)(2,1)S(1)}, bf16[197,256]{1,0:T(8,128)(2,1)S(1)}, u32[]{:S(2)}, u32[]{:S(2)}) collective-permute-start(bf16[197,256]{1,0:T(8,128)(2,1)S(1)} %collective-permute-done.1.f2), channel_id=1, source_target_pairs={{0,1},{1,0},{2,3},{3,2},{4,5},{5,4},{6,7},{7,6},{8,9},{9,8},{10,11... | collective-permute-start | bytes 302600 | tf_op jit(solution)/shard_map/ppermute | solution.py:28
  11.3 2.1 %collective-permute-start.5 = (bf16[197,256]{1,0:T(8,128)(2,1)S(1)}, bf16[197,256]{1,0:T(8,128)(2,1)S(1)}, u32[]{:S(2)}, u32[]{:S(2)}) collective-permute-start(bf16[197,256]{1,0:T(8,128)(2,1)S(1)} %collective-permute-done.4.l2), channel_id=1, source_target_pairs={{0,1},{1,0},{2,3},{3,2},{4,5},{5,4},{6,7},{7,6},{8,9},{9,8},{10,11... | collective-permute-start | bytes 302600 | tf_op jit(solution)/shard_map/ppermute | solution.py:28
  13.4 0.9 copy-start.1
  14.3 0.9 copy-start.3
  15.2 1.6 copy-start.6
  16.8 0.9 copy-start.7
  17.7 0.9 copy-start.8
  18.6 0.7 copy-start.9
  19.3 0.7 copy-start.10
  24.8 14.8 %copy-start.15 = (bf16[208,1024]{1,0:T(8,128)(2,1)}, bf16[208,1024]{1,0:T(8,128)(2,1)S(1)}, u32[]{:S(2)}) copy-start(bf16[208,1024]{1,0:T(8,128)(2,1)S(1)} %get-tuple-element.52.refs_1_) | copy-start | bytes 1277956
  24.8 14.8 %copy-start.17 = (bf16[208,1024]{1,0:T(8,128)(2,1)}, bf16[208,1024]{1,0:T(8,128)(2,1)S(1)}, u32[]{:S(2)}) copy-start(bf16[208,1024]{1,0:T(8,128)(2,1)S(1)} %get-tuple-element.53.refs_2_) | copy-start | bytes 1277956
  24.8 14.8 %copy-start.19 = (bf16[208,1024]{1,0:T(8,128)(2,1)}, bf16[208,1024]{1,0:T(8,128)(2,1)S(1)}, u32[]{:S(2)}) copy-start(bf16[208,1024]{1,0:T(8,128)(2,1)S(1)} %get-tuple-element.54.refs_3_) | copy-start | bytes 1277956
  24.9 14.8 %copy-start.21 = (bf16[208,1024]{1,0:T(8,128)(2,1)}, bf16[208,1024]{1,0:T(8,128)(2,1)S(1)}, u32[]{:S(2)}) copy-start(bf16[208,1024]{1,0:T(8,128)(2,1)S(1)} %get-tuple-element.55.refs_4_) | copy-start | bytes 1277956
  24.9 1.9 collective-permute-start.6
  26.8 12.6 %collective-permute-start.7 = (bf16[208,1024]{1,0:T(8,128)(2,1)S(1)}, bf16[208,1024]{1,0:T(8,128)(2,1)S(1)}, u32[]{:S(2)}, u32[]{:S(2)}) collective-permute-start(bf16[208,1024]{1,0:T(8,128)(2,1)S(1)} %add_convert_fusion.3), channel_id=1, source_target_pairs={{0,2},{2,0},{1,3},{3,1},{4,6},{6,4},{5,7},{7,5},{8,10},{10,8},{9,1... | collective-permute-start | bytes 1277960 | tf_op jit(solution)/shard_map/ppermute | solution.py:28
  39.6 5.9 %collective-permute-start.8 = (bf16[208,1024]{1,0:T(8,128)(2,1)S(1)}, bf16[208,1024]{1,0:T(8,128)(2,1)S(1)}, u32[]{:S(2)}, u32[]{:S(2)}) collective-permute-start(bf16[208,1024]{1,0:T(8,128)(2,1)S(1)} %add_convert_fusion.2.done), channel_id=1, source_target_pairs={{0,1},{1,0},{2,3},{3,2},{4,5},{5,4},{6,7},{7,6},{8,9},{9,8},{10,11... | collective-permute-start | bytes 1277960 | tf_op jit(solution)/shard_map/ppermute | solution.py:28
  43.7 1.8 copy-start
  43.7 1.8 copy-start.5
  49.7 0.8 copy-start.13
  50.5 2.4 %copy-start.11 = (bf16[208,1024]{1,0:T(8,128)(2,1)}, bf16[208,1024]{1,0:T(8,128)(2,1)S(1)}, u32[]{:S(2)}) copy-start(bf16[208,1024]{1,0:T(8,128)(2,1)S(1)} %get-tuple-element.45.refs_1_) | copy-start | bytes 1277956
  52.9 14.5 %collective-permute-start.9 = (bf16[208,1024]{1,0:T(8,128)(2,1)}, bf16[208,1024]{1,0:T(8,128)(2,1)}, u32[]{:S(2)}, u32[]{:S(2)}) collective-permute-start(bf16[208,1024]{1,0:T(8,128)(2,1)} %get-tuple-element.42), channel_id=1, source_target_pairs={{0,1},{1,0},{2,3},{3,2},{4,5},{5,4},{6,7},{7,6},{8,9},{9,8},{10,11... | collective-permute-start | bytes 1277960 | tf_op jit(solution)/shard_map/ppermute | solution.py:28
  52.9 1.0 copy-start.16
  54.0 1.0 copy-start.18
  55.0 1.0 copy-start.20
  56.0 1.0 copy-start.22
  57.0 4.3 %copy-start.12 = (bf16[208,1024]{1,0:T(8,128)(2,1)S(1)}, bf16[208,1024]{1,0:T(8,128)(2,1)}, u32[]{:S(2)}) copy-start(bf16[208,1024]{1,0:T(8,128)(2,1)} %copy-done.11) | copy-start | bytes 1277956
  57.0 4.3 %copy-start.14 = (bf16[208,1024]{1,0:T(8,128)(2,1)S(1)}, bf16[208,1024]{1,0:T(8,128)(2,1)}, u32[]{:S(2)}) copy-start(bf16[208,1024]{1,0:T(8,128)(2,1)} %copy-done.13) | copy-start | bytes 1277956
  60.7 87.7 %collective-permute-start.18 = (bf16[256,2176]{1,0:T(8,128)(2,1)}, bf16[256,2176]{1,0:T(8,128)(2,1)}, u32[]{:S(2)}, u32[]{:S(2)}) collective-permute-start(bf16[256,2176]{1,0:T(8,128)(2,1)} %get-tuple-element.58), channel_id=1, source_target_pairs={{0,4},{4,8},{8,12},{12,0},{1,5},{5,9},{9,13},{13,1},{2,6},{6,10},{... | collective-permute-start | bytes 3342344 | tf_op jit(solution)/shard_map/ppermute | solution.py:254
  62.8 36.2 %collective-permute-start.11 = (bf16[256,1024]{1,0:T(8,128)(2,1)S(1)}, bf16[256,1024]{1,0:T(8,128)(2,1)S(1)}, u32[]{:S(2)}, u32[]{:S(2)}) collective-permute-start(bf16[256,1024]{1,0:T(8,128)(2,1)S(1)} %get-tuple-element.48), channel_id=1, source_target_pairs={{0,4},{4,8},{8,12},{12,0},{1,5},{5,9},{9,13},{13,1},{2,6},{6,10},{... | collective-permute-start | bytes 1572872 | tf_op jit(solution)/shard_map/ppermute | solution.py:254
  64.1 46.4 %collective-permute-start.12 = (bf16[256,1024]{1,0:T(8,128)(2,1)S(1)}, bf16[256,1024]{1,0:T(8,128)(2,1)S(1)}, u32[]{:S(2)}, u32[]{:S(2)}) collective-permute-start(bf16[256,1024]{1,0:T(8,128)(2,1)S(1)} %get-tuple-element.49), channel_id=1, source_target_pairs={{0,8},{4,12},{8,0},{12,4},{1,9},{5,13},{9,1},{13,5},{2,10},{6,14},... | collective-permute-start | bytes 1572872 | tf_op jit(solution)/shard_map/ppermute | solution.py:254
  66.2 44.8 %collective-permute-start.13 = (bf16[256,1024]{1,0:T(8,128)(2,1)S(1)}, bf16[256,1024]{1,0:T(8,128)(2,1)S(1)}, u32[]{:S(2)}, u32[]{:S(2)}) collective-permute-start(bf16[256,1024]{1,0:T(8,128)(2,1)S(1)} %get-tuple-element.50), channel_id=1, source_target_pairs={{0,12},{4,0},{8,4},{12,8},{1,13},{5,1},{9,5},{13,9},{2,14},{6,2},{... | collective-permute-start | bytes 1572872 | tf_op jit(solution)/shard_map/ppermute | solution.py:254
  68.6 6.8 %collective-permute-start.10 = (bf16[208,512]{1,0:T(8,128)(2,1)S(1)}, bf16[208,512]{1,0:T(8,128)(2,1)S(1)}, u32[]{:S(2)}, u32[]{:S(2)}) collective-permute-start(bf16[208,512]{1,0:T(8,128)(2,1)S(1)} %pad_maximum_fusion.1), channel_id=1, source_target_pairs={{0,2},{2,0},{1,3},{3,1},{4,6},{6,4},{5,7},{7,5},{8,10},{10,8},{9,1... | collective-permute-start | bytes 638984 | tf_op jit(solution)/shard_map/ppermute | solution.py:28
  75.4 73.0 %collective-permute-start.19 = (bf16[256,2176]{1,0:T(8,128)(2,1)}, bf16[256,2176]{1,0:T(8,128)(2,1)}, u32[]{:S(2)}, u32[]{:S(2)}) collective-permute-start(bf16[256,2176]{1,0:T(8,128)(2,1)} %get-tuple-element.59), channel_id=1, source_target_pairs={{0,8},{4,12},{8,0},{12,4},{1,9},{5,13},{9,1},{13,5},{2,10},{6,14},... | collective-permute-start | bytes 3342344 | tf_op jit(solution)/shard_map/ppermute | solution.py:254
  99.0 49.4 %collective-permute-start.20 = (bf16[256,2176]{1,0:T(8,128)(2,1)}, bf16[256,2176]{1,0:T(8,128)(2,1)}, u32[]{:S(2)}, u32[]{:S(2)}) collective-permute-start(bf16[256,2176]{1,0:T(8,128)(2,1)} %get-tuple-element.60), channel_id=1, source_target_pairs={{0,12},{4,0},{8,4},{12,8},{1,13},{5,1},{9,5},{13,9},{2,14},{6,2},{... | collective-permute-start | bytes 3342344 | tf_op jit(solution)/shard_map/ppermute | solution.py:254
  110.5 24.0 %collective-permute-start.15 = (f32[4,128]{1,0:T(4,128)S(1)}, f32[4,128]{1,0:T(4,128)S(1)}, u32[]{:S(2)}, u32[]{:S(2)}) collective-permute-start(f32[4,128]{1,0:T(4,128)S(1)} %pad_maximum_fusion.4), channel_id=1, source_target_pairs={{0,8},{4,12},{8,0},{12,4},{1,9},{5,13},{9,1},{13,5},{2,10},{6,14},... | collective-permute-start | bytes 6152 | tf_op jit(solution)/shard_map/ppermute | solution.py:254
  111.0 27.2 %collective-permute-start.16 = (f32[4,128]{1,0:T(4,128)S(1)}, f32[4,128]{1,0:T(4,128)S(1)}, u32[]{:S(2)}, u32[]{:S(2)}) collective-permute-start(f32[4,128]{1,0:T(4,128)S(1)} %pad_maximum_fusion.4), channel_id=1, source_target_pairs={{0,12},{4,0},{8,4},{12,8},{1,13},{5,1},{9,5},{13,9},{2,14},{6,2},{... | collective-permute-start | bytes 6152 | tf_op jit(solution)/shard_map/ppermute | solution.py:254
  134.5 4.8 %collective-permute-start.14 = (f32[4,128]{1,0:T(4,128)S(1)}, f32[4,128]{1,0:T(4,128)S(1)}, u32[]{:S(2)}, u32[]{:S(2)}) collective-permute-start(f32[4,128]{1,0:T(4,128)S(1)} %pad_maximum_fusion.4), channel_id=1, source_target_pairs={{0,4},{4,8},{8,12},{12,0},{1,5},{5,9},{9,13},{13,1},{2,6},{6,10},{... | collective-permute-start | bytes 6152 | tf_op jit(solution)/shard_map/ppermute | solution.py:254
  140.2 24.4 %all-to-all-start = ((bf16[8,32,1152]{2,1,0:T(8,128)(2,1)}), bf16[8,32,1152]{2,1,0:T(8,128)(2,1)S(1)}, u32[]{:S(2)}, u32[]{:S(2)}) async-start(bf16[8,32,1152]{2,1,0:T(8,128)(2,1)} %pad_maximum_fusion), calls=%async_computation | async-start | bytes 1179648 | tf_op jit(solution)/shard_map/all_to_all | solution.py:259
  164.6 4.3 %copy-start.2 = (bf16[1,197,256]{2,1,0:T(8,128)(2,1)S(1)}, bf16[1,197,256]{2,1,0:T(8,128)(2,1)}, u32[]{:S(2)}) copy-start(bf16[1,197,256]{2,1,0:T(8,128)(2,1)} %param.11) | copy-start | bytes 302596
  164.6 4.3 %copy-start.4 = (bf16[1,197,256]{2,1,0:T(8,128)(2,1)S(1)}, bf16[1,197,256]{2,1,0:T(8,128)(2,1)}, u32[]{:S(2)}) copy-start(bf16[1,197,256]{2,1,0:T(8,128)(2,1)} %param.14) | copy-start | bytes 302596
  164.6 31.5 %all-to-all-start.1 = ((bf16[8,32,2176]{2,1,0:T(8,128)(2,1)}), bf16[8,32,2176]{2,1,0:T(8,128)(2,1)S(1)}, u32[]{:S(2)}, u32[]{:S(2)}) async-start(bf16[8,32,2176]{2,1,0:T(8,128)(2,1)} %bitcast.20), calls=%async_computation.1 | async-start | bytes 2228224 | tf_op jit(solution)/shard_map/all_to_all | solution.py:259
  168.4 2.9 %collective-permute-start.17 = (bf16[16,1152]{1,0:T(8,128)(2,1)S(1)}, bf16[16,1152]{1,0:T(8,128)(2,1)S(1)}, u32[]{:S(2)}, u32[]{:S(2)}) collective-permute-start(bf16[16,1152]{1,0:T(8,128)(2,1)S(1)} %pad_maximum_fusion.3), channel_id=1, source_target_pairs={{0,16},{16,0},{1,17},{17,1},{2,18},{18,2},{3,19},{19,3},{4,20},{20... | collective-permute-start | bytes 110600 | tf_op jit(solution)/shard_map/ppermute | solution.py:28
  196.3 3.2 %collective-permute-start.21 = (bf16[16,2176]{1,0:T(8,128)(2,1)S(1)}, bf16[16,2176]{1,0:T(8,128)(2,1)S(1)}, u32[]{:S(2)}, u32[]{:S(2)}) collective-permute-start(bf16[16,2176]{1,0:T(8,128)(2,1)S(1)} %pad_maximum_fusion.2), channel_id=1, source_target_pairs={{0,16},{16,0},{1,17},{17,1},{2,18},{18,2},{3,19},{19,3},{4,20},{20... | collective-permute-start | bytes 208904 | tf_op jit(solution)/shard_map/ppermute | solution.py:28

commit v2 on v1

v2 whole, which is shorter than its diff:
```python
import jax
import jax.numpy as jnp
from jax import lax
from jax.experimental import pallas as pl
from jax.experimental.pallas import tpu as pltpu
from jax.sharding import Mesh
from jax.sharding import PartitionSpec as P

D = 1024
AXES = ("z", "ylo", "x", "yhi", "core")
DP = ("z", "ylo", "x")
TENSOR = ("yhi", "core")
SWAP = [(0, 1), (1, 0)]
BF = jnp.bfloat16
F32 = jnp.float32
SEQ = 197
ROWS = 208
WIDTH = 256
HALF = 512
WIDE = 2 * D
STEPS = (2, 1, 3, 0)
HEAD_DIM = 64
FACTOR = HEAD_DIM ** (-0.5)

epsilon = 1e-06


def swap(x, axis):
    return lax.ppermute(x, axis, SWAP)


def around(x, step):
    return lax.ppermute(x, "x", [(i, (i + step) % 4) for i in range(4)])


def normalize(values):
    centre = values - jnp.mean(values, -1, keepdims=True)
    spread = lax.rsqrt(jnp.mean(centre * centre, -1, keepdims=True) + epsilon)
    return (centre * spread, spread)


def norm_back(grad_in, normed, spread, gain):
    scaled = grad_in * gain
    first_mean = jnp.mean(scaled, -1, keepdims=True)
    second_mean = jnp.mean(scaled * normed, -1, keepdims=True)
    return spread * (scaled - first_mean - normed * second_mean)


def dot(a, b):
    return jnp.dot(a, b, preferred_element_type=F32)


def dot_t(a, b):
    return lax.dot_general(a, b, (((1,), (1,)), ((), ())), preferred_element_type=F32)


def t_dot(a, b):
    return lax.dot_general(a, b, (((0,), (0,)), ((), ())), preferred_element_type=F32)


def gelu_both(h):
    c = (2.0 / jnp.pi) ** 0.5
    square = h * h
    bent = jnp.tanh(c * h * (1.0 + 0.044715 * square))
    half = 0.5 * (1.0 + bent)
    slope = half + 0.5 * h * (1.0 - bent * bent) * (c * (1.0 + 3.0 * 0.044715 * square))
    return h * half, slope


def at_rows():
    return lax.broadcasted_iota(jnp.int32, (ROWS, 1), 0)


def columns(start, width):
    return pl.ds(pl.multiple_of(start, 128), width)


VMEM = pl.BlockSpec(memory_space=pltpu.VMEM)
SMEM = pl.BlockSpec(memory_space=pltpu.SMEM)
ANY = pl.BlockSpec(memory_space=pl.ANY)


def call(kernel, outs, scratch, flops, *args, limit=20):
    return pl.pallas_call(
        kernel,
        out_shape=[jax.ShapeDtypeStruct(s, d) for s, d in outs],
        in_specs=[SMEM] + [VMEM] * (len(args) - 1),
        out_specs=[VMEM] * len(outs),
        scratch_shapes=scratch,
        cost_estimate=pl.CostEstimate(flops=flops, bytes_accessed=4 << 20, transcendentals=0),
        compiler_params=pltpu.CompilerParams(vmem_limit_bytes=limit << 20),
    )(*args)


def pause_kernel(out):
    out[...] = jnp.zeros((8, 128), F32)


def pause(size):
    return pl.pallas_call(
        pause_kernel,
        out_shape=jax.ShapeDtypeStruct((8, 128), F32),
        out_specs=VMEM,
        cost_estimate=pl.CostEstimate(flops=size, bytes_accessed=size >> 13, transcendentals=0),
        compiler_params=pltpu.CompilerParams(vmem_limit_bytes=1 << 20),
    )()


def pass_kernel(values, out):
    out[...] = values[...]


def passed(values):
    return pl.pallas_call(
        pass_kernel,
        out_shape=jax.ShapeDtypeStruct(values.shape, values.dtype),
        in_specs=[VMEM],
        out_specs=VMEM,
        cost_estimate=pl.CostEstimate(flops=8 << 30, bytes_accessed=1 << 20, transcendentals=0),
        compiler_params=pltpu.CompilerParams(vmem_limit_bytes=1 << 20),
    )(values)


def mlp_kernel(
    at, f0, f1, f2, f3, l0, l1, l2, l3, second, upper, vectors, inner, outer, mark,
    keep, away, left_in, left_out, right, bias_part, whole, part,
):
    tensor, core = at[0], at[1]
    half = columns(core * HALF, HALF)
    rest = columns((1 - core) * HALF, HALF)
    gain, bias = vectors[0:1, :], vectors[1:2, :]

    def gathered(blocks):
        whole[192:ROWS, :] = jnp.zeros((ROWS - 192, D), F32)
        for k, b in enumerate(blocks):
            whole[0:SEQ, columns((tensor ^ k) * WIDTH, WIDTH)] = b[...].astype(F32)
        return whole[...]

    normed, spread = normalize(gathered((f0, f1, f2, f3)))
    given = (normed * gain).astype(BF)
    left_in[...] = given
    hidden = dot(given, inner[...]) + bias
    active, slope = gelu_both(hidden)
    active = active.astype(BF)
    right[:, D:] = active
    part[...] = -dot_t(active, outer[...])
    mine = columns(tensor * WIDTH, WIDTH)
    part[0:SEQ, mine] = part[0:SEQ, mine] + second[...].astype(F32)
    keep[:, 0:HALF] = part[:, half]
    away[:, 0:HALF] = part[:, rest].astype(BF)

    lower = gathered((l0, l1, l2, l3)).astype(BF)
    left_out[...] = lower
    grad_hidden = (dot(lower, outer[...]) * slope).astype(BF)
    right[:, :D] = grad_hidden
    bias_part[...] = jnp.sum(grad_hidden.astype(F32), 0, keepdims=True)
    grad_norm = dot_t(grad_hidden, inner[...])
    gain_part = jnp.sum(grad_norm * normed, 0, keepdims=True)
    back = norm_back(grad_norm, normed, spread, gain)
    part[...] = jnp.where(at_rows() == SEQ, gain_part, back)
    part[0:SEQ, mine] = part[0:SEQ, mine] + upper[...].astype(F32)
    keep[:, HALF:D] = part[:, half]
    away[:, HALF:D] = part[:, rest].astype(BF)


def before_kernel(
    at, done, theirs, gain, mark,
    given_out, back_in, normed_out, spread_out, second_out, back_out, gain_out, keep, away, whole, turned,
):
    tensor, core = at[0], at[1]
    mine = columns(tensor * WIDTH, WIDTH)
    half = columns(core * HALF, HALF)
    rest = columns((1 - core) * HALF, HALF)
    real = at_rows() < SEQ

    def sorted_rows(values, first):
        turned[...] = values.T.astype(BF)
        for out, y in ((keep, at[3]), (away, 1 - at[3])):
            for to, (k, z) in enumerate((k, z) for k in STEPS for z in range(8)):
                row = (z * 8 + y * 4 + (at[2] + k) % 4) * 16
                out[first + to * 16 : first + (to + 1) * 16, :] = turned[pl.ds(pl.multiple_of(row, 16), 16), :]

    whole[:, half] = done[:, 0:HALF].astype(F32)
    whole[:, rest] = theirs[:, 0:HALF].astype(F32)
    second_out[...] = whole[0:SEQ, mine].astype(BF)
    normed, spread = normalize(jnp.where(real, whole[...], 0.0))
    normed_out[...] = normed
    spread_out[...] = spread
    given = (normed * gain[...]).astype(BF)
    given_out[...] = given
    sorted_rows(given.astype(F32), 0)
    whole[:, half] = done[:, HALF:D].astype(F32)
    whole[:, rest] = theirs[:, HALF:D].astype(F32)
    back_out[...] = whole[0:SEQ, mine].astype(BF)
    gain_out[...] = whole[192:200, mine]
    back = jnp.where(real, whole[...], 0.0)
    back_in[...] = back.astype(BF)
    sorted_rows(back, 512)


def attention_kernel(at, given, back, qkv, proj, rows_out):
    rows = [dot(given[...], qkv[c]).astype(BF) for c in range(3)]
    grads = dot(back[...], proj[...]).astype(BF)
    valid = lax.broadcasted_iota(jnp.int32, (1, ROWS), 1) < SEQ
    query_parts, key_parts, value_parts, out_parts = [], [], [], []
    for h in range(4):
        s = slice(h * HEAD_DIM, (h + 1) * HEAD_DIM)
        q, k, v = (r[:, s] for r in rows)
        g = grads[:, s]
        scores = jnp.where(valid, dot_t(q, k) * FACTOR, -1e30)
        raised = jnp.exp(scores - jnp.max(scores, -1, keepdims=True))
        probs = raised / jnp.sum(raised, -1, keepdims=True)
        low = probs.astype(BF)
        out_parts.append(dot(low, v))
        grad_probs = dot_t(g, v)
        value_parts.append(t_dot(low, g))
        row_dot = jnp.sum(grad_probs * probs, -1, keepdims=True)
        grad_scores = (probs * (grad_probs - row_dot)).astype(BF)
        query_parts.append(dot(grad_scores, k) * FACTOR)
        key_parts.append(t_dot(grad_scores, q) * FACTOR)
    for n, parts in enumerate((query_parts, key_parts, value_parts, out_parts)):
        rows_out[:, n * WIDTH : (n + 1) * WIDTH] = jnp.concatenate(parts, 1).astype(BF)


def close_kernel(at, rows, normed, spread, gain, qkv, proj, keep, away, part):
    core = at[1]

    def quarters(first_column):
        for k in range(2):
            to = slice(first_column + k * WIDTH, first_column + (k + 1) * WIDTH)
            keep[:, to] = part[:, columns((2 * k + core) * WIDTH, WIDTH)]
            away[:, to] = part[:, columns((2 * k + 1 - core) * WIDTH, WIDTH)].astype(BF)

    grad_norm = sum(dot_t(rows[:, c * WIDTH : (c + 1) * WIDTH], qkv[c]) for c in range(3))
    gain_part = jnp.sum(grad_norm * normed[...], 0, keepdims=True)
    back = norm_back(grad_norm, normed[...], spread[...], gain[...])
    part[...] = jnp.where(at_rows() == SEQ, gain_part, back)
    quarters(HALF)
    part[...] = dot_t(rows[:, 3 * WIDTH :], proj[...])
    quarters(0)


def close_pair_kernel(at, keep, came, mine, sent):
    yhi = at[0] // 2
    for k in range(2):
        to = slice(k * WIDTH, (k + 1) * WIDTH)
        low, high = (
            keep[:, c : c + WIDTH] + came[:, c : c + WIDTH].astype(F32)
            for c in (k * HALF, k * HALF + WIDTH)
        )
        mine[:, to] = jnp.where(yhi == 0, low, high)
        sent[:, to] = jnp.where(yhi == 0, high, low).astype(BF)


def close_end_kernel(at, mine, came, first, lower, gain_m, bias, input_first, back_second, small):
    total = mine[...] + came[...].astype(F32)
    input_first[...] = (first[...].astype(F32) - total[0:SEQ, :WIDTH]).astype(BF)
    back_second[...] = (lower[...].astype(F32) + total[0:SEQ, WIDTH:]).astype(BF)
    row = total[192:200, WIDTH:]
    small[0:8, :] = bias[...]
    for k in range(2):
        small[8 + k : 9 + k, :] = row[5:6, k * 128 : (k + 1) * 128]
        small[10 + k : 11 + k, :] = gain_m[5:6, k * 128 : (k + 1) * 128]


def turn(left, turned):
    turned[...] = left[...].astype(F32).T.astype(BF)


def rows_of(turned, chosen, blocks):
    for to, b in enumerate(blocks):
        chosen[to * 16 : (to + 1) * 16, :] = turned[pl.ds(pl.multiple_of(b * 16, 16), 16), :]
    return chosen[...]


def far_kernel(at, left_in, left_out, right, far_a, far_b, turned_in, turned_out, chosen):
    turn(left_in, turned_in)
    turn(left_out, turned_out)
    blocks = [b * 4 + (at[2] + 2) % 4 for b in range(16)]
    far_a[...] = dot(rows_of(turned_in, chosen, blocks), right[:, :D]).astype(BF)
    far_b[...] = dot(rows_of(turned_out, chosen, blocks), right[:, D:]).astype(BF)


def near_kernel(at, turned_in, turned_out, right, a1, b1, a3, b3, a0, b0, chosen):
    for k, a, b in ((1, a1, b1), (3, a3, b3), (0, a0, b0)):
        blocks = [r * 4 + (at[2] + k) % 4 for r in range(16)]
        a[...] = dot(rows_of(turned_in, chosen, blocks), right[:, :D]).astype(BF)
        b[...] = dot(rows_of(turned_out, chosen, blocks), right[:, D:]).astype(BF)


def pieces_kernel(at, own_left, came_left, own_right, came_right, *pieces):
    for to, piece in enumerate(pieces):
        for first, low, high in ((0, 0, 3 * WIDTH), (512, 3 * WIDTH, D)):
            r = slice(first + to * 128, first + (to + 1) * 128)
            piece[:, low:high] = (
                dot(own_left[r, :], own_right[:, low:high]) + dot(came_left[r, :], came_right[:, low:high])
            ).astype(BF)


def added(a, b):
    return (a.astype(F32) + b.astype(F32)).astype(BF)


def sum_kernel(at, a0, a1, a2, b0, b1, b2, keep, away):
    split = a0.shape[1]
    for cols, terms in ((slice(0, split), (a0, a1, a2)), (slice(split, WIDE), (b0, b1, b2))):
        total = sum(t[...].astype(F32) for t in terms[1:]) + terms[0][...].astype(F32)
        for z in range(8):
            to = slice(z * 16, (z + 1) * 16)
            low, high = total[z * 32 : z * 32 + 16], total[z * 32 + 16 : z * 32 + 32]
            keep[to, cols] = jnp.where(at[3] == 0, low, high).astype(BF)
            away[to, cols] = jnp.where(at[3] == 0, high, low).astype(BF)


def merge_kernel(at, keep, came, a, b, c, d, small, total):
    total[:, :WIDE] = (keep[...].astype(F32) + came[...].astype(F32)).astype(BF)
    terms = [r[...].astype(F32) for r in (a, b, c, d)]
    total[:, WIDE : WIDE + D] = (terms[0] + terms[1] + terms[2] + terms[3]).astype(BF)
    block = jnp.concatenate([small[...], jnp.zeros((4, 128), F32)], 0).astype(BF)
    total[:, WIDE + D :] = jnp.concatenate([block] * 8, 0)


def end_kernel(at, came, inner, outer, bias, qkv, proj, gain_a, gain_m):
    total = came[0].astype(F32)
    for k in range(1, 8):
        total = total + came[k].astype(F32)
    inner[...] = total[:, :D]
    outer[...] = total[:, D:WIDE]
    for c in range(3):
        qkv[c] = total[:, WIDE + c * WIDTH : WIDE + (c + 1) * WIDTH]
    proj[...] = total[:, WIDE + 3 * WIDTH : WIDE + D]
    small = total[:, WIDE + D :]
    for k in range(8):
        bias[:, k * 128 : (k + 1) * 128] = small[k : k + 1, :]
    for k in range(2):
        gain_a[:, k * 128 : (k + 1) * 128] = small[8 + k : 9 + k, :]
        gain_m[:, k * 128 : (k + 1) * 128] = small[10 + k : 11 + k, :]


def on_device(
    out_first,
    out_second,
    grad_first,
    grad_second,
    gain_attn,
    gain_mlp,
    qkv_weight,
    proj_weight,
    inner_weight,
    inner_bias,
    outer_weight,
):
    yhi, core, ylo, x = (lax.axis_index(a) for a in ("yhi", "core", "ylo", "x"))
    at = jnp.stack([yhi * 2 + core, core, x, ylo]).astype(jnp.int32)
    first, second, upper, lower = (
        a.reshape(SEQ, WIDTH) for a in (out_first, out_second, grad_first, grad_second)
    )
    block = (ROWS, D)

    first_y, lower_y = swap(first, "yhi"), swap(lower, "yhi")
    first_c, lower_c = swap(first, "core"), swap(lower, "core")
    first_b, lower_b = swap(first_y, "core"), swap(lower_y, "core")
    gain_a = gain_attn.reshape(1, D)
    qkv = jnp.moveaxis(qkv_weight, 1, 0)
    proj = proj_weight
    keep, away, left_in, left_out, right, bias_part = call(
        mlp_kernel,
        [(block, F32), (block, BF), (block, BF), (block, BF), ((ROWS, 2 * D), BF), ((1, D), F32)],
        [pltpu.VMEM(block, F32), pltpu.VMEM(block, F32)],
        8 * ROWS * D * D,
        at,
        first,
        first_c,
        first_y,
        first_b,
        lower,
        lower_c,
        lower_y,
        lower_b,
        second,
        upper,
        passed(jnp.stack([gain_mlp, inner_bias])),
        inner_weight,
        outer_weight,
        pause(8 << 30),
    )
    come = swap(away, "core")
    pair = (keep + come.astype(F32)).astype(BF)
    other = swap(pair, "yhi")
    done = added(pair, other)
    theirs = swap(done, "core")

    far_a, far_b, turned_in, turned_out = call(
        far_kernel,
        [((256, D), BF), ((256, D), BF), ((D, ROWS), BF), ((D, ROWS), BF)],
        [pltpu.VMEM((256, ROWS), BF)],
        D * ROWS * D,
        at,
        left_in,
        left_out,
        right,
    )
    came_a, came_b = around(far_a, 1), around(far_b, -1)
    a1, b1, a3, b3, a0, b0 = call(
        near_kernel,
        [((256, D), BF)] * 6,
        [pltpu.VMEM((256, ROWS), BF)],
        3 * D * ROWS * D,
        at,
        turned_in,
        turned_out,
        right,
    )
    near_b, near_a = around(b1, 1), around(a3, -1)
    join_a, join_b = added(a1, came_a), added(b3, came_b)
    joined_a, joined_b = around(join_a, 1), around(join_b, -1)
    mlp_keep, mlp_away = call(
        sum_kernel,
        [((128, WIDE), BF)] * 2,
        [],
        1 << 24,
        at,
        a0,
        near_a,
        joined_a,
        b0,
        near_b,
        joined_b,
    )
    mlp_came = swap(mlp_away, "ylo")

    given, back, normed, spread, input_second, back_first, gain_rows, own_left, away_left = call(
        before_kernel,
        [
            (block, BF),
            (block, BF),
            (block, F32),
            ((ROWS, 1), F32),
            ((SEQ, WIDTH), BF),
            ((SEQ, WIDTH), BF),
            ((8, WIDTH), F32),
            ((D, ROWS), BF),
            ((D, ROWS), BF),
        ],
        [pltpu.VMEM(block, F32), pltpu.VMEM((D, ROWS), BF)],
        ROWS * D * D,
        at,
        done,
        theirs,
        gain_a,
        pause(1 << 20),
    )
    came_left = swap(away_left, "ylo")
    (rows,) = call(attention_kernel, [(block, BF)], [], 4 * ROWS * D * D, at, given, back, qkv, proj)
    came_rows = swap(rows, "ylo")
    keep, away = call(
        close_kernel,
        [(block, F32), (block, BF)],
        [pltpu.VMEM(block, F32)],
        2 * ROWS * D * D,
        at,
        rows,
        normed,
        spread,
        gain_a,
        qkv,
        proj,
    )
    pieces = call(
        pieces_kernel,
        [((128, D), BF)] * 4,
        [],
        2 * D * ROWS * D,
        at,
        own_left,
        came_left,
        rows,
        came_rows,
    )
    came = [around(pieces[to], k) for to, k in enumerate(STEPS[:3])]
    mine, sent = call(
        close_pair_kernel,
        [((ROWS, HALF), F32), ((ROWS, HALF), BF)],
        [],
        1 << 22,
        at,
        keep,
        swap(away, "core"),
    )
    input_first, back_second, small = call(
        close_end_kernel,
        [((SEQ, WIDTH), BF), ((SEQ, WIDTH), BF), ((12, 128), F32)],
        [],
        1 << 22,
        at,
        mine,
        swap(sent, "yhi"),
        first,
        lower,
        gain_rows,
        bias_part.reshape(8, 128),
    )
    small = small + swap(small, "ylo")
    small = small + sum(around(small, k) for k in (1, 2, 3))
    (total,) = call(
        merge_kernel,
        [((128, WIDE + D + 128), BF)],
        [],
        1 << 22,
        at,
        mlp_keep,
        mlp_came,
        pieces[3],
        *came,
        small,
    )
    came = lax.all_to_all(total.reshape(8, 16, -1), "z", 0, 0, tiled=True)
    grad_inner, grad_outer, bias_sum, grad_qkv, grad_proj, gain_a_sum, gain_m_sum = call(
        end_kernel,
        [
            ((16, D), F32),
            ((16, D), F32),
            ((1, D), F32),
            ((3, 16, WIDTH), F32),
            ((16, WIDTH), F32),
            ((1, WIDTH), F32),
            ((1, WIDTH), F32),
        ],
        [],
        1 << 20,
        at,
        came,
    )

    shape_out = (1, SEQ, WIDTH)
    return (
        input_first.reshape(shape_out),
        input_second.reshape(shape_out),
        back_first.reshape(shape_out),
        back_second.reshape(shape_out),
        jnp.moveaxis(grad_qkv, 0, 1),
        grad_proj,
        grad_inner,
        bias_sum.reshape(D),
        grad_outer,
        gain_a_sum.reshape(WIDTH),
        gain_m_sum.reshape(WIDTH),
    )


def solution(mesh):
    split = Mesh(mesh.devices.reshape(8, 2, 4, 2, 2), AXES)
    rows = P(DP, None, TENSOR)
    return jax.shard_map(
        on_device,
        mesh=split,
        in_specs=(
            rows,
            rows,
            rows,
            rows,
            P(),
            P(),
            P(None, None, TENSOR),
            P(None, TENSOR),
            P(None, TENSOR),
            P(TENSOR),
            P(None, TENSOR),
        ),
        out_specs=(
            rows,
            rows,
            rows,
            rows,
            rows,
            P(DP, TENSOR),
            P(DP, TENSOR),
            P(TENSOR),
            P(DP, TENSOR),
            P(TENSOR),
            P(TENSOR),
        ),
        check_vma=False,
    )
```

time: 204 us -> 136 us (0.67)
  the two profiles are of different devices: /device:TPU:1 before, /device:TPU:8 now
where the time goes in v2:
time: 136 us
  waiting for transfers between devices  57.7 us (42%)
  starting transfers between devices  28.6 us (21%)
  blocking collectives  26.7 us (20%)
  Pallas kernels  19.8 us (15%)
  local copies, waits for them, and re-layouts  1.64 us (1%)
    ppermute x15, waiting for transfers between devices, swap(): return lax.ppermute(x, axis, SWAP)  31.3 us
    all_to_all x1, blocking collectives, on_device(): came = lax.all_to_all(total.reshape(8, 16, -1), 'z', 0, 0, tiled=True)  26.7 us
    ppermute x12, waiting for transfers between devices, around(): return lax.ppermute(x, 'x', [(i, (i + step) % 4) for i in range(4)])  26.4 us
    pallas_call x12, Pallas kernels, call(): pl.pallas_call(kernel, out_shape=[jax.ShapeDtypeStruct(s, d) for s, d in...  19.8 us
    ppermute x12, starting transfers between devices, around(): return lax.ppermute(x, 'x', [(i, (i + step) % 4) for i in range(4)])  15.9 us
    ppermute x15, starting transfers between devices, swap(): return lax.ppermute(x, axis, SWAP)  12.7 us
  transfers between devices with their start and end apart: 27, of which 14 were waited for; matrix products, arithmetic and copies ran while one was open for 0% of the time, Pallas kernels for 10%

profile of v2, /device:TPU:8, one launch (start us, length us, event | category | flops | bytes accessed | tf_op | source)
XLA Modules:
  0.0 136.0 jit_solution(4531288108448630473)
XLA Ops:
  0.6 2.4 %collective-permute-start.1 = (bf16[197,256]{1,0:T(8,128)(2,1)}, bf16[197,256]{1,0:T(8,128)(2,1)S(1)}, u32[]{:S(2)}, u32[]{:S(2)}) collective-permute-start(bf16[197,256]{1,0:T(8,128)(2,1)} %bitcast.25), channel_id=1, source_target_pairs={{0,2},{2,0},{1,3},{3,1},{4,6},{6,4},{5,7},{7,5},{8,10},{10,8},{9,1... | collective-permute-start | bytes 302600 | tf_op jit(solution)/shard_map/ppermute | solution.py:29
  3.0 1.2 collective-permute-start.4
  4.6 2.5 %collective-permute-done.1.f2 = bf16[197,256]{1,0:T(8,128)(2,1)S(1)} collective-permute-done((bf16[197,256]{1,0:T(8,128)(2,1)}, bf16[197,256]{1,0:T(8,128)(2,1)S(1)}, u32[]{:S(2)}, u32[]{:S(2)}) %collective-permute-start.1) | collective-permute-done | bytes 100896 | tf_op jit(solution)/shard_map/ppermute | solution.py:29
  7.1 2.9 %collective-permute-done.4.l2 = bf16[197,256]{1,0:T(8,128)(2,1)S(1)} collective-permute-done((bf16[197,256]{1,0:T(8,128)(2,1)}, bf16[197,256]{1,0:T(8,128)(2,1)S(1)}, u32[]{:S(2)}, u32[]{:S(2)}) %collective-permute-start.4) | collective-permute-done | bytes 100896 | tf_op jit(solution)/shard_map/ppermute | solution.py:29
  10.1 1.2 collective-permute-done.5.l3
  11.4 1.6 %copy-done.6 = bf16[1024,1024]{1,0:T(8,128)(2,1)S(1)} copy-done((bf16[1024,1024]{1,0:T(8,128)(2,1)S(1)}, bf16[1024,1024]{1,0:T(8,128)(2,1)}, u32[]{:S(2)}) %copy-start.6) | copy-done | bytes 2097176
  13.0 3.9 %shard_map.196 = (f32[208,1024]{1,0:T(8,128)S(1)}, bf16[208,1024]{1,0:T(8,128)(2,1)S(1)}, bf16[208,1024]{1,0:T(8,128)(2,1)S(1)}, bf16[208,1024]{1,0:T(8,128)(2,1...) custom-call(s32[4]{0:T(128)S(1)} %pad_add_fusion.at, bf16[197,256]{1,0:T(8,128)(2,1)S(1)} %bitcast.27, ...), custom_call_target="tpu_custom_call" | custom-call | flops 1744830464 | bytes 4194304 | tf_op jit(solution)/shard_map/pallas_call | solution.py:84
  16.9 0.2 collective-permute-start.6
  17.1 1.6 %collective-permute-done.6 = bf16[208,1024]{1,0:T(8,128)(2,1)S(1)} collective-permute-done((bf16[208,1024]{1,0:T(8,128)(2,1)S(1)}, bf16[208,1024]{1,0:T(8,128)(2,1)S(1)}, u32[]{:S(2)}, u32[]{:S(2)}) %collective-permute-start.6) | collective-permute-done | bytes 426016 | tf_op jit(solution)/shard_map/ppermute | solution.py:29
  18.9 1.6 %collective-permute-start.7 = (bf16[208,1024]{1,0:T(8,128)(2,1)S(1)}, bf16[208,1024]{1,0:T(8,128)(2,1)S(1)}, u32[]{:S(2)}, u32[]{:S(2)}) collective-permute-start(bf16[208,1024]{1,0:T(8,128)(2,1)S(1)} %add_convert_fusion.3), channel_id=1, source_target_pairs={{0,2},{2,0},{1,3},{3,1},{4,6},{6,4},{5,7},{7,5},{8,10},{10,8},{9,1... | collective-permute-start | bytes 1277960 | tf_op jit(solution)/shard_map/ppermute | solution.py:29
  20.5 1.2 shard_map.203
  21.7 1.6 %collective-permute-start.12 = (bf16[256,1024]{1,0:T(8,128)(2,1)S(1)}, bf16[256,1024]{1,0:T(8,128)(2,1)S(1)}, u32[]{:S(2)}, u32[]{:S(2)}) collective-permute-start(bf16[256,1024]{1,0:T(8,128)(2,1)S(1)} %get-tuple-element.80), channel_id=1, source_target_pairs={{0,4},{4,8},{8,12},{12,0},{1,5},{5,9},{9,13},{13,1},{2,6},{6,10},{... | collective-permute-start | bytes 1572872 | tf_op jit(solution)/shard_map/ppermute | solution.py:33
  23.3 1.7 %collective-permute-start.15 = (bf16[256,1024]{1,0:T(8,128)(2,1)S(1)}, bf16[256,1024]{1,0:T(8,128)(2,1)S(1)}, u32[]{:S(2)}, u32[]{:S(2)}) collective-permute-start(bf16[256,1024]{1,0:T(8,128)(2,1)S(1)} %get-tuple-element.84), channel_id=1, source_target_pairs={{0,12},{4,0},{8,4},{12,8},{1,13},{5,1},{9,5},{13,9},{2,14},{6,2},{... | collective-permute-start | bytes 1572872 | tf_op jit(solution)/shard_map/ppermute | solution.py:33
  25.0 1.5 %shard_map.204 = (bf16[256,1024]{1,0:T(8,128)(2,1)S(1)}, bf16[256,1024]{1,0:T(8,128)(2,1)S(1)}, bf16[256,1024]{1,0:T(8,128)(2,1)S(1)}, bf16[256,1024]{1,0:T(8,12...) custom-call(s32[4]{0:T(128)S(1)} %pad_add_fusion.at, ...), custom_call_target="tpu_custom_call" | custom-call | flops 654311424 | bytes 4194304 | tf_op jit(solution)/shard_map/pallas_call | solution.py:84
  26.6 1.6 %collective-permute-start.11 = (bf16[256,1024]{1,0:T(8,128)(2,1)S(1)}, bf16[256,1024]{1,0:T(8,128)(2,1)S(1)}, u32[]{:S(2)}, u32[]{:S(2)}) collective-permute-start(bf16[256,1024]{1,0:T(8,128)(2,1)S(1)} %get-tuple-element.78), channel_id=1, source_target_pairs={{0,12},{4,0},{8,4},{12,8},{1,13},{5,1},{9,5},{13,9},{2,14},{6,2},{... | collective-permute-start | bytes 1572872 | tf_op jit(solution)/shard_map/ppermute | solution.py:33
  28.2 0.5 collective-permute-start.14
  28.7 3.7 %collective-permute-done.7 = bf16[208,1024]{1,0:T(8,128)(2,1)S(1)} collective-permute-done((bf16[208,1024]{1,0:T(8,128)(2,1)S(1)}, bf16[208,1024]{1,0:T(8,128)(2,1)S(1)}, u32[]{:S(2)}, u32[]{:S(2)}) %collective-permute-start.7) | collective-permute-done | bytes 426016 | tf_op jit(solution)/shard_map/ppermute | solution.py:29
  32.6 5.2 %collective-permute-done.12 = bf16[256,1024]{1,0:T(8,128)(2,1)S(1)} collective-permute-done((bf16[256,1024]{1,0:T(8,128)(2,1)S(1)}, bf16[256,1024]{1,0:T(8,128)(2,1)S(1)}, u32[]{:S(2)}, u32[]{:S(2)}) %collective-permute-start.12) | collective-permute-done | bytes 524320 | tf_op jit(solution)/shard_map/ppermute | solution.py:33
  38.0 0.4 collective-permute-start.13
  38.5 3.0 %collective-permute-start.16 = (bf16[256,1024]{1,0:T(8,128)(2,1)S(1)}, bf16[256,1024]{1,0:T(8,128)(2,1)S(1)}, u32[]{:S(2)}, u32[]{:S(2)}) collective-permute-start(bf16[256,1024]{1,0:T(8,128)(2,1)S(1)} %add_convert_fusion), channel_id=1, source_target_pairs={{0,12},{4,0},{8,4},{12,8},{1,13},{5,1},{9,5},{13,9},{2,14},{6,2},{... | collective-permute-start | bytes 1572872 | tf_op jit(solution)/shard_map/ppermute | solution.py:33
  41.6 2.0 %shard_map.198 = (bf16[208,1024]{1,0:T(8,128)(2,1)S(1)}, bf16[208,1024]{1,0:T(8,128)(2,1)S(1)}, f32[208,1024]{1,0:T(8,128)S(1)}, f32[208,1]{1,0:T(8,128)S(1)}, b...) custom-call(s32[4]{0:T(128)S(1)} %pad_add_fusion.at, ...), custom_call_target="tpu_custom_call" | custom-call | flops 218103808 | bytes 4194304 | tf_op jit(solution)/shard_map/pallas_call | solution.py:84
  43.6 3.3 %shard_map.199.rows.own_right = bf16[208,1024]{1,0:T(8,128)(2,1)S(1)} custom-call(s32[4]{0:T(128)S(1)} %pad_add_fusion.at, bf16[208,1024]{1,0:T(8,128)(2,1)S(1)} %get-tuple-element.58.given, bf16[208,1024]{1,0:T(8,128)(2,1)S(1)} %get-tuple-element.59.back, bf16[3,1024,256]{2,1,0:T(8,128)(2,1)S(1)} %bitcast.22, bf16[1024,256]{1,0:T(8,128)(2,1)S(1)} %copy-done.1), custom_call_target="tpu_custom_call" | custom-call | flops 872415232 | bytes 4194304 | tf_op jit(solution)/shard_map/pallas_call | solution.py:84
  46.8 1.7 %shard_map.200 = (f32[208,1024]{1,0:T(8,128)S(1)}, bf16[208,1024]{1,0:T(8,128)(2,1)S(1)}) custom-call(s32[4]{0:T(128)S(1)} %pad_add_fusion.at, bf16[208,1024]{1,0:T(8,128)(2,1)S(1)} %shard_map.199.rows.own_right, f32[208,1024]{1,0:T(8,128)S(1)} %get-tuple-element.60.normed, f32[208,1]{1,0:T(8,128)S(1)} %get-tuple-element.61.spread, f32[1,1024]{1,0:T(1,128)S(1)} %bitcast.34, ...), custom_call_target="tpu_custom_call" | custom-call | flops 436207616 | bytes 4194304 | tf_op jit(solution)/shard_map/pallas_call | solution.py:84
  48.6 0.7 collective-permute-done.11.a1
  49.3 1.3 collective-permute-start.19
  50.6 0.7 collective-permute-start.18
  51.3 7.8 %collective-permute-done.13.a2 = bf16[256,1024]{1,0:T(8,128)(2,1)S(1)} collective-permute-done((bf16[256,1024]{1,0:T(8,128)(2,1)S(1)}, bf16[256,1024]{1,0:T(8,128)(2,1)S(1)}, u32[]{:S(2)}, u32[]{:S(2)}) %collective-permute-start.13) | collective-permute-done | bytes 524320 | tf_op jit(solution)/shard_map/ppermute | solution.py:33
  59.1 1.0 shard_map.205
  60.1 1.9 %collective-permute-start.17 = (bf16[128,2048]{1,0:T(8,128)(2,1)S(1)}, bf16[128,2048]{1,0:T(8,128)(2,1)S(1)}, u32[]{:S(2)}, u32[]{:S(2)}) collective-permute-start(bf16[128,2048]{1,0:T(8,128)(2,1)S(1)} %get-tuple-element.86), channel_id=1, source_target_pairs={{0,16},{16,0},{1,17},{17,1},{2,18},{18,2},{3,19},{19,3},{4,20},{20... | collective-permute-start | bytes 1572872 | tf_op jit(solution)/shard_map/ppermute | solution.py:29
  62.1 0.7 shard_map.201
  62.7 1.0 collective-permute-start.10
  63.8 9.5 %collective-permute-done.18.came_left = bf16[1024,208]{1,0:T(8,128)(2,1)S(1)} collective-permute-done((bf16[1024,208]{1,0:T(8,128)(2,1)S(1)}, bf16[1024,208]{1,0:T(8,128)(2,1)S(1)}, u32[]{:S(2)}, u32[]{:S(2)}) %collective-permute-start.18) | collective-permute-done | bytes 426016 | tf_op jit(solution)/shard_map/ppermute | solution.py:29
  73.2 1.3 shard_map.206
  74.5 2.8 %collective-permute-start.20 = (bf16[128,1024]{1,0:T(8,128)(2,1)S(1)}, bf16[128,1024]{1,0:T(8,128)(2,1)S(1)}, u32[]{:S(2)}, u32[]{:S(2)}) collective-permute-start(bf16[128,1024]{1,0:T(8,128)(2,1)S(1)} %get-tuple-element.90), channel_id=1, source_target_pairs={{0,8},{4,12},{8,0},{12,4},{1,9},{5,13},{9,1},{13,5},{2,10},{6,14},... | collective-permute-start | bytes 786440 | tf_op jit(solution)/shard_map/ppermute | solution.py:33
  77.3 1.1 collective-permute-start.21
  78.4 2.2 %collective-permute-start.22 = (bf16[128,1024]{1,0:T(8,128)(2,1)S(1)}, bf16[128,1024]{1,0:T(8,128)(2,1)S(1)}, u32[]{:S(2)}, u32[]{:S(2)}) collective-permute-start(bf16[128,1024]{1,0:T(8,128)(2,1)S(1)} %get-tuple-element.92), channel_id=1, source_target_pairs={{0,12},{4,0},{8,4},{12,8},{1,13},{5,1},{9,5},{13,9},{2,14},{6,2},{... | collective-permute-start | bytes 786440 | tf_op jit(solution)/shard_map/ppermute | solution.py:33
  80.6 8.1 %collective-permute-done.10.came = bf16[208,512]{1,0:T(8,128)(2,1)S(1)} collective-permute-done((bf16[208,512]{1,0:T(8,128)(2,1)S(1)}, bf16[208,512]{1,0:T(8,128)(2,1)S(1)}, u32[]{:S(2)}, u32[]{:S(2)}) %collective-permute-start.10) | collective-permute-done | bytes 213024 | tf_op jit(solution)/shard_map/ppermute | solution.py:29
  88.6 1.3 shard_map.202
  89.9 1.8 %collective-permute-start.23 = (f32[12,128]{1,0:T(8,128)S(1)}, f32[12,128]{1,0:T(8,128)S(1)}, u32[]{:S(2)}, u32[]{:S(2)}) collective-permute-start(f32[12,128]{1,0:T(8,128)S(1)} %get-tuple-element.93), channel_id=1, source_target_pairs={{0,16},{16,0},{1,17},{17,1},{2,18},{18,2},{3,19},{19,3},{4,20},{20... | collective-permute-start | bytes 18440 | tf_op jit(solution)/shard_map/ppermute | solution.py:29
  91.7 1.8 %collective-permute-done.23 = f32[12,128]{1,0:T(8,128)S(1)} collective-permute-done((f32[12,128]{1,0:T(8,128)S(1)}, f32[12,128]{1,0:T(8,128)S(1)}, u32[]{:S(2)}, u32[]{:S(2)}) %collective-permute-start.23) | collective-permute-done | bytes 6176 | tf_op jit(solution)/shard_map/ppermute | solution.py:29
  93.5 0.5 collective-permute-start.26
  94.0 3.2 %collective-permute-done.26 = f32[12,128]{1,0:T(8,128)S(1)} collective-permute-done((f32[12,128]{1,0:T(8,128)S(1)}, f32[12,128]{1,0:T(8,128)S(1)}, u32[]{:S(2)}, u32[]{:S(2)}) %collective-permute-start.26) | collective-permute-done | bytes 6176 | tf_op jit(solution)/shard_map/ppermute | solution.py:33
  97.2 0.5 collective-permute-start.25
  97.7 4.6 %collective-permute-done.25 = f32[12,128]{1,0:T(8,128)S(1)} collective-permute-done((f32[12,128]{1,0:T(8,128)S(1)}, f32[12,128]{1,0:T(8,128)S(1)}, u32[]{:S(2)}, u32[]{:S(2)}) %collective-permute-start.25) | collective-permute-done | bytes 6176 | tf_op jit(solution)/shard_map/ppermute | solution.py:33
  102.3 4.9 %collective-permute-done.24 = f32[12,128]{1,0:T(8,128)S(1)} collective-permute-done((f32[12,128]{1,0:T(8,128)S(1)}, f32[12,128]{1,0:T(8,128)S(1)}, u32[]{:S(2)}, u32[]{:S(2)}) %collective-permute-start.24) | collective-permute-done | bytes 6176 | tf_op jit(solution)/shard_map/ppermute | solution.py:33
  107.3 0.8 shard_map.207
  108.1 26.7 %all_to_all.5.came = bf16[8,16,3200]{2,1,0:T(8,128)(2,1)S(1)} all-to-all(bf16[8,16,3200]{2,1,0:T(8,128)(2,1)S(1)} %bitcast.24), channel_id=1, replica_groups=mesh['z'=8,'ylo'=2,'x'=4,'yhi'=2,'core'=2] {'z'}, dimensions={0} | all-to-all | bytes 1638400 | tf_op jit(solution)/shard_map/all_to_all | solution.py:517
  134.7 1.3 shard_map.208
  (52 shorter events, 1.3 us)
Async XLA Ops:
  0.6 6.5 %collective-permute-start.1 = (bf16[197,256]{1,0:T(8,128)(2,1)}, bf16[197,256]{1,0:T(8,128)(2,1)S(1)}, u32[]{:S(2)}, u32[]{:S(2)}) collective-permute-start(bf16[197,256]{1,0:T(8,128)(2,1)} %bitcast.25), channel_id=1, source_target_pairs={{0,2},{2,0},{1,3},{3,1},{4,6},{6,4},{5,7},{7,5},{8,10},{10,8},{9,1... | collective-permute-start | bytes 302600 | tf_op jit(solution)/shard_map/ppermute | solution.py:29
  3.0 7.1 %collective-permute-start = (bf16[197,256]{1,0:T(8,128)(2,1)}, bf16[197,256]{1,0:T(8,128)(2,1)S(1)}, u32[]{:S(2)}, u32[]{:S(2)}) collective-permute-start(bf16[197,256]{1,0:T(8,128)(2,1)} %bitcast.26), channel_id=1, source_target_pairs={{0,1},{1,0},{2,3},{3,2},{4,5},{5,4},{6,7},{7,6},{8,9},{9,8},{10,11... | collective-permute-start | bytes 302600 | tf_op jit(solution)/shard_map/ppermute | solution.py:29
  3.0 1.5 %copy-start.9 = (f32[1024]{0:T(1024)S(1)}, f32[1024]{0:T(1024)}, u32[]{:S(2)}) copy-start(f32[1024]{0:T(1024)} %param.20) | copy-start | bytes 12292
  3.0 1.5 %copy-start.10 = (f32[1024]{0:T(1024)S(1)}, f32[1024]{0:T(1024)}, u32[]{:S(2)}) copy-start(f32[1024]{0:T(1024)} %param.16) | copy-start | bytes 12292
  3.0 7.0 %collective-permute-start.4 = (bf16[197,256]{1,0:T(8,128)(2,1)}, bf16[197,256]{1,0:T(8,128)(2,1)S(1)}, u32[]{:S(2)}, u32[]{:S(2)}) collective-permute-start(bf16[197,256]{1,0:T(8,128)(2,1)} %bitcast.29), channel_id=1, source_target_pairs={{0,2},{2,0},{1,3},{3,1},{4,6},{6,4},{5,7},{7,5},{8,10},{10,8},{9,1... | collective-permute-start | bytes 302600 | tf_op jit(solution)/shard_map/ppermute | solution.py:29
  4.3 5.9 %collective-permute-start.3 = (bf16[197,256]{1,0:T(8,128)(2,1)}, bf16[197,256]{1,0:T(8,128)(2,1)S(1)}, u32[]{:S(2)}, u32[]{:S(2)}) collective-permute-start(bf16[197,256]{1,0:T(8,128)(2,1)} %bitcast.30), channel_id=1, source_target_pairs={{0,1},{1,0},{2,3},{3,2},{4,5},{5,4},{6,7},{7,6},{8,9},{9,8},{10,11... | collective-permute-start | bytes 302600 | tf_op jit(solution)/shard_map/ppermute | solution.py:29
  4.5 6.8 %copy-start.2 = (bf16[1,197,256]{2,1,0:T(8,128)(2,1)S(1)}, bf16[1,197,256]{2,1,0:T(8,128)(2,1)}, u32[]{:S(2)}) copy-start(bf16[1,197,256]{2,1,0:T(8,128)(2,1)} %param.11) | copy-start | bytes 302596
  4.5 6.8 %copy-start.3 = (bf16[1,197,256]{2,1,0:T(8,128)(2,1)S(1)}, bf16[1,197,256]{2,1,0:T(8,128)(2,1)}, u32[]{:S(2)}) copy-start(bf16[1,197,256]{2,1,0:T(8,128)(2,1)} %param.14) | copy-start | bytes 302596
  4.5 6.8 %copy-start.5 = (bf16[1024,1024]{1,0:T(8,128)(2,1)S(1)}, bf16[1024,1024]{1,0:T(8,128)(2,1)}, u32[]{:S(2)}) copy-start(bf16[1024,1024]{1,0:T(8,128)(2,1)} %inner.1) | copy-start | bytes 6291460
  4.6 6.8 %copy-start.7 = (bf16[1,197,256]{2,1,0:T(8,128)(2,1)S(1)}, bf16[1,197,256]{2,1,0:T(8,128)(2,1)}, u32[]{:S(2)}) copy-start(bf16[1,197,256]{2,1,0:T(8,128)(2,1)} %param.12) | copy-start | bytes 302596
  4.6 6.8 %copy-start.8 = (bf16[1,197,256]{2,1,0:T(8,128)(2,1)S(1)}, bf16[1,197,256]{2,1,0:T(8,128)(2,1)}, u32[]{:S(2)}) copy-start(bf16[1,197,256]{2,1,0:T(8,128)(2,1)} %param.13) | copy-start | bytes 302596
  7.1 3.0 %collective-permute-start.2 = (bf16[197,256]{1,0:T(8,128)(2,1)S(1)}, bf16[197,256]{1,0:T(8,128)(2,1)S(1)}, u32[]{:S(2)}, u32[]{:S(2)}) collective-permute-start(bf16[197,256]{1,0:T(8,128)(2,1)S(1)} %collective-permute-done.1.f2), channel_id=1, source_target_pairs={{0,1},{1,0},{2,3},{3,2},{4,5},{5,4},{6,7},{7,6},{8,9},{9,8},{10,11... | collective-permute-start | bytes 302600 | tf_op jit(solution)/shard_map/ppermute | solution.py:29
  10.0 1.3 collective-permute-start.5
  11.4 1.6 %copy-start.6 = (bf16[1024,1024]{1,0:T(8,128)(2,1)S(1)}, bf16[1024,1024]{1,0:T(8,128)(2,1)}, u32[]{:S(2)}) copy-start(bf16[1024,1024]{1,0:T(8,128)(2,1)} %outer.1) | copy-start | bytes 6291460
  16.9 1.9 %collective-permute-start.6 = (bf16[208,1024]{1,0:T(8,128)(2,1)S(1)}, bf16[208,1024]{1,0:T(8,128)(2,1)S(1)}, u32[]{:S(2)}, u32[]{:S(2)}) collective-permute-start(bf16[208,1024]{1,0:T(8,128)(2,1)S(1)} %get-tuple-element.57), channel_id=1, source_target_pairs={{0,1},{1,0},{2,3},{3,2},{4,5},{5,4},{6,7},{7,6},{8,9},{9,8},{10,11... | collective-permute-start | bytes 1277960 | tf_op jit(solution)/shard_map/ppermute | solution.py:29
  18.9 13.5 %collective-permute-start.7 = (bf16[208,1024]{1,0:T(8,128)(2,1)S(1)}, bf16[208,1024]{1,0:T(8,128)(2,1)S(1)}, u32[]{:S(2)}, u32[]{:S(2)}) collective-permute-start(bf16[208,1024]{1,0:T(8,128)(2,1)S(1)} %add_convert_fusion.3), channel_id=1, source_target_pairs={{0,2},{2,0},{1,3},{3,1},{4,6},{6,4},{5,7},{7,5},{8,10},{10,8},{9,1... | collective-permute-start | bytes 1277960 | tf_op jit(solution)/shard_map/ppermute | solution.py:29
  21.7 16.1 %collective-permute-start.12 = (bf16[256,1024]{1,0:T(8,128)(2,1)S(1)}, bf16[256,1024]{1,0:T(8,128)(2,1)S(1)}, u32[]{:S(2)}, u32[]{:S(2)}) collective-permute-start(bf16[256,1024]{1,0:T(8,128)(2,1)S(1)} %get-tuple-element.80), channel_id=1, source_target_pairs={{0,4},{4,8},{8,12},{12,0},{1,5},{5,9},{9,13},{13,1},{2,6},{6,10},{... | collective-permute-start | bytes 1572872 | tf_op jit(solution)/shard_map/ppermute | solution.py:33
  23.3 15.1 %collective-permute-start.15 = (bf16[256,1024]{1,0:T(8,128)(2,1)S(1)}, bf16[256,1024]{1,0:T(8,128)(2,1)S(1)}, u32[]{:S(2)}, u32[]{:S(2)}) collective-permute-start(bf16[256,1024]{1,0:T(8,128)(2,1)S(1)} %get-tuple-element.84), channel_id=1, source_target_pairs={{0,12},{4,0},{8,4},{12,8},{1,13},{5,1},{9,5},{13,9},{2,14},{6,2},{... | collective-permute-start | bytes 1572872 | tf_op jit(solution)/shard_map/ppermute | solution.py:33
  26.6 22.7 %collective-permute-start.11 = (bf16[256,1024]{1,0:T(8,128)(2,1)S(1)}, bf16[256,1024]{1,0:T(8,128)(2,1)S(1)}, u32[]{:S(2)}, u32[]{:S(2)}) collective-permute-start(bf16[256,1024]{1,0:T(8,128)(2,1)S(1)} %get-tuple-element.78), channel_id=1, source_target_pairs={{0,12},{4,0},{8,4},{12,8},{1,13},{5,1},{9,5},{13,9},{2,14},{6,2},{... | collective-permute-start | bytes 1572872 | tf_op jit(solution)/shard_map/ppermute | solution.py:33
  28.2 13.4 %copy-start.4 = (f32[1024]{0:T(1024)S(1)}, f32[1024]{0:T(1024)}, u32[]{:S(2)}) copy-start(f32[1024]{0:T(1024)} %param.15) | copy-start | bytes 12292
  28.2 22.4 %collective-permute-start.14 = (bf16[256,1024]{1,0:T(8,128)(2,1)S(1)}, bf16[256,1024]{1,0:T(8,128)(2,1)S(1)}, u32[]{:S(2)}, u32[]{:S(2)}) collective-permute-start(bf16[256,1024]{1,0:T(8,128)(2,1)S(1)} %get-tuple-element.82), channel_id=1, source_target_pairs={{0,4},{4,8},{8,12},{12,0},{1,5},{5,9},{9,13},{13,1},{2,6},{6,10},{... | collective-permute-start | bytes 1572872 | tf_op jit(solution)/shard_map/ppermute | solution.py:33
  32.5 11.1 %copy-start = (bf16[1024,3,256]{2,0,1:T(8,128)(2,1)S(1)}, bf16[1024,3,256]{2,0,1:T(8,128)(2,1)}, u32[]{:S(2)}) copy-start(bf16[1024,3,256]{2,0,1:T(8,128)(2,1)} %param.17) | copy-start | bytes 4718596
  32.5 11.1 %copy-start.1 = (bf16[1024,256]{1,0:T(8,128)(2,1)S(1)}, bf16[1024,256]{1,0:T(8,128)(2,1)}, u32[]{:S(2)}) copy-start(bf16[1024,256]{1,0:T(8,128)(2,1)} %proj.3) | copy-start | bytes 1572868
  32.5 9.1 %collective-permute-start.8 = (bf16[208,1024]{1,0:T(8,128)(2,1)S(1)}, bf16[208,1024]{1,0:T(8,128)(2,1)S(1)}, u32[]{:S(2)}, u32[]{:S(2)}) collective-permute-start(bf16[208,1024]{1,0:T(8,128)(2,1)S(1)} %add_convert_fusion.2.done), channel_id=1, source_target_pairs={{0,1},{1,0},{2,3},{3,2},{4,5},{5,4},{6,7},{7,6},{8,9},{9,8},{10,11... | collective-permute-start | bytes 1277960 | tf_op jit(solution)/shard_map/ppermute | solution.py:29
  38.0 21.2 %collective-permute-start.13 = (bf16[256,1024]{1,0:T(8,128)(2,1)S(1)}, bf16[256,1024]{1,0:T(8,128)(2,1)S(1)}, u32[]{:S(2)}, u32[]{:S(2)}) collective-permute-start(bf16[256,1024]{1,0:T(8,128)(2,1)S(1)} %add_convert_fusion.1), channel_id=1, source_target_pairs={{0,4},{4,8},{8,12},{12,0},{1,5},{5,9},{9,13},{13,1},{2,6},{6,10},{... | collective-permute-start | bytes 1572872 | tf_op jit(solution)/shard_map/ppermute | solution.py:33
  38.5 20.6 %collective-permute-start.16 = (bf16[256,1024]{1,0:T(8,128)(2,1)S(1)}, bf16[256,1024]{1,0:T(8,128)(2,1)S(1)}, u32[]{:S(2)}, u32[]{:S(2)}) collective-permute-start(bf16[256,1024]{1,0:T(8,128)(2,1)S(1)} %add_convert_fusion), channel_id=1, source_target_pairs={{0,12},{4,0},{8,4},{12,8},{1,13},{5,1},{9,5},{13,9},{2,14},{6,2},{... | collective-permute-start | bytes 1572872 | tf_op jit(solution)/shard_map/ppermute | solution.py:33
  48.5 13.6 %collective-permute-start.9 = (bf16[208,1024]{1,0:T(8,128)(2,1)S(1)}, bf16[208,1024]{1,0:T(8,128)(2,1)S(1)}, u32[]{:S(2)}, u32[]{:S(2)}) collective-permute-start(bf16[208,1024]{1,0:T(8,128)(2,1)S(1)} %get-tuple-element.63), channel_id=1, source_target_pairs={{0,1},{1,0},{2,3},{3,2},{4,5},{5,4},{6,7},{7,6},{8,9},{9,8},{10,11... | collective-permute-start | bytes 1277960 | tf_op jit(solution)/shard_map/ppermute | solution.py:29
  49.3 14.5 %collective-permute-start.19 = (bf16[208,1024]{1,0:T(8,128)(2,1)S(1)}, bf16[208,1024]{1,0:T(8,128)(2,1)S(1)}, u32[]{:S(2)}, u32[]{:S(2)}) collective-permute-start(bf16[208,1024]{1,0:T(8,128)(2,1)S(1)} %shard_map.199.rows.own_right), channel_id=1, source_target_pairs={{0,16},{16,0},{1,17},{17,1},{2,18},{18,2},{3,19},{19,3},{4,20},{20... | collective-permute-start | bytes 1277960 | tf_op jit(solution)/shard_map/ppermute | solution.py:29
  50.6 22.6 %collective-permute-start.18 = (bf16[1024,208]{1,0:T(8,128)(2,1)S(1)}, bf16[1024,208]{1,0:T(8,128)(2,1)S(1)}, u32[]{:S(2)}, u32[]{:S(2)}) collective-permute-start(bf16[1024,208]{1,0:T(8,128)(2,1)S(1)} %get-tuple-element.88), channel_id=1, source_target_pairs={{0,16},{16,0},{1,17},{17,1},{2,18},{18,2},{3,19},{19,3},{4,20},{20... | collective-permute-start | bytes 1277960 | tf_op jit(solution)/shard_map/ppermute | solution.py:29
  60.1 47.1 %collective-permute-start.17 = (bf16[128,2048]{1,0:T(8,128)(2,1)S(1)}, bf16[128,2048]{1,0:T(8,128)(2,1)S(1)}, u32[]{:S(2)}, u32[]{:S(2)}) collective-permute-start(bf16[128,2048]{1,0:T(8,128)(2,1)S(1)} %get-tuple-element.86), channel_id=1, source_target_pairs={{0,16},{16,0},{1,17},{17,1},{2,18},{18,2},{3,19},{19,3},{4,20},{20... | collective-permute-start | bytes 1572872 | tf_op jit(solution)/shard_map/ppermute | solution.py:29
  62.7 25.9 %collective-permute-start.10 = (bf16[208,512]{1,0:T(8,128)(2,1)S(1)}, bf16[208,512]{1,0:T(8,128)(2,1)S(1)}, u32[]{:S(2)}, u32[]{:S(2)}) collective-permute-start(bf16[208,512]{1,0:T(8,128)(2,1)S(1)} %get-tuple-element.65), channel_id=1, source_target_pairs={{0,2},{2,0},{1,3},{3,1},{4,6},{6,4},{5,7},{7,5},{8,10},{10,8},{9,1... | collective-permute-start | bytes 638984 | tf_op jit(solution)/shard_map/ppermute | solution.py:29
  74.5 32.7 %collective-permute-start.20 = (bf16[128,1024]{1,0:T(8,128)(2,1)S(1)}, bf16[128,1024]{1,0:T(8,128)(2,1)S(1)}, u32[]{:S(2)}, u32[]{:S(2)}) collective-permute-start(bf16[128,1024]{1,0:T(8,128)(2,1)S(1)} %get-tuple-element.90), channel_id=1, source_target_pairs={{0,8},{4,12},{8,0},{12,4},{1,9},{5,13},{9,1},{13,5},{2,10},{6,14},... | collective-permute-start | bytes 786440 | tf_op jit(solution)/shard_map/ppermute | solution.py:33
  77.3 29.9 %collective-permute-start.21 = (bf16[128,1024]{1,0:T(8,128)(2,1)S(1)}, bf16[128,1024]{1,0:T(8,128)(2,1)S(1)}, u32[]{:S(2)}, u32[]{:S(2)}) collective-permute-start(bf16[128,1024]{1,0:T(8,128)(2,1)S(1)} %get-tuple-element.91), channel_id=1, source_target_pairs={{0,4},{4,8},{8,12},{12,0},{1,5},{5,9},{9,13},{13,1},{2,6},{6,10},{... | collective-permute-start | bytes 786440 | tf_op jit(solution)/shard_map/ppermute | solution.py:33
  78.4 28.8 %collective-permute-start.22 = (bf16[128,1024]{1,0:T(8,128)(2,1)S(1)}, bf16[128,1024]{1,0:T(8,128)(2,1)S(1)}, u32[]{:S(2)}, u32[]{:S(2)}) collective-permute-start(bf16[128,1024]{1,0:T(8,128)(2,1)S(1)} %get-tuple-element.92), channel_id=1, source_target_pairs={{0,12},{4,0},{8,4},{12,8},{1,13},{5,1},{9,5},{13,9},{2,14},{6,2},{... | collective-permute-start | bytes 786440 | tf_op jit(solution)/shard_map/ppermute | solution.py:33
  89.9 3.7 %collective-permute-start.23 = (f32[12,128]{1,0:T(8,128)S(1)}, f32[12,128]{1,0:T(8,128)S(1)}, u32[]{:S(2)}, u32[]{:S(2)}) collective-permute-start(f32[12,128]{1,0:T(8,128)S(1)} %get-tuple-element.93), channel_id=1, source_target_pairs={{0,16},{16,0},{1,17},{17,1},{2,18},{18,2},{3,19},{19,3},{4,20},{20... | collective-permute-start | bytes 18440 | tf_op jit(solution)/shard_map/ppermute | solution.py:29
  93.5 3.7 %collective-permute-start.26 = (f32[12,128]{1,0:T(8,128)S(1)}, f32[12,128]{1,0:T(8,128)S(1)}, u32[]{:S(2)}, u32[]{:S(2)}) collective-permute-start(f32[12,128]{1,0:T(8,128)S(1)} %add.32), channel_id=1, source_target_pairs={{0,12},{4,0},{8,4},{12,8},{1,13},{5,1},{9,5},{13,9},{2,14},{6,2},{... | collective-permute-start | bytes 18440 | tf_op jit(solution)/shard_map/ppermute | solution.py:33
  97.2 5.2 %collective-permute-start.25 = (f32[12,128]{1,0:T(8,128)S(1)}, f32[12,128]{1,0:T(8,128)S(1)}, u32[]{:S(2)}, u32[]{:S(2)}) collective-permute-start(f32[12,128]{1,0:T(8,128)S(1)} %add.32), channel_id=1, source_target_pairs={{0,8},{4,12},{8,0},{12,4},{1,9},{5,13},{9,1},{13,5},{2,10},{6,14},... | collective-permute-start | bytes 18440 | tf_op jit(solution)/shard_map/ppermute | solution.py:33
  102.3 4.9 %collective-permute-start.24 = (f32[12,128]{1,0:T(8,128)S(1)}, f32[12,128]{1,0:T(8,128)S(1)}, u32[]{:S(2)}, u32[]{:S(2)}) collective-permute-start(f32[12,128]{1,0:T(8,128)S(1)} %add.32), channel_id=1, source_target_pairs={{0,4},{4,8},{8,12},{12,0},{1,5},{5,9},{9,13},{13,1},{2,6},{6,10},{... | collective-permute-start | bytes 18440 | tf_op jit(solution)/shard_map/ppermute | solution.py:33

commit v3 on v2

--- a/solution.py
+++ b/solution.py
@@ -106,19 +106,19 @@
     )()
 
 
-def pass_kernel(values, out):
+def pass_kernel(values, weight, out):
     out[...] = values[...]
 
 
-def passed(values):
+def passed(values, weight):
     return pl.pallas_call(
         pass_kernel,
         out_shape=jax.ShapeDtypeStruct(values.shape, values.dtype),
-        in_specs=[VMEM],
+        in_specs=[VMEM, ANY],
         out_specs=VMEM,
         cost_estimate=pl.CostEstimate(flops=8 << 30, bytes_accessed=1 << 20, transcendentals=0),
         compiler_params=pltpu.CompilerParams(vmem_limit_bytes=1 << 20),
-    )(values)
+    )(values, weight)
 
 
 def mlp_kernel(
@@ -198,7 +198,7 @@
     sorted_rows(back, 512)
 
 
-def attention_kernel(at, given, back, qkv, proj, rows_out):
+def attention_kernel(at, given, back, qkv, proj, bias, gain_m, rows_out):
     rows = [dot(given[...], qkv[c]).astype(BF) for c in range(3)]
     grads = dot(back[...], proj[...]).astype(BF)
     valid = lax.broadcasted_iota(jnp.int32, (1, ROWS), 1) < SEQ
@@ -219,10 +219,14 @@
         query_parts.append(dot(grad_scores, k) * FACTOR)
         key_parts.append(t_dot(grad_scores, q) * FACTOR)
     for n, parts in enumerate((query_parts, key_parts, value_parts, out_parts)):
-        rows_out[:, n * WIDTH : (n + 1) * WIDTH] = jnp.concatenate(parts, 1).astype(BF)
-
-
-def close_kernel(at, rows, normed, spread, gain, qkv, proj, keep, away, part):
+        to = slice(n * WIDTH, (n + 1) * WIDTH)
+        values = jnp.where(at_rows() == SEQ, bias[:, to], jnp.concatenate(parts, 1))
+        if n == 0:
+            values = jnp.where(at_rows() == SEQ + 1, gain_m[5:6, :], values)
+        rows_out[:, to] = values.astype(BF)
+
+
+def close_kernel(at, rows, normed, spread, gain, qkv, proj, keep, away, gain_out, part):
     core = at[1]
 
     def quarters(first_column):
@@ -233,8 +237,9 @@
 
     grad_norm = sum(dot_t(rows[:, c * WIDTH : (c + 1) * WIDTH], qkv[c]) for c in range(3))
     gain_part = jnp.sum(grad_norm * normed[...], 0, keepdims=True)
-    back = norm_back(grad_norm, normed[...], spread[...], gain[...])
-    part[...] = jnp.where(at_rows() == SEQ, gain_part, back)
+    for k in range(8):
+        gain_out[k : k + 1, :] = gain_part[:, k * 128 : (k + 1) * 128]
+    part[...] = norm_back(grad_norm, normed[...], spread[...], gain[...])
     quarters(HALF)
     part[...] = dot_t(rows[:, 3 * WIDTH :], proj[...])
     quarters(0)
@@ -252,15 +257,16 @@
         sent[:, to] = jnp.where(yhi == 0, high, low).astype(BF)
 
 
-def close_end_kernel(at, mine, came, first, lower, gain_m, bias, input_first, back_second, small):
+def close_end_kernel(at, mine, came, first, lower, input_first, back_second):
     total = mine[...] + came[...].astype(F32)
     input_first[...] = (first[...].astype(F32) - total[0:SEQ, :WIDTH]).astype(BF)
     back_second[...] = (lower[...].astype(F32) + total[0:SEQ, WIDTH:]).astype(BF)
-    row = total[192:200, WIDTH:]
-    small[0:8, :] = bias[...]
-    for k in range(2):
-        small[8 + k : 9 + k, :] = row[5:6, k * 128 : (k + 1) * 128]
-        small[10 + k : 11 + k, :] = gain_m[5:6, k * 128 : (k + 1) * 128]
+
+
+def over_z_each(values):
+    for step in (4, 2, 1):
+        values = values + lax.ppermute(values, "z", [(k, k ^ step) for k in range(8)])
+    return values
 
 
 def turn(left, turned):
@@ -288,13 +294,17 @@
         b[...] = dot(rows_of(turned_out, chosen, blocks), right[:, D:]).astype(BF)
 
 
-def pieces_kernel(at, own_left, came_left, own_right, came_right, *pieces):
+def pieces_kernel(at, own_left, came_left, own_right, came_right, gain_a, *pieces):
+    tail = own_right[192:ROWS, :].astype(F32) + came_right[192:ROWS, :].astype(F32)
+    line = jnp.concatenate([gain_a[k : k + 1, :] for k in range(8)], 1)
+    low = jnp.concatenate([tail[5:6], tail[6:7], line, jnp.zeros((5, D), F32)], 0).astype(BF)
     for to, piece in enumerate(pieces):
-        for first, low, high in ((0, 0, 3 * WIDTH), (512, 3 * WIDTH, D)):
+        for first, start, stop in ((0, 0, 3 * WIDTH), (512, 3 * WIDTH, D)):
             r = slice(first + to * 128, first + (to + 1) * 128)
-            piece[:, low:high] = (
-                dot(own_left[r, :], own_right[:, low:high]) + dot(came_left[r, :], came_right[:, low:high])
+            piece[0:128, start:stop] = (
+                dot(own_left[r, :], own_right[:, start:stop]) + dot(came_left[r, :], came_right[:, start:stop])
             ).astype(BF)
+        piece[128:136, :] = low
 
 
 def added(a, b):
@@ -312,15 +322,24 @@
             away[to, cols] = jnp.where(at[3] == 0, high, low).astype(BF)
 
 
-def merge_kernel(at, keep, came, a, b, c, d, small, total):
+def merge_kernel(at, keep, came, a, b, c, d, total, gain_a):
     total[:, :WIDE] = (keep[...].astype(F32) + came[...].astype(F32)).astype(BF)
     terms = [r[...].astype(F32) for r in (a, b, c, d)]
-    total[:, WIDE : WIDE + D] = (terms[0] + terms[1] + terms[2] + terms[3]).astype(BF)
-    block = jnp.concatenate([small[...], jnp.zeros((4, 128), F32)], 0).astype(BF)
+    x_sum = terms[0] + terms[1] + terms[2] + terms[3]
+    total[:, WIDE : WIDE + D] = x_sum[:128].astype(BF)
+    low = x_sum[128:136]
+    block = jnp.concatenate(
+        [low[0:1, k * 128 : (k + 1) * 128] for k in range(8)]
+        + [low[1:2, k * 128 : (k + 1) * 128] for k in range(2)]
+        + [jnp.zeros((6, 128), F32)],
+        0,
+    ).astype(BF)
     total[:, WIDE + D :] = jnp.concatenate([block] * 8, 0)
-
-
-def end_kernel(at, came, inner, outer, bias, qkv, proj, gain_a, gain_m):
+    for k in range(8):
+        gain_a[k : k + 1, :] = low[2:3, k * 128 : (k + 1) * 128]
+
+
+def end_kernel(at, came, whole, inner, outer, bias, qkv, proj, gain_a, gain_m):
     total = came[0].astype(F32)
     for k in range(1, 8):
         total = total + came[k].astype(F32)
@@ -333,8 +352,9 @@
     for k in range(8):
         bias[:, k * 128 : (k + 1) * 128] = small[k : k + 1, :]
     for k in range(2):
-        gain_a[:, k * 128 : (k + 1) * 128] = small[8 + k : 9 + k, :]
-        gain_m[:, k * 128 : (k + 1) * 128] = small[10 + k : 11 + k, :]
+        to = slice(k * 128, (k + 1) * 128)
+        gain_a[:, to] = sum(jnp.where(at[0] == t, whole[2 * t + k : 2 * t + k + 1, :], 0.0) for t in range(4))
+        gain_m[:, to] = small[8 + k : 9 + k, :]
 
 
 def on_device(
@@ -379,7 +399,7 @@
         lower_b,
         second,
         upper,
-        passed(jnp.stack([gain_mlp, inner_bias])),
+        passed(jnp.stack([gain_mlp, inner_bias]), outer_weight),
         inner_weight,
         outer_weight,
         pause(8 << 30),
@@ -451,11 +471,11 @@
         pause(1 << 20),
     )
     came_left = swap(away_left, "ylo")
-    (rows,) = call(attention_kernel, [(block, BF)], [], 4 * ROWS * D * D, at, given, back, qkv, proj)
+    (rows,) = call(attention_kernel, [(block, BF)], [], 4 * ROWS * D * D, at, given, back, qkv, proj, bias_part, gain_rows)
     came_rows = swap(rows, "ylo")
-    keep, away = call(
+    keep, away, gain_part = call(
         close_kernel,
-        [(block, F32), (block, BF)],
+        [(block, F32), (block, BF), ((8, 128), F32)],
         [pltpu.VMEM(block, F32)],
         2 * ROWS * D * D,
         at,
@@ -468,7 +488,7 @@
     )
     pieces = call(
         pieces_kernel,
-        [((128, D), BF)] * 4,
+        [((136, D), BF)] * 4,
         [],
         2 * D * ROWS * D,
         at,
@@ -476,6 +496,7 @@
         came_left,
         rows,
         came_rows,
+        over_z_each(gain_part),
     )
     came = [around(pieces[to], k) for to, k in enumerate(STEPS[:3])]
     mine, sent = call(
@@ -487,9 +508,9 @@
         keep,
         swap(away, "core"),
     )
-    input_first, back_second, small = call(
+    input_first, back_second = call(
         close_end_kernel,
-        [((SEQ, WIDTH), BF), ((SEQ, WIDTH), BF), ((12, 128), F32)],
+        [((SEQ, WIDTH), BF), ((SEQ, WIDTH), BF)],
         [],
         1 << 22,
         at,
@@ -497,14 +518,10 @@
         swap(sent, "yhi"),
         first,
         lower,
-        gain_rows,
-        bias_part.reshape(8, 128),
-    )
-    small = small + swap(small, "ylo")
-    small = small + sum(around(small, k) for k in (1, 2, 3))
-    (total,) = call(
+    )
+    total, whole = call(
         merge_kernel,
-        [((128, WIDE + D + 128), BF)],
+        [((128, WIDE + D + 128), BF), ((8, 128), F32)],
         [],
         1 << 22,
         at,
@@ -512,8 +529,9 @@
         mlp_came,
         pieces[3],
         *came,
-        small,
-    )
+    )
+    for axis in ("core", "yhi", "ylo"):
+        whole = whole + swap(whole, axis)
     came = lax.all_to_all(total.reshape(8, 16, -1), "z", 0, 0, tiled=True)
     grad_inner, grad_outer, bias_sum, grad_qkv, grad_proj, gain_a_sum, gain_m_sum = call(
         end_kernel,
@@ -530,6 +548,7 @@
         1 << 20,
         at,
         came,
+        whole,
     )
 
     shape_out = (1, SEQ, WIDTH)

time: 136 us -> 124 us (0.912)
  the two profiles are of different devices: /device:TPU:8 before, /device:TPU:20 now
where the time goes in v3:
time: 124 us
  waiting for transfers between devices  57.1 us (46%)
  starting transfers between devices  41.5 us (33%)
  Pallas kernels  20.7 us (17%)
  local copies, waits for them, and re-layouts  3.23 us (3%)
    ppermute x9, waiting for transfers between devices, around(): return lax.ppermute(x, 'x', [(i, (i + step) % 4) for i in range(4)])  29.2 us
    pallas_call x12, Pallas kernels, call(): pl.pallas_call(kernel, out_shape=[jax.ShapeDtypeStruct(s, d) for s, d in...  20.6 us
    ppermute x17, starting transfers between devices, swap(): return lax.ppermute(x, axis, SWAP)  14.6 us
    ppermute x17, waiting for transfers between devices, swap(): return lax.ppermute(x, axis, SWAP)  14.6 us
    ppermute x3, starting transfers between devices, over_z_each(): lax.ppermute(values, 'z', [(k, k ^ step) for k in range(8)])  10.3 us
    ppermute x9, starting transfers between devices, around(): return lax.ppermute(x, 'x', [(i, (i + step) % 4) for i in range(4)])  9.62 us
    all_to_all x1, starting transfers between devices, on_device(): came = lax.all_to_all(total.reshape(8, 16, -1), 'z', 0, 0, tiled=True)  6.92 us
    ppermute x3, waiting for transfers between devices, over_z_each(): lax.ppermute(values, 'z', [(k, k ^ step) for k in range(8)])  6.65 us
  transfers between devices with their start and end apart: 30, of which 19 were waited for; matrix products, arithmetic and copies ran while one was open for 1% of the time, Pallas kernels for 11%

profile of v3, /device:TPU:20, one launch (start us, length us, event | category | flops | bytes accessed | tf_op | source)
XLA Modules:
  0.0 124.1 jit_solution(11840648039105622898)
XLA Ops:
  1.1 3.3 %collective-permute-start.4 = (bf16[197,256]{1,0:T(8,128)(2,1)}, bf16[197,256]{1,0:T(8,128)(2,1)S(1)}, u32[]{:S(2)}, u32[]{:S(2)}) collective-permute-start(bf16[197,256]{1,0:T(8,128)(2,1)} %bitcast.27), channel_id=1, source_target_pairs={{0,2},{2,0},{1,3},{3,1},{4,6},{6,4},{5,7},{7,5},{8,10},{10,8},{9,1... | collective-permute-start | bytes 302600 | tf_op jit(solution)/shard_map/ppermute | solution.py:29
  4.6 3.6 %collective-permute-done.1.f2 = bf16[197,256]{1,0:T(8,128)(2,1)S(1)} collective-permute-done((bf16[197,256]{1,0:T(8,128)(2,1)}, bf16[197,256]{1,0:T(8,128)(2,1)S(1)}, u32[]{:S(2)}, u32[]{:S(2)}) %collective-permute-start.1) | collective-permute-done | bytes 100896 | tf_op jit(solution)/shard_map/ppermute | solution.py:29
  8.2 1.1 collective-permute-done.4.l2
  9.5 1.1 collective-permute-done.5.l3
  10.6 1.6 %copy-done.6 = bf16[1024,1024]{1,0:T(8,128)(2,1)S(1)} copy-done((bf16[1024,1024]{1,0:T(8,128)(2,1)S(1)}, bf16[1024,1024]{1,0:T(8,128)(2,1)}, u32[]{:S(2)}) %copy-start.6) | copy-done | bytes 2097176
  12.2 1.6 %copy-done.7 = bf16[1024,1024]{1,0:T(8,128)(2,1)S(1)} copy-done((bf16[1024,1024]{1,0:T(8,128)(2,1)S(1)}, bf16[1024,1024]{1,0:T(8,128)(2,1)}, u32[]{:S(2)}) %copy-start.7) | copy-done | bytes 2097176
  13.8 3.8 %shard_map.196 = (f32[208,1024]{1,0:T(8,128)S(1)}, bf16[208,1024]{1,0:T(8,128)(2,1)S(1)}, bf16[208,1024]{1,0:T(8,128)(2,1)S(1)}, bf16[208,1024]{1,0:T(8,128)(2,1...) custom-call(s32[4]{0:T(128)S(1)} %pad_add_fusion.at, bf16[197,256]{1,0:T(8,128)(2,1)S(1)} %bitcast.25, ...), custom_call_target="tpu_custom_call" | custom-call | flops 1744830464 | bytes 4194304 | tf_op jit(solution)/shard_map/pallas_call | solution.py:84
  17.8 1.2 shard_map.203
  19.0 1.3 %collective-permute-start.12 = (bf16[256,1024]{1,0:T(8,128)(2,1)S(1)}, bf16[256,1024]{1,0:T(8,128)(2,1)S(1)}, u32[]{:S(2)}, u32[]{:S(2)}) collective-permute-start(bf16[256,1024]{1,0:T(8,128)(2,1)S(1)} %get-tuple-element.82), channel_id=1, source_target_pairs={{0,4},{4,8},{8,12},{12,0},{1,5},{5,9},{9,13},{13,1},{2,6},{6,10},{... | collective-permute-start | bytes 1572872 | tf_op jit(solution)/shard_map/ppermute | solution.py:33
  20.4 2.1 %collective-permute-start.7 = (bf16[208,1024]{1,0:T(8,128)(2,1)S(1)}, bf16[208,1024]{1,0:T(8,128)(2,1)S(1)}, u32[]{:S(2)}, u32[]{:S(2)}) collective-permute-start(bf16[208,1024]{1,0:T(8,128)(2,1)S(1)} %add_convert_fusion.3), channel_id=1, source_target_pairs={{0,2},{2,0},{1,3},{3,1},{4,6},{6,4},{5,7},{7,5},{8,10},{10,8},{9,1... | collective-permute-start | bytes 1277960 | tf_op jit(solution)/shard_map/ppermute | solution.py:29
  23.3 1.5 %shard_map.204 = (bf16[256,1024]{1,0:T(8,128)(2,1)S(1)}, bf16[256,1024]{1,0:T(8,128)(2,1)S(1)}, bf16[256,1024]{1,0:T(8,128)(2,1)S(1)}, bf16[256,1024]{1,0:T(8,12...) custom-call(s32[4]{0:T(128)S(1)} %pad_add_fusion.at, ...), custom_call_target="tpu_custom_call" | custom-call | flops 654311424 | bytes 4194304 | tf_op jit(solution)/shard_map/pallas_call | solution.py:84
  25.5 1.5 %collective-permute-start.14 = (bf16[256,1024]{1,0:T(8,128)(2,1)S(1)}, bf16[256,1024]{1,0:T(8,128)(2,1)S(1)}, u32[]{:S(2)}, u32[]{:S(2)}) collective-permute-start(bf16[256,1024]{1,0:T(8,128)(2,1)S(1)} %get-tuple-element.84), channel_id=1, source_target_pairs={{0,4},{4,8},{8,12},{12,0},{1,5},{5,9},{9,13},{13,1},{2,6},{6,10},{... | collective-permute-start | bytes 1572872 | tf_op jit(solution)/shard_map/ppermute | solution.py:33
  27.0 6.9 %collective-permute-done.12 = bf16[256,1024]{1,0:T(8,128)(2,1)S(1)} collective-permute-done((bf16[256,1024]{1,0:T(8,128)(2,1)S(1)}, bf16[256,1024]{1,0:T(8,128)(2,1)S(1)}, u32[]{:S(2)}, u32[]{:S(2)}) %collective-permute-start.12) | collective-permute-done | bytes 524320 | tf_op jit(solution)/shard_map/ppermute | solution.py:33
  34.1 1.3 %collective-permute-start.13 = (bf16[256,1024]{1,0:T(8,128)(2,1)S(1)}, bf16[256,1024]{1,0:T(8,128)(2,1)S(1)}, u32[]{:S(2)}, u32[]{:S(2)}) collective-permute-start(bf16[256,1024]{1,0:T(8,128)(2,1)S(1)} %add_convert_fusion.1), channel_id=1, source_target_pairs={{0,4},{4,8},{8,12},{12,0},{1,5},{5,9},{9,13},{13,1},{2,6},{6,10},{... | collective-permute-start | bytes 1572872 | tf_op jit(solution)/shard_map/ppermute | solution.py:33
  35.7 1.7 %collective-permute-done.15 = bf16[256,1024]{1,0:T(8,128)(2,1)S(1)} collective-permute-done((bf16[256,1024]{1,0:T(8,128)(2,1)S(1)}, bf16[256,1024]{1,0:T(8,128)(2,1)S(1)}, u32[]{:S(2)}, u32[]{:S(2)}) %collective-permute-start.15) | collective-permute-done | bytes 524320 | tf_op jit(solution)/shard_map/ppermute | solution.py:33
  37.5 0.9 collective-permute-start.16
  38.4 2.0 %shard_map.198 = (bf16[208,1024]{1,0:T(8,128)(2,1)S(1)}, bf16[208,1024]{1,0:T(8,128)(2,1)S(1)}, f32[208,1024]{1,0:T(8,128)S(1)}, f32[208,1]{1,0:T(8,128)S(1)}, b...) custom-call(s32[4]{0:T(128)S(1)} %pad_add_fusion.at, ...), custom_call_target="tpu_custom_call" | custom-call | flops 218103808 | bytes 4194304 | tf_op jit(solution)/shard_map/pallas_call | solution.py:84
  40.4 3.3 %shard_map.199.rows.own_right = bf16[208,1024]{1,0:T(8,128)(2,1)S(1)} custom-call(s32[4]{0:T(128)S(1)} %pad_add_fusion.at, bf16[208,1024]{1,0:T(8,128)(2,1)S(1)} %get-tuple-element.60.given, bf16[208,1024]{1,0:T(8,128)(2,1)S(1)} %get-tuple-element.61.back, bf16[3,1024,256]{2,1,0:T(8,128)(2,1)S(1)} %bitcast.21, bf16[1024,256]{1,0:T(8,128)(2,1)S(1)} %copy-done.1, ...), custom_call_target="tpu_custom_call" | custom-call | flops 872415232 | bytes 4194304 | tf_op jit(solution)/shard_map/pallas_call | solution.py:84
  43.7 1.4 %collective-permute-start.19 = (bf16[208,1024]{1,0:T(8,128)(2,1)S(1)}, bf16[208,1024]{1,0:T(8,128)(2,1)S(1)}, u32[]{:S(2)}, u32[]{:S(2)}) collective-permute-start(bf16[208,1024]{1,0:T(8,128)(2,1)S(1)} %shard_map.199.rows.own_right), channel_id=1, source_target_pairs={{0,16},{16,0},{1,17},{17,1},{2,18},{18,2},{3,19},{19,3},{4,20},{20... | collective-permute-start | bytes 1277960 | tf_op jit(solution)/shard_map/ppermute | solution.py:29
  45.1 3.5 %collective-permute-done.11.a1 = bf16[256,1024]{1,0:T(8,128)(2,1)S(1)} collective-permute-done((bf16[256,1024]{1,0:T(8,128)(2,1)S(1)}, bf16[256,1024]{1,0:T(8,128)(2,1)S(1)}, u32[]{:S(2)}, u32[]{:S(2)}) %collective-permute-start.11) | collective-permute-done | bytes 524320 | tf_op jit(solution)/shard_map/ppermute | solution.py:33
  48.6 1.3 %collective-permute-start.18 = (bf16[1024,208]{1,0:T(8,128)(2,1)S(1)}, bf16[1024,208]{1,0:T(8,128)(2,1)S(1)}, u32[]{:S(2)}, u32[]{:S(2)}) collective-permute-start(bf16[1024,208]{1,0:T(8,128)(2,1)S(1)} %get-tuple-element.90), channel_id=1, source_target_pairs={{0,16},{16,0},{1,17},{17,1},{2,18},{18,2},{3,19},{19,3},{4,20},{20... | collective-permute-start | bytes 1277960 | tf_op jit(solution)/shard_map/ppermute | solution.py:29
  49.8 5.9 %collective-permute-done.13.a2 = bf16[256,1024]{1,0:T(8,128)(2,1)S(1)} collective-permute-done((bf16[256,1024]{1,0:T(8,128)(2,1)S(1)}, bf16[256,1024]{1,0:T(8,128)(2,1)S(1)}, u32[]{:S(2)}, u32[]{:S(2)}) %collective-permute-start.13) | collective-permute-done | bytes 524320 | tf_op jit(solution)/shard_map/ppermute | solution.py:33
  55.8 2.9 %collective-permute-done.16.b2 = bf16[256,1024]{1,0:T(8,128)(2,1)S(1)} collective-permute-done((bf16[256,1024]{1,0:T(8,128)(2,1)S(1)}, bf16[256,1024]{1,0:T(8,128)(2,1)S(1)}, u32[]{:S(2)}, u32[]{:S(2)}) %collective-permute-start.16) | collective-permute-done | bytes 524320 | tf_op jit(solution)/shard_map/ppermute | solution.py:33
  58.6 1.0 shard_map.205
  59.6 1.4 %collective-permute-start.17 = (bf16[128,2048]{1,0:T(8,128)(2,1)S(1)}, bf16[128,2048]{1,0:T(8,128)(2,1)S(1)}, u32[]{:S(2)}, u32[]{:S(2)}) collective-permute-start(bf16[128,2048]{1,0:T(8,128)(2,1)S(1)} %get-tuple-element.88), channel_id=1, source_target_pairs={{0,16},{16,0},{1,17},{17,1},{2,18},{18,2},{3,19},{19,3},{4,20},{20... | collective-permute-start | bytes 1572872 | tf_op jit(solution)/shard_map/ppermute | solution.py:29
  61.0 1.7 %shard_map.200 = (f32[208,1024]{1,0:T(8,128)S(1)}, bf16[208,1024]{1,0:T(8,128)(2,1)S(1)}, f32[8,128]{1,0:T(8,128)S(1)}) custom-call(s32[4]{0:T(128)S(1)} %pad_add_fusion.at, bf16[208,1024]{1,0:T(8,128)(2,1)S(1)} %shard_map.199.rows.own_right, f32[208,1024]{1,0:T(8,128)S(1)} %get-tuple-element.64.normed, f32[208,1]{1,0:T(8,128)S(1)} %get-tuple-element.65.spread, ...), custom_call_target="tpu_custom_call" | custom-call | flops 436207616 | bytes 4194304 | tf_op jit(solution)/shard_map/pallas_call | solution.py:84
  62.7 7.3 %collective-permute-start.20 = (f32[8,128]{1,0:T(8,128)S(1)}, f32[8,128]{1,0:T(8,128)S(1)}, u32[]{:S(2)}, u32[]{:S(2)}) collective-permute-start(f32[8,128]{1,0:T(8,128)S(1)} %get-tuple-element.91), channel_id=1, source_target_pairs={{0,128},{32,160},{64,192},{96,224},{128,0},{160,32},{192,64},{224,... | collective-permute-start | bytes 12296 | tf_op jit(solution)/shard_map/ppermute | solution.py:268
  69.9 1.6 %collective-permute-done.20 = f32[8,128]{1,0:T(8,128)S(1)} collective-permute-done((f32[8,128]{1,0:T(8,128)S(1)}, f32[8,128]{1,0:T(8,128)S(1)}, u32[]{:S(2)}, u32[]{:S(2)}) %collective-permute-start.20) | collective-permute-done | bytes 4128 | tf_op jit(solution)/shard_map/ppermute | solution.py:268
  71.5 2.0 %collective-permute-start.21 = (f32[8,128]{1,0:T(8,128)S(1)}, f32[8,128]{1,0:T(8,128)S(1)}, u32[]{:S(2)}, u32[]{:S(2)}) collective-permute-start(f32[8,128]{1,0:T(8,128)S(1)} %add.38), channel_id=1, source_target_pairs={{0,64},{32,96},{64,0},{96,32},{128,192},{160,224},{192,128},{224,1... | collective-permute-start | bytes 12296 | tf_op jit(solution)/shard_map/ppermute | solution.py:268
  73.5 2.5 %collective-permute-done.21 = f32[8,128]{1,0:T(8,128)S(1)} collective-permute-done((f32[8,128]{1,0:T(8,128)S(1)}, f32[8,128]{1,0:T(8,128)S(1)}, u32[]{:S(2)}, u32[]{:S(2)}) %collective-permute-start.21) | collective-permute-done | bytes 4128 | tf_op jit(solution)/shard_map/ppermute | solution.py:268
  76.0 1.0 collective-permute-start.22
  77.1 2.6 %collective-permute-done.22 = f32[8,128]{1,0:T(8,128)S(1)} collective-permute-done((f32[8,128]{1,0:T(8,128)S(1)}, f32[8,128]{1,0:T(8,128)S(1)}, u32[]{:S(2)}, u32[]{:S(2)}) %collective-permute-start.22) | collective-permute-done | bytes 4128 | tf_op jit(solution)/shard_map/ppermute | solution.py:268
  79.6 1.3 %shard_map.206 = (bf16[136,1024]{1,0:T(8,128)(2,1)S(1)}, bf16[136,1024]{1,0:T(8,128)(2,1)S(1)}, bf16[136,1024]{1,0:T(8,128)(2,1)S(1)}, bf16[136,1024]{1,0:T(8,128)(2,1)S(1)}) custom-call(s32[4]{0:T(128)S(1)} %pad_add_fusion.at, bf16[1024,208]{1,0:T(8,128)(2,1)S(1)} %get-tuple-element.89.own_left, bf16[1024,208]{1,0:T(8,128)(2,1)S(1)} %collective-permute-done.18.came_left, ...), custom_call_target="tpu_custom_call" | custom-call | flops 436207616 | bytes 4194304 | tf_op jit(solution)/shard_map/pallas_call | solution.py:84
  81.0 0.9 collective-permute-start.23
  81.8 2.1 %collective-permute-start.24 = (bf16[136,1024]{1,0:T(8,128)(2,1)S(1)}, bf16[136,1024]{1,0:T(8,128)(2,1)S(1)}, u32[]{:S(2)}, u32[]{:S(2)}) collective-permute-start(bf16[136,1024]{1,0:T(8,128)(2,1)S(1)} %get-tuple-element.94), channel_id=1, source_target_pairs={{0,4},{4,8},{8,12},{12,0},{1,5},{5,9},{9,13},{13,1},{2,6},{6,10},{... | collective-permute-start | bytes 835592 | tf_op jit(solution)/shard_map/ppermute | solution.py:33
  84.2 5.8 %collective-permute-done.23.b = bf16[136,1024]{1,0:T(8,128)(2,1)S(1)} collective-permute-done((bf16[136,1024]{1,0:T(8,128)(2,1)S(1)}, bf16[136,1024]{1,0:T(8,128)(2,1)S(1)}, u32[]{:S(2)}, u32[]{:S(2)}) %collective-permute-start.23) | collective-permute-done | bytes 278560 | tf_op jit(solution)/shard_map/ppermute | solution.py:33
  90.0 2.5 %collective-permute-done.24.c = bf16[136,1024]{1,0:T(8,128)(2,1)S(1)} collective-permute-done((bf16[136,1024]{1,0:T(8,128)(2,1)S(1)}, bf16[136,1024]{1,0:T(8,128)(2,1)S(1)}, u32[]{:S(2)}, u32[]{:S(2)}) %collective-permute-start.24) | collective-permute-done | bytes 278560 | tf_op jit(solution)/shard_map/ppermute | solution.py:33
  92.5 1.7 %shard_map.207 = (bf16[128,3200]{1,0:T(8,128)(2,1)}, f32[8,128]{1,0:T(8,128)S(1)}) custom-call(s32[4]{0:T(128)S(1)} %pad_add_fusion.at, bf16[128,2048]{1,0:T(8,128)(2,1)S(1)} %get-tuple-element.87.keep, bf16[128,2048]{1,0:T(8,128)(2,1)S(1)} %collective-permute-done.17.came, bf16[136,1024]{1,0:T(8,128)(2,1)S(1)} %get-tuple-element.92.a, ...), custom_call_target="tpu_custom_call" | custom-call | flops 4194304 | bytes 4194304 | tf_op jit(solution)/shard_map/pallas_call | solution.py:84
  94.2 6.9 %all-to-all-start = ((bf16[8,16,3200]{2,1,0:T(8,128)(2,1)}), bf16[8,16,3200]{2,1,0:T(8,128)(2,1)S(1)}, u32[]{:S(2)}, u32[]{:S(2)}) async-start(bf16[8,16,3200]{2,1,0:T(8,128)(2,1)} %bitcast.16), calls=%async_computation | async-start | bytes 1638400 | tf_op jit(solution)/shard_map/all_to_all | solution.py:535
  101.2 1.8 %collective-permute-done.9.came = bf16[208,1024]{1,0:T(8,128)(2,1)S(1)} collective-permute-done((bf16[208,1024]{1,0:T(8,128)(2,1)S(1)}, bf16[208,1024]{1,0:T(8,128)(2,1)S(1)}, u32[]{:S(2)}, u32[]{:S(2)}) %collective-permute-start.9) | collective-permute-done | bytes 426016 | tf_op jit(solution)/shard_map/ppermute | solution.py:29
  103.6 1.0 collective-permute-start.10
  104.6 1.2 collective-permute-done.26
  105.8 2.6 %collective-permute-start.27 = (f32[8,128]{1,0:T(8,128)S(1)}, f32[8,128]{1,0:T(8,128)S(1)}, u32[]{:S(2)}, u32[]{:S(2)}) collective-permute-start(f32[8,128]{1,0:T(8,128)S(1)} %add.41), channel_id=1, source_target_pairs={{0,2},{2,0},{1,3},{3,1},{4,6},{6,4},{5,7},{7,5},{8,10},{10,8},{9,1... | collective-permute-start | bytes 12296 | tf_op jit(solution)/shard_map/ppermute | solution.py:29
  108.4 4.2 %collective-permute-done.27 = f32[8,128]{1,0:T(8,128)S(1)} collective-permute-done((f32[8,128]{1,0:T(8,128)S(1)}, f32[8,128]{1,0:T(8,128)S(1)}, u32[]{:S(2)}, u32[]{:S(2)}) %collective-permute-start.27) | collective-permute-done | bytes 4128 | tf_op jit(solution)/shard_map/ppermute | solution.py:29
  113.3 1.3 %shard_map.202 = (bf16[197,256]{1,0:T(8,128)(2,1)}, bf16[197,256]{1,0:T(8,128)(2,1)}) custom-call(s32[4]{0:T(128)S(1)} %pad_add_fusion.at, f32[208,512]{1,0:T(8,128)S(1)} %get-tuple-element.68.mine, bf16[208,512]{1,0:T(8,128)(2,1)S(1)} %collective-permute-done.10.came, bf16[197,256]{1,0:T(8,128)(2,1)S(1)} %bitcast.26, bf16[197,256]{1,0:T(8,128)(2,1)S(1)} %bitcast.30), custom_call_target="tpu_custom_call" | custom-call | flops 4194304 | bytes 4194304 | tf_op jit(solution)/shard_map/pallas_call | solution.py:84
  114.6 1.6 %collective-permute-done.28 = f32[8,128]{1,0:T(8,128)S(1)} collective-permute-done((f32[8,128]{1,0:T(8,128)S(1)}, f32[8,128]{1,0:T(8,128)S(1)}, u32[]{:S(2)}, u32[]{:S(2)}) %collective-permute-start.28) | collective-permute-done | bytes 4128 | tf_op jit(solution)/shard_map/ppermute | solution.py:29
  116.2 6.7 %all-to-all-done.came = bf16[8,16,3200]{2,1,0:T(8,128)(2,1)S(1)} async-done(((bf16[8,16,3200]{2,1,0:T(8,128)(2,1)}), bf16[8,16,3200]{2,1,0:T(8,128)(2,1)S(1)}, u32[]{:S(2)}, u32[]{:S(2)}) %all-to-all-start) | async-done | bytes 819232 | tf_op jit(solution)/shard_map/all_to_all | solution.py:535
  122.8 1.3 %shard_map.208 = (f32[16,1024]{1,0:T(8,128)}, f32[16,1024]{1,0:T(8,128)}, f32[1,1024]{1,0:T(1,128)}, f32[3,16,256]{2,1,0:T(8,128)}, f32[16,256]{1,0:T(8,128)}, /*index=5*/f32[1,256]{1,0:T(1,128)}, f32[1,256]{1,0:T(1,128)}) custom-call(s32[4]{0:T(128)S(1)} %pad_add_fusion.at, bf16[8,16,3200]{2,1,0:T(8,128)(2,1)S(1)} %all-to-all-done.came, f32[8,128]{1,0:T(8,128)S(1)} %add.43.whole), custom_call_target="tpu_custom_call" | custom-call | flops 1048576 | bytes 4194304 | tf_op jit(solution)/shard_map/pallas_call | solution.py:84
  (63 shorter events, 4.9 us)
Async XLA Ops:
  0.6 7.5 %collective-permute-start.1 = (bf16[197,256]{1,0:T(8,128)(2,1)}, bf16[197,256]{1,0:T(8,128)(2,1)S(1)}, u32[]{:S(2)}, u32[]{:S(2)}) collective-permute-start(bf16[197,256]{1,0:T(8,128)(2,1)} %bitcast.23), channel_id=1, source_target_pairs={{0,2},{2,0},{1,3},{3,1},{4,6},{6,4},{5,7},{7,5},{8,10},{10,8},{9,1... | collective-permute-start | bytes 302600 | tf_op jit(solution)/shard_map/ppermute | solution.py:29
  1.1 8.3 %collective-permute-start = (bf16[197,256]{1,0:T(8,128)(2,1)}, bf16[197,256]{1,0:T(8,128)(2,1)S(1)}, u32[]{:S(2)}, u32[]{:S(2)}) collective-permute-start(bf16[197,256]{1,0:T(8,128)(2,1)} %bitcast.24), channel_id=1, source_target_pairs={{0,1},{1,0},{2,3},{3,2},{4,5},{5,4},{6,7},{7,6},{8,9},{9,8},{10,11... | collective-permute-start | bytes 302600 | tf_op jit(solution)/shard_map/ppermute | solution.py:29
  1.1 3.4 %copy-start.10 = (f32[1024]{0:T(1024)S(1)}, f32[1024]{0:T(1024)}, u32[]{:S(2)}) copy-start(f32[1024]{0:T(1024)} %param.20) | copy-start | bytes 12292
  1.1 3.4 %copy-start.11 = (f32[1024]{0:T(1024)S(1)}, f32[1024]{0:T(1024)}, u32[]{:S(2)}) copy-start(f32[1024]{0:T(1024)} %param.16) | copy-start | bytes 12292
  1.1 3.4 %copy-start.5 = (bf16[1024,1024]{1,0:T(8,128)(2,1)S(1)}, bf16[1024,1024]{1,0:T(8,128)(2,1)}, u32[]{:S(2)}) copy-start(bf16[1024,1024]{1,0:T(8,128)(2,1)} %outer.1) | copy-start | bytes 6291460
  1.1 8.2 %collective-permute-start.4 = (bf16[197,256]{1,0:T(8,128)(2,1)}, bf16[197,256]{1,0:T(8,128)(2,1)S(1)}, u32[]{:S(2)}, u32[]{:S(2)}) collective-permute-start(bf16[197,256]{1,0:T(8,128)(2,1)} %bitcast.27), channel_id=1, source_target_pairs={{0,2},{2,0},{1,3},{3,1},{4,6},{6,4},{5,7},{7,5},{8,10},{10,8},{9,1... | collective-permute-start | bytes 302600 | tf_op jit(solution)/shard_map/ppermute | solution.py:29
  4.4 5.0 %collective-permute-start.3 = (bf16[197,256]{1,0:T(8,128)(2,1)}, bf16[197,256]{1,0:T(8,128)(2,1)S(1)}, u32[]{:S(2)}, u32[]{:S(2)}) collective-permute-start(bf16[197,256]{1,0:T(8,128)(2,1)} %bitcast.28), channel_id=1, source_target_pairs={{0,1},{1,0},{2,3},{3,2},{4,5},{5,4},{6,7},{7,6},{8,9},{9,8},{10,11... | collective-permute-start | bytes 302600 | tf_op jit(solution)/shard_map/ppermute | solution.py:29
  4.5 6.0 %copy-start.2 = (bf16[1,197,256]{2,1,0:T(8,128)(2,1)S(1)}, bf16[1,197,256]{2,1,0:T(8,128)(2,1)}, u32[]{:S(2)}) copy-start(bf16[1,197,256]{2,1,0:T(8,128)(2,1)} %param.11) | copy-start | bytes 302596
  4.5 6.0 %copy-start.3 = (bf16[1,197,256]{2,1,0:T(8,128)(2,1)S(1)}, bf16[1,197,256]{2,1,0:T(8,128)(2,1)}, u32[]{:S(2)}) copy-start(bf16[1,197,256]{2,1,0:T(8,128)(2,1)} %param.14) | copy-start | bytes 302596
  4.6 6.0 %copy-start.8 = (bf16[1,197,256]{2,1,0:T(8,128)(2,1)S(1)}, bf16[1,197,256]{2,1,0:T(8,128)(2,1)}, u32[]{:S(2)}) copy-start(bf16[1,197,256]{2,1,0:T(8,128)(2,1)} %param.12) | copy-start | bytes 302596
  4.6 6.0 %copy-start.9 = (bf16[1,197,256]{2,1,0:T(8,128)(2,1)S(1)}, bf16[1,197,256]{2,1,0:T(8,128)(2,1)}, u32[]{:S(2)}) copy-start(bf16[1,197,256]{2,1,0:T(8,128)(2,1)} %param.13) | copy-start | bytes 302596
  8.2 1.3 %collective-permute-start.2 = (bf16[197,256]{1,0:T(8,128)(2,1)S(1)}, bf16[197,256]{1,0:T(8,128)(2,1)S(1)}, u32[]{:S(2)}, u32[]{:S(2)}) collective-permute-start(bf16[197,256]{1,0:T(8,128)(2,1)S(1)} %collective-permute-done.1.f2), channel_id=1, source_target_pairs={{0,1},{1,0},{2,3},{3,2},{4,5},{5,4},{6,7},{7,6},{8,9},{9,8},{10,11... | collective-permute-start | bytes 302600 | tf_op jit(solution)/shard_map/ppermute | solution.py:29
  9.3 1.3 %collective-permute-start.5 = (bf16[197,256]{1,0:T(8,128)(2,1)S(1)}, bf16[197,256]{1,0:T(8,128)(2,1)S(1)}, u32[]{:S(2)}, u32[]{:S(2)}) collective-permute-start(bf16[197,256]{1,0:T(8,128)(2,1)S(1)} %collective-permute-done.4.l2), channel_id=1, source_target_pairs={{0,1},{1,0},{2,3},{3,2},{4,5},{5,4},{6,7},{7,6},{8,9},{9,8},{10,11... | collective-permute-start | bytes 302600 | tf_op jit(solution)/shard_map/ppermute | solution.py:29
  10.6 1.6 %copy-start.6 = (bf16[1024,1024]{1,0:T(8,128)(2,1)S(1)}, bf16[1024,1024]{1,0:T(8,128)(2,1)}, u32[]{:S(2)}) copy-start(bf16[1024,1024]{1,0:T(8,128)(2,1)} %outer.1) | copy-start | bytes 6291460
  12.2 1.6 %copy-start.7 = (bf16[1024,1024]{1,0:T(8,128)(2,1)S(1)}, bf16[1024,1024]{1,0:T(8,128)(2,1)}, u32[]{:S(2)}) copy-start(bf16[1024,1024]{1,0:T(8,128)(2,1)} %inner.1) | copy-start | bytes 6291460
  17.6 2.7 %collective-permute-start.6 = (bf16[208,1024]{1,0:T(8,128)(2,1)S(1)}, bf16[208,1024]{1,0:T(8,128)(2,1)S(1)}, u32[]{:S(2)}, u32[]{:S(2)}) collective-permute-start(bf16[208,1024]{1,0:T(8,128)(2,1)S(1)} %get-tuple-element.59), channel_id=1, source_target_pairs={{0,1},{1,0},{2,3},{3,2},{4,5},{5,4},{6,7},{7,6},{8,9},{9,8},{10,11... | collective-permute-start | bytes 1277960 | tf_op jit(solution)/shard_map/ppermute | solution.py:29
  19.0 14.9 %collective-permute-start.12 = (bf16[256,1024]{1,0:T(8,128)(2,1)S(1)}, bf16[256,1024]{1,0:T(8,128)(2,1)S(1)}, u32[]{:S(2)}, u32[]{:S(2)}) collective-permute-start(bf16[256,1024]{1,0:T(8,128)(2,1)S(1)} %get-tuple-element.82), channel_id=1, source_target_pairs={{0,4},{4,8},{8,12},{12,0},{1,5},{5,9},{9,13},{13,1},{2,6},{6,10},{... | collective-permute-start | bytes 1572872 | tf_op jit(solution)/shard_map/ppermute | solution.py:33
  20.4 15.0 %collective-permute-start.7 = (bf16[208,1024]{1,0:T(8,128)(2,1)S(1)}, bf16[208,1024]{1,0:T(8,128)(2,1)S(1)}, u32[]{:S(2)}, u32[]{:S(2)}) collective-permute-start(bf16[208,1024]{1,0:T(8,128)(2,1)S(1)} %add_convert_fusion.3), channel_id=1, source_target_pairs={{0,2},{2,0},{1,3},{3,1},{4,6},{6,4},{5,7},{7,5},{8,10},{10,8},{9,1... | collective-permute-start | bytes 1277960 | tf_op jit(solution)/shard_map/ppermute | solution.py:29
  22.5 14.8 %collective-permute-start.15 = (bf16[256,1024]{1,0:T(8,128)(2,1)S(1)}, bf16[256,1024]{1,0:T(8,128)(2,1)S(1)}, u32[]{:S(2)}, u32[]{:S(2)}) collective-permute-start(bf16[256,1024]{1,0:T(8,128)(2,1)S(1)} %get-tuple-element.86), channel_id=1, source_target_pairs={{0,12},{4,0},{8,4},{12,8},{1,13},{5,1},{9,5},{13,9},{2,14},{6,2},{... | collective-permute-start | bytes 1572872 | tf_op jit(solution)/shard_map/ppermute | solution.py:33
  24.9 23.7 %collective-permute-start.11 = (bf16[256,1024]{1,0:T(8,128)(2,1)S(1)}, bf16[256,1024]{1,0:T(8,128)(2,1)S(1)}, u32[]{:S(2)}, u32[]{:S(2)}) collective-permute-start(bf16[256,1024]{1,0:T(8,128)(2,1)S(1)} %get-tuple-element.80), channel_id=1, source_target_pairs={{0,12},{4,0},{8,4},{12,8},{1,13},{5,1},{9,5},{13,9},{2,14},{6,2},{... | collective-permute-start | bytes 1572872 | tf_op jit(solution)/shard_map/ppermute | solution.py:33
  25.5 24.3 %collective-permute-start.14 = (bf16[256,1024]{1,0:T(8,128)(2,1)S(1)}, bf16[256,1024]{1,0:T(8,128)(2,1)S(1)}, u32[]{:S(2)}, u32[]{:S(2)}) collective-permute-start(bf16[256,1024]{1,0:T(8,128)(2,1)S(1)} %get-tuple-element.84), channel_id=1, source_target_pairs={{0,4},{4,8},{8,12},{12,0},{1,5},{5,9},{9,13},{13,1},{2,6},{6,10},{... | collective-permute-start | bytes 1572872 | tf_op jit(solution)/shard_map/ppermute | solution.py:33
  33.9 4.5 %copy-start.4 = (f32[1024]{0:T(1024)S(1)}, f32[1024]{0:T(1024)}, u32[]{:S(2)}) copy-start(f32[1024]{0:T(1024)} %param.15) | copy-start | bytes 12292
  34.1 6.3 %copy-start = (bf16[1024,3,256]{2,0,1:T(8,128)(2,1)S(1)}, bf16[1024,3,256]{2,0,1:T(8,128)(2,1)}, u32[]{:S(2)}) copy-start(bf16[1024,3,256]{2,0,1:T(8,128)(2,1)} %param.17) | copy-start | bytes 4718596
  34.1 6.3 %copy-start.1 = (bf16[1024,256]{1,0:T(8,128)(2,1)S(1)}, bf16[1024,256]{1,0:T(8,128)(2,1)}, u32[]{:S(2)}) copy-start(bf16[1024,256]{1,0:T(8,128)(2,1)} %proj.3) | copy-start | bytes 1572868
  34.1 21.7 %collective-permute-start.13 = (bf16[256,1024]{1,0:T(8,128)(2,1)S(1)}, bf16[256,1024]{1,0:T(8,128)(2,1)S(1)}, u32[]{:S(2)}, u32[]{:S(2)}) collective-permute-start(bf16[256,1024]{1,0:T(8,128)(2,1)S(1)} %add_convert_fusion.1), channel_id=1, source_target_pairs={{0,4},{4,8},{8,12},{12,0},{1,5},{5,9},{9,13},{13,1},{2,6},{6,10},{... | collective-permute-start | bytes 1572872 | tf_op jit(solution)/shard_map/ppermute | solution.py:33
  35.6 2.9 %collective-permute-start.8 = (bf16[208,1024]{1,0:T(8,128)(2,1)S(1)}, bf16[208,1024]{1,0:T(8,128)(2,1)S(1)}, u32[]{:S(2)}, u32[]{:S(2)}) collective-permute-start(bf16[208,1024]{1,0:T(8,128)(2,1)S(1)} %add_convert_fusion.2.done), channel_id=1, source_target_pairs={{0,1},{1,0},{2,3},{3,2},{4,5},{5,4},{6,7},{7,6},{8,9},{9,8},{10,11... | collective-permute-start | bytes 1277960 | tf_op jit(solution)/shard_map/ppermute | solution.py:29
  37.5 21.1 %collective-permute-start.16 = (bf16[256,1024]{1,0:T(8,128)(2,1)S(1)}, bf16[256,1024]{1,0:T(8,128)(2,1)S(1)}, u32[]{:S(2)}, u32[]{:S(2)}) collective-permute-start(bf16[256,1024]{1,0:T(8,128)(2,1)S(1)} %add_convert_fusion), channel_id=1, source_target_pairs={{0,12},{4,0},{8,4},{12,8},{1,13},{5,1},{9,5},{13,9},{2,14},{6,2},{... | collective-permute-start | bytes 1572872 | tf_op jit(solution)/shard_map/ppermute | solution.py:33
  43.7 36.0 %collective-permute-start.19 = (bf16[208,1024]{1,0:T(8,128)(2,1)S(1)}, bf16[208,1024]{1,0:T(8,128)(2,1)S(1)}, u32[]{:S(2)}, u32[]{:S(2)}) collective-permute-start(bf16[208,1024]{1,0:T(8,128)(2,1)S(1)} %shard_map.199.rows.own_right), channel_id=1, source_target_pairs={{0,16},{16,0},{1,17},{17,1},{2,18},{18,2},{3,19},{19,3},{4,20},{20... | collective-permute-start | bytes 1277960 | tf_op jit(solution)/shard_map/ppermute | solution.py:29
  48.6 31.1 %collective-permute-start.18 = (bf16[1024,208]{1,0:T(8,128)(2,1)S(1)}, bf16[1024,208]{1,0:T(8,128)(2,1)S(1)}, u32[]{:S(2)}, u32[]{:S(2)}) collective-permute-start(bf16[1024,208]{1,0:T(8,128)(2,1)S(1)} %get-tuple-element.90), channel_id=1, source_target_pairs={{0,16},{16,0},{1,17},{17,1},{2,18},{18,2},{3,19},{19,3},{4,20},{20... | collective-permute-start | bytes 1277960 | tf_op jit(solution)/shard_map/ppermute | solution.py:29
  59.6 24.6 %collective-permute-start.17 = (bf16[128,2048]{1,0:T(8,128)(2,1)S(1)}, bf16[128,2048]{1,0:T(8,128)(2,1)S(1)}, u32[]{:S(2)}, u32[]{:S(2)}) collective-permute-start(bf16[128,2048]{1,0:T(8,128)(2,1)S(1)} %get-tuple-element.88), channel_id=1, source_target_pairs={{0,16},{16,0},{1,17},{17,1},{2,18},{18,2},{3,19},{19,3},{4,20},{20... | collective-permute-start | bytes 1572872 | tf_op jit(solution)/shard_map/ppermute | solution.py:29
  62.7 8.9 %collective-permute-start.20 = (f32[8,128]{1,0:T(8,128)S(1)}, f32[8,128]{1,0:T(8,128)S(1)}, u32[]{:S(2)}, u32[]{:S(2)}) collective-permute-start(f32[8,128]{1,0:T(8,128)S(1)} %get-tuple-element.91), channel_id=1, source_target_pairs={{0,128},{32,160},{64,192},{96,224},{128,0},{160,32},{192,64},{224,... | collective-permute-start | bytes 12296 | tf_op jit(solution)/shard_map/ppermute | solution.py:268
  71.5 4.5 %collective-permute-start.21 = (f32[8,128]{1,0:T(8,128)S(1)}, f32[8,128]{1,0:T(8,128)S(1)}, u32[]{:S(2)}, u32[]{:S(2)}) collective-permute-start(f32[8,128]{1,0:T(8,128)S(1)} %add.38), channel_id=1, source_target_pairs={{0,64},{32,96},{64,0},{96,32},{128,192},{160,224},{192,128},{224,1... | collective-permute-start | bytes 12296 | tf_op jit(solution)/shard_map/ppermute | solution.py:268
  76.0 3.6 %collective-permute-start.22 = (f32[8,128]{1,0:T(8,128)S(1)}, f32[8,128]{1,0:T(8,128)S(1)}, u32[]{:S(2)}, u32[]{:S(2)}) collective-permute-start(f32[8,128]{1,0:T(8,128)S(1)} %add.39), channel_id=1, source_target_pairs={{0,32},{32,0},{64,96},{96,64},{128,160},{160,128},{192,224},{224,1... | collective-permute-start | bytes 12296 | tf_op jit(solution)/shard_map/ppermute | solution.py:268
  81.0 9.1 %collective-permute-start.23 = (bf16[136,1024]{1,0:T(8,128)(2,1)S(1)}, bf16[136,1024]{1,0:T(8,128)(2,1)S(1)}, u32[]{:S(2)}, u32[]{:S(2)}) collective-permute-start(bf16[136,1024]{1,0:T(8,128)(2,1)S(1)} %get-tuple-element.93), channel_id=1, source_target_pairs={{0,8},{4,12},{8,0},{12,4},{1,9},{5,13},{9,1},{13,5},{2,10},{6,14},... | collective-permute-start | bytes 835592 | tf_op jit(solution)/shard_map/ppermute | solution.py:33
  81.8 10.7 %collective-permute-start.24 = (bf16[136,1024]{1,0:T(8,128)(2,1)S(1)}, bf16[136,1024]{1,0:T(8,128)(2,1)S(1)}, u32[]{:S(2)}, u32[]{:S(2)}) collective-permute-start(bf16[136,1024]{1,0:T(8,128)(2,1)S(1)} %get-tuple-element.94), channel_id=1, source_target_pairs={{0,4},{4,8},{8,12},{12,0},{1,5},{5,9},{9,13},{13,1},{2,6},{6,10},{... | collective-permute-start | bytes 835592 | tf_op jit(solution)/shard_map/ppermute | solution.py:33
  83.9 8.6 %collective-permute-start.25 = (bf16[136,1024]{1,0:T(8,128)(2,1)S(1)}, bf16[136,1024]{1,0:T(8,128)(2,1)S(1)}, u32[]{:S(2)}, u32[]{:S(2)}) collective-permute-start(bf16[136,1024]{1,0:T(8,128)(2,1)S(1)} %get-tuple-element.95), channel_id=1, source_target_pairs={{0,12},{4,0},{8,4},{12,8},{1,13},{5,1},{9,5},{13,9},{2,14},{6,2},{... | collective-permute-start | bytes 835592 | tf_op jit(solution)/shard_map/ppermute | solution.py:33
  94.2 28.6 %all-to-all-start = ((bf16[8,16,3200]{2,1,0:T(8,128)(2,1)}), bf16[8,16,3200]{2,1,0:T(8,128)(2,1)S(1)}, u32[]{:S(2)}, u32[]{:S(2)}) async-start(bf16[8,16,3200]{2,1,0:T(8,128)(2,1)} %bitcast.16), calls=%async_computation | async-start | bytes 1638400 | tf_op jit(solution)/shard_map/all_to_all | solution.py:535
  101.2 1.8 %collective-permute-start.9 = (bf16[208,1024]{1,0:T(8,128)(2,1)S(1)}, bf16[208,1024]{1,0:T(8,128)(2,1)S(1)}, u32[]{:S(2)}, u32[]{:S(2)}) collective-permute-start(bf16[208,1024]{1,0:T(8,128)(2,1)S(1)} %get-tuple-element.67), channel_id=1, source_target_pairs={{0,1},{1,0},{2,3},{3,2},{4,5},{5,4},{6,7},{7,6},{8,9},{9,8},{10,11... | collective-permute-start | bytes 1277960 | tf_op jit(solution)/shard_map/ppermute | solution.py:29
  103.6 9.7 %collective-permute-start.10 = (bf16[208,512]{1,0:T(8,128)(2,1)S(1)}, bf16[208,512]{1,0:T(8,128)(2,1)S(1)}, u32[]{:S(2)}, u32[]{:S(2)}) collective-permute-start(bf16[208,512]{1,0:T(8,128)(2,1)S(1)} %get-tuple-element.69), channel_id=1, source_target_pairs={{0,2},{2,0},{1,3},{3,1},{4,6},{6,4},{5,7},{7,5},{8,10},{10,8},{9,1... | collective-permute-start | bytes 638984 | tf_op jit(solution)/shard_map/ppermute | solution.py:29
  104.6 1.2 collective-permute-start.26
  105.8 6.8 %collective-permute-start.27 = (f32[8,128]{1,0:T(8,128)S(1)}, f32[8,128]{1,0:T(8,128)S(1)}, u32[]{:S(2)}, u32[]{:S(2)}) collective-permute-start(f32[8,128]{1,0:T(8,128)S(1)} %add.41), channel_id=1, source_target_pairs={{0,2},{2,0},{1,3},{3,1},{4,6},{6,4},{5,7},{7,5},{8,10},{10,8},{9,1... | collective-permute-start | bytes 12296 | tf_op jit(solution)/shard_map/ppermute | solution.py:29
  112.6 3.6 %collective-permute-start.28 = (f32[8,128]{1,0:T(8,128)S(1)}, f32[8,128]{1,0:T(8,128)S(1)}, u32[]{:S(2)}, u32[]{:S(2)}) collective-permute-start(f32[8,128]{1,0:T(8,128)S(1)} %add.42), channel_id=1, source_target_pairs={{0,16},{16,0},{1,17},{17,1},{2,18},{18,2},{3,19},{19,3},{4,20},{20... | collective-permute-start | bytes 12296 | tf_op jit(solution)/shard_map/ppermute | solution.py:29

commit v4 on v3

--- a/solution.py
+++ b/solution.py
@@ -294,15 +294,15 @@
         b[...] = dot(rows_of(turned_out, chosen, blocks), right[:, D:]).astype(BF)
 
 
-def pieces_kernel(at, own_left, came_left, own_right, came_right, gain_a, *pieces):
+def pieces_kernel(start, at, own_left, came_left, own_right, came_right, gain_a, *pieces):
     tail = own_right[192:ROWS, :].astype(F32) + came_right[192:ROWS, :].astype(F32)
     line = jnp.concatenate([gain_a[k : k + 1, :] for k in range(8)], 1)
     low = jnp.concatenate([tail[5:6], tail[6:7], line, jnp.zeros((5, D), F32)], 0).astype(BF)
-    for to, piece in enumerate(pieces):
-        for first, start, stop in ((0, 0, 3 * WIDTH), (512, 3 * WIDTH, D)):
+    for to, piece in enumerate(pieces, start):
+        for first, low_c, stop in ((0, 0, 3 * WIDTH), (512, 3 * WIDTH, D)):
             r = slice(first + to * 128, first + (to + 1) * 128)
-            piece[0:128, start:stop] = (
-                dot(own_left[r, :], own_right[:, start:stop]) + dot(came_left[r, :], came_right[:, start:stop])
+            piece[0:128, low_c:stop] = (
+                dot(own_left[r, :], own_right[:, low_c:stop]) + dot(came_left[r, :], came_right[:, low_c:stop])
             ).astype(BF)
         piece[128:136, :] = low
 
@@ -486,18 +486,26 @@
         qkv,
         proj,
     )
-    pieces = call(
-        pieces_kernel,
-        [((136, D), BF)] * 4,
-        [],
-        2 * D * ROWS * D,
-        at,
-        own_left,
-        came_left,
-        rows,
-        came_rows,
-        over_z_each(gain_part),
-    )
+    gain_z = over_z_each(gain_part)
+
+    def some_pieces(start, count):
+        def kernel(*refs):
+            pieces_kernel(start, *refs)
+
+        return call(
+            kernel,
+            [((136, D), BF)] * count,
+            [],
+            D * ROWS * D * count // 2,
+            at,
+            own_left,
+            came_left,
+            rows,
+            came_rows,
+            gain_z,
+        )
+
+    pieces = [*some_pieces(0, 1), *some_pieces(1, 3)]
     came = [around(pieces[to], k) for to, k in enumerate(STEPS[:3])]
     mine, sent = call(
         close_pair_kernel,

time: 124 us -> 123 us (level)
  the two profiles are of different devices: /device:TPU:20 before, /device:TPU:8 now
where the time goes in v4:
time: 123 us
  waiting for transfers between devices  50.6 us (41%)
  starting transfers between devices  45.7 us (37%)
  Pallas kernels  21.3 us (17%)
  local copies, waits for them, and re-layouts  3.35 us (3%)
    ppermute x9, waiting for transfers between devices, around(): return lax.ppermute(x, 'x', [(i, (i + step) % 4) for i in range(4)])  25.2 us
    pallas_call x13, Pallas kernels, call(): pl.pallas_call(kernel, out_shape=[jax.ShapeDtypeStruct(s, d) for s, d in...  21.3 us
    ppermute x17, waiting for transfers between devices, swap(): return lax.ppermute(x, axis, SWAP)  15.3 us
    ppermute x17, starting transfers between devices, swap(): return lax.ppermute(x, axis, SWAP)  14.8 us
    ppermute x9, starting transfers between devices, around(): return lax.ppermute(x, 'x', [(i, (i + step) % 4) for i in range(4)])  13.7 us
    ppermute x3, starting transfers between devices, over_z_each(): lax.ppermute(values, 'z', [(k, k ^ step) for k in range(8)])  10.3 us
    all_to_all x1, starting transfers between devices, on_device(): came = lax.all_to_all(total.reshape(8, 16, -1), 'z', 0, 0, tiled=True)  6.92 us
    ppermute x3, waiting for transfers between devices, over_z_each(): lax.ppermute(values, 'z', [(k, k ^ step) for k in range(8)])  6.68 us
  transfers between devices with their start and end apart: 30, of which 19 were waited for; matrix products, arithmetic and copies ran while one was open for 1% of the time, Pallas kernels for 12%

profile of v4, /device:TPU:8, one launch (start us, length us, event | category | flops | bytes accessed | tf_op | source)
XLA Modules:
  0.0 122.6 jit_solution(8402466551579010401)
XLA Ops:
  0.6 2.4 %collective-permute-start.1 = (bf16[197,256]{1,0:T(8,128)(2,1)}, bf16[197,256]{1,0:T(8,128)(2,1)S(1)}, u32[]{:S(2)}, u32[]{:S(2)}) collective-permute-start(bf16[197,256]{1,0:T(8,128)(2,1)} %bitcast.23), channel_id=1, source_target_pairs={{0,2},{2,0},{1,3},{3,1},{4,6},{6,4},{5,7},{7,5},{8,10},{10,8},{9,1... | collective-permute-start | bytes 302600 | tf_op jit(solution)/shard_map/ppermute | solution.py:29
  3.0 1.3 %collective-permute-start.4 = (bf16[197,256]{1,0:T(8,128)(2,1)}, bf16[197,256]{1,0:T(8,128)(2,1)S(1)}, u32[]{:S(2)}, u32[]{:S(2)}) collective-permute-start(bf16[197,256]{1,0:T(8,128)(2,1)} %bitcast.27), channel_id=1, source_target_pairs={{0,2},{2,0},{1,3},{3,1},{4,6},{6,4},{5,7},{7,5},{8,10},{10,8},{9,1... | collective-permute-start | bytes 302600 | tf_op jit(solution)/shard_map/ppermute | solution.py:29
  4.7 2.4 %collective-permute-done.1.f2 = bf16[197,256]{1,0:T(8,128)(2,1)S(1)} collective-permute-done((bf16[197,256]{1,0:T(8,128)(2,1)}, bf16[197,256]{1,0:T(8,128)(2,1)S(1)}, u32[]{:S(2)}, u32[]{:S(2)}) %collective-permute-start.1) | collective-permute-done | bytes 100896 | tf_op jit(solution)/shard_map/ppermute | solution.py:29
  7.1 2.9 %collective-permute-done.4.l2 = bf16[197,256]{1,0:T(8,128)(2,1)S(1)} collective-permute-done((bf16[197,256]{1,0:T(8,128)(2,1)}, bf16[197,256]{1,0:T(8,128)(2,1)S(1)}, u32[]{:S(2)}, u32[]{:S(2)}) %collective-permute-start.4) | collective-permute-done | bytes 100896 | tf_op jit(solution)/shard_map/ppermute | solution.py:29
  10.1 1.2 collective-permute-done.5.l3
  11.4 1.6 %copy-done.6 = bf16[1024,1024]{1,0:T(8,128)(2,1)S(1)} copy-done((bf16[1024,1024]{1,0:T(8,128)(2,1)S(1)}, bf16[1024,1024]{1,0:T(8,128)(2,1)}, u32[]{:S(2)}) %copy-start.6) | copy-done | bytes 2097176
  13.0 1.6 %copy-done.7 = bf16[1024,1024]{1,0:T(8,128)(2,1)S(1)} copy-done((bf16[1024,1024]{1,0:T(8,128)(2,1)S(1)}, bf16[1024,1024]{1,0:T(8,128)(2,1)}, u32[]{:S(2)}) %copy-start.7) | copy-done | bytes 2097176
  14.6 3.8 %shard_map.196 = (f32[208,1024]{1,0:T(8,128)S(1)}, bf16[208,1024]{1,0:T(8,128)(2,1)S(1)}, bf16[208,1024]{1,0:T(8,128)(2,1)S(1)}, bf16[208,1024]{1,0:T(8,128)(2,1...) custom-call(s32[4]{0:T(128)S(1)} %pad_add_fusion.at.refs_0_, bf16[197,256]{1,0:T(8,128)(2,1)S(1)} %bitcast.25, ...), custom_call_target="tpu_custom_call" | custom-call | flops 1744830464 | bytes 4194304 | tf_op jit(solution)/shard_map/pallas_call | solution.py:84
  18.6 1.2 shard_map.203
  19.8 1.6 %collective-permute-start.12 = (bf16[256,1024]{1,0:T(8,128)(2,1)S(1)}, bf16[256,1024]{1,0:T(8,128)(2,1)S(1)}, u32[]{:S(2)}, u32[]{:S(2)}) collective-permute-start(bf16[256,1024]{1,0:T(8,128)(2,1)S(1)} %get-tuple-element.81), channel_id=1, source_target_pairs={{0,4},{4,8},{8,12},{12,0},{1,5},{5,9},{9,13},{13,1},{2,6},{6,10},{... | collective-permute-start | bytes 1572872 | tf_op jit(solution)/shard_map/ppermute | solution.py:33
  21.5 1.6 %collective-permute-start.7 = (bf16[208,1024]{1,0:T(8,128)(2,1)S(1)}, bf16[208,1024]{1,0:T(8,128)(2,1)S(1)}, u32[]{:S(2)}, u32[]{:S(2)}) collective-permute-start(bf16[208,1024]{1,0:T(8,128)(2,1)S(1)} %add_convert_fusion.3), channel_id=1, source_target_pairs={{0,2},{2,0},{1,3},{3,1},{4,6},{6,4},{5,7},{7,5},{8,10},{10,8},{9,1... | collective-permute-start | bytes 1277960 | tf_op jit(solution)/shard_map/ppermute | solution.py:29
  23.1 1.8 %collective-permute-start.15 = (bf16[256,1024]{1,0:T(8,128)(2,1)S(1)}, bf16[256,1024]{1,0:T(8,128)(2,1)S(1)}, u32[]{:S(2)}, u32[]{:S(2)}) collective-permute-start(bf16[256,1024]{1,0:T(8,128)(2,1)S(1)} %get-tuple-element.85), channel_id=1, source_target_pairs={{0,12},{4,0},{8,4},{12,8},{1,13},{5,1},{9,5},{13,9},{2,14},{6,2},{... | collective-permute-start | bytes 1572872 | tf_op jit(solution)/shard_map/ppermute | solution.py:33
  24.9 1.5 %shard_map.204 = (bf16[256,1024]{1,0:T(8,128)(2,1)S(1)}, bf16[256,1024]{1,0:T(8,128)(2,1)S(1)}, bf16[256,1024]{1,0:T(8,128)(2,1)S(1)}, bf16[256,1024]{1,0:T(8,12...) custom-call(s32[4]{0:T(128)S(1)} %pad_add_fusion.at.refs_0_, ...), custom_call_target="tpu_custom_call" | custom-call | flops 654311424 | bytes 4194304 | tf_op jit(solution)/shard_map/pallas_call | solution.py:84
  26.4 1.6 %collective-permute-start.11 = (bf16[256,1024]{1,0:T(8,128)(2,1)S(1)}, bf16[256,1024]{1,0:T(8,128)(2,1)S(1)}, u32[]{:S(2)}, u32[]{:S(2)}) collective-permute-start(bf16[256,1024]{1,0:T(8,128)(2,1)S(1)} %get-tuple-element.79), channel_id=1, source_target_pairs={{0,12},{4,0},{8,4},{12,8},{1,13},{5,1},{9,5},{13,9},{2,14},{6,2},{... | collective-permute-start | bytes 1572872 | tf_op jit(solution)/shard_map/ppermute | solution.py:33
  28.5 7.4 %collective-permute-done.12 = bf16[256,1024]{1,0:T(8,128)(2,1)S(1)} collective-permute-done((bf16[256,1024]{1,0:T(8,128)(2,1)S(1)}, bf16[256,1024]{1,0:T(8,128)(2,1)S(1)}, u32[]{:S(2)}, u32[]{:S(2)}) %collective-permute-start.12) | collective-permute-done | bytes 524320 | tf_op jit(solution)/shard_map/ppermute | solution.py:33
  36.7 1.2 collective-permute-done.15
  38.1 3.0 %collective-permute-start.16 = (bf16[256,1024]{1,0:T(8,128)(2,1)S(1)}, bf16[256,1024]{1,0:T(8,128)(2,1)S(1)}, u32[]{:S(2)}, u32[]{:S(2)}) collective-permute-start(bf16[256,1024]{1,0:T(8,128)(2,1)S(1)} %add_convert_fusion), channel_id=1, source_target_pairs={{0,12},{4,0},{8,4},{12,8},{1,13},{5,1},{9,5},{13,9},{2,14},{6,2},{... | collective-permute-start | bytes 1572872 | tf_op jit(solution)/shard_map/ppermute | solution.py:33
  41.2 2.0 %shard_map.198 = (bf16[208,1024]{1,0:T(8,128)(2,1)S(1)}, bf16[208,1024]{1,0:T(8,128)(2,1)S(1)}, f32[208,1024]{1,0:T(8,128)S(1)}, f32[208,1]{1,0:T(8,128)S(1)}, b...) custom-call(s32[4]{0:T(128)S(1)} %pad_add_fusion.at.refs_0_, ...), custom_call_target="tpu_custom_call" | custom-call | flops 218103808 | bytes 4194304 | tf_op jit(solution)/shard_map/pallas_call | solution.py:84
  43.2 3.3 %shard_map.199.rows.refs_3_ = bf16[208,1024]{1,0:T(8,128)(2,1)S(1)} custom-call(s32[4]{0:T(128)S(1)} %pad_add_fusion.at.refs_0_, bf16[208,1024]{1,0:T(8,128)(2,1)S(1)} %get-tuple-element.59.given, bf16[208,1024]{1,0:T(8,128)(2,1)S(1)} %get-tuple-element.60.back, bf16[3,1024,256]{2,1,0:T(8,128)(2,1)S(1)} %bitcast.21, bf16[1024,256]{1,0:T(8,128)(2,1)S(1)} %copy-done.1, ...), custom_call_target="tpu_custom_call" | custom-call | flops 872415232 | bytes 4194304 | tf_op jit(solution)/shard_map/pallas_call | solution.py:84
  46.4 1.9 %collective-permute-start.19 = (bf16[208,1024]{1,0:T(8,128)(2,1)S(1)}, bf16[208,1024]{1,0:T(8,128)(2,1)S(1)}, u32[]{:S(2)}, u32[]{:S(2)}) collective-permute-start(bf16[208,1024]{1,0:T(8,128)(2,1)S(1)} %shard_map.199.rows.refs_3_), channel_id=1, source_target_pairs={{0,16},{16,0},{1,17},{17,1},{2,18},{18,2},{3,19},{19,3},{4,20},{20... | collective-permute-start | bytes 1277960 | tf_op jit(solution)/shard_map/ppermute | solution.py:29
  49.2 1.3 %collective-permute-start.18 = (bf16[1024,208]{1,0:T(8,128)(2,1)S(1)}, bf16[1024,208]{1,0:T(8,128)(2,1)S(1)}, u32[]{:S(2)}, u32[]{:S(2)}) collective-permute-start(bf16[1024,208]{1,0:T(8,128)(2,1)S(1)} %get-tuple-element.89), channel_id=1, source_target_pairs={{0,16},{16,0},{1,17},{17,1},{2,18},{18,2},{3,19},{19,3},{4,20},{20... | collective-permute-start | bytes 1277960 | tf_op jit(solution)/shard_map/ppermute | solution.py:29
  50.5 7.3 %collective-permute-done.13.a2 = bf16[256,1024]{1,0:T(8,128)(2,1)S(1)} collective-permute-done((bf16[256,1024]{1,0:T(8,128)(2,1)S(1)}, bf16[256,1024]{1,0:T(8,128)(2,1)S(1)}, u32[]{:S(2)}, u32[]{:S(2)}) %collective-permute-start.13) | collective-permute-done | bytes 524320 | tf_op jit(solution)/shard_map/ppermute | solution.py:33
  57.8 1.5 %collective-permute-done.16.b2 = bf16[256,1024]{1,0:T(8,128)(2,1)S(1)} collective-permute-done((bf16[256,1024]{1,0:T(8,128)(2,1)S(1)}, bf16[256,1024]{1,0:T(8,128)(2,1)S(1)}, u32[]{:S(2)}, u32[]{:S(2)}) %collective-permute-start.16) | collective-permute-done | bytes 524320 | tf_op jit(solution)/shard_map/ppermute | solution.py:33
  60.3 1.4 %collective-permute-start.17 = (bf16[128,2048]{1,0:T(8,128)(2,1)S(1)}, bf16[128,2048]{1,0:T(8,128)(2,1)S(1)}, u32[]{:S(2)}, u32[]{:S(2)}) collective-permute-start(bf16[128,2048]{1,0:T(8,128)(2,1)S(1)} %get-tuple-element.87), channel_id=1, source_target_pairs={{0,16},{16,0},{1,17},{17,1},{2,18},{18,2},{3,19},{19,3},{4,20},{20... | collective-permute-start | bytes 1572872 | tf_op jit(solution)/shard_map/ppermute | solution.py:29
  61.7 1.6 %shard_map.200 = (f32[208,1024]{1,0:T(8,128)S(1)}, bf16[208,1024]{1,0:T(8,128)(2,1)S(1)}, f32[8,128]{1,0:T(8,128)S(1)}) custom-call(s32[4]{0:T(128)S(1)} %pad_add_fusion.at.refs_0_, bf16[208,1024]{1,0:T(8,128)(2,1)S(1)} %shard_map.199.rows.refs_3_, f32[208,1024]{1,0:T(8,128)S(1)} %get-tuple-element.63.normed, f32[208,1]{1,0:T(8,128)S(1)} %get-tuple-element.64.spread, ...), custom_call_target="tpu_custom_call" | custom-call | flops 436207616 | bytes 4194304 | tf_op jit(solution)/shard_map/pallas_call | solution.py:84
  63.3 7.3 %collective-permute-start.20 = (f32[8,128]{1,0:T(8,128)S(1)}, f32[8,128]{1,0:T(8,128)S(1)}, u32[]{:S(2)}, u32[]{:S(2)}) collective-permute-start(f32[8,128]{1,0:T(8,128)S(1)} %get-tuple-element.90), channel_id=1, source_target_pairs={{0,128},{32,160},{64,192},{96,224},{128,0},{160,32},{192,64},{224,... | collective-permute-start | bytes 12296 | tf_op jit(solution)/shard_map/ppermute | solution.py:268
  70.6 1.6 %collective-permute-done.20 = f32[8,128]{1,0:T(8,128)S(1)} collective-permute-done((f32[8,128]{1,0:T(8,128)S(1)}, f32[8,128]{1,0:T(8,128)S(1)}, u32[]{:S(2)}, u32[]{:S(2)}) %collective-permute-start.20) | collective-permute-done | bytes 4128 | tf_op jit(solution)/shard_map/ppermute | solution.py:268
  72.2 2.0 %collective-permute-start.21 = (f32[8,128]{1,0:T(8,128)S(1)}, f32[8,128]{1,0:T(8,128)S(1)}, u32[]{:S(2)}, u32[]{:S(2)}) collective-permute-start(f32[8,128]{1,0:T(8,128)S(1)} %add.38), channel_id=1, source_target_pairs={{0,64},{32,96},{64,0},{96,32},{128,192},{160,224},{192,128},{224,1... | collective-permute-start | bytes 12296 | tf_op jit(solution)/shard_map/ppermute | solution.py:268
  74.2 2.5 %collective-permute-done.21 = f32[8,128]{1,0:T(8,128)S(1)} collective-permute-done((f32[8,128]{1,0:T(8,128)S(1)}, f32[8,128]{1,0:T(8,128)S(1)}, u32[]{:S(2)}, u32[]{:S(2)}) %collective-permute-start.21) | collective-permute-done | bytes 4128 | tf_op jit(solution)/shard_map/ppermute | solution.py:268
  77.7 2.6 %collective-permute-done.22 = f32[8,128]{1,0:T(8,128)S(1)} collective-permute-done((f32[8,128]{1,0:T(8,128)S(1)}, f32[8,128]{1,0:T(8,128)S(1)}, u32[]{:S(2)}, u32[]{:S(2)}) %collective-permute-start.22) | collective-permute-done | bytes 4128 | tf_op jit(solution)/shard_map/ppermute | solution.py:268
  80.3 1.1 shard_map.206
  81.4 1.6 %collective-permute-start.24 = (bf16[136,1024]{1,0:T(8,128)(2,1)S(1)}, bf16[136,1024]{1,0:T(8,128)(2,1)S(1)}, u32[]{:S(2)}, u32[]{:S(2)}) collective-permute-start(bf16[136,1024]{1,0:T(8,128)(2,1)S(1)} %get-tuple-element.92), channel_id=1, source_target_pairs={{0,4},{4,8},{8,12},{12,0},{1,5},{5,9},{9,13},{13,1},{2,6},{6,10},{... | collective-permute-start | bytes 835592 | tf_op jit(solution)/shard_map/ppermute | solution.py:33
  83.0 1.8 %collective-permute-start.25 = (bf16[136,1024]{1,0:T(8,128)(2,1)S(1)}, bf16[136,1024]{1,0:T(8,128)(2,1)S(1)}, u32[]{:S(2)}, u32[]{:S(2)}) collective-permute-start(bf16[136,1024]{1,0:T(8,128)(2,1)S(1)} %get-tuple-element.93), channel_id=1, source_target_pairs={{0,12},{4,0},{8,4},{12,8},{1,13},{5,1},{9,5},{13,9},{2,14},{6,2},{... | collective-permute-start | bytes 835592 | tf_op jit(solution)/shard_map/ppermute | solution.py:33
  85.6 1.6 %collective-permute-start.23 = (bf16[136,1024]{1,0:T(8,128)(2,1)S(1)}, bf16[136,1024]{1,0:T(8,128)(2,1)S(1)}, u32[]{:S(2)}, u32[]{:S(2)}) collective-permute-start(bf16[136,1024]{1,0:T(8,128)(2,1)S(1)} %shard_map.207), channel_id=1, source_target_pairs={{0,8},{4,12},{8,0},{12,4},{1,9},{5,13},{9,1},{13,5},{2,10},{6,14},... | collective-permute-start | bytes 835592 | tf_op jit(solution)/shard_map/ppermute | solution.py:33
  87.2 4.1 %collective-permute-done.24.c = bf16[136,1024]{1,0:T(8,128)(2,1)S(1)} collective-permute-done((bf16[136,1024]{1,0:T(8,128)(2,1)S(1)}, bf16[136,1024]{1,0:T(8,128)(2,1)S(1)}, u32[]{:S(2)}, u32[]{:S(2)}) %collective-permute-start.24) | collective-permute-done | bytes 278560 | tf_op jit(solution)/shard_map/ppermute | solution.py:33
  91.3 1.4 %collective-permute-done.25.d = bf16[136,1024]{1,0:T(8,128)(2,1)S(1)} collective-permute-done((bf16[136,1024]{1,0:T(8,128)(2,1)S(1)}, bf16[136,1024]{1,0:T(8,128)(2,1)S(1)}, u32[]{:S(2)}, u32[]{:S(2)}) %collective-permute-start.25) | collective-permute-done | bytes 278560 | tf_op jit(solution)/shard_map/ppermute | solution.py:33
  92.6 1.6 %collective-permute-done.23.b = bf16[136,1024]{1,0:T(8,128)(2,1)S(1)} collective-permute-done((bf16[136,1024]{1,0:T(8,128)(2,1)S(1)}, bf16[136,1024]{1,0:T(8,128)(2,1)S(1)}, u32[]{:S(2)}, u32[]{:S(2)}) %collective-permute-start.23) | collective-permute-done | bytes 278560 | tf_op jit(solution)/shard_map/ppermute | solution.py:33
  94.3 1.7 %shard_map.208 = (bf16[128,3200]{1,0:T(8,128)(2,1)}, f32[8,128]{1,0:T(8,128)S(1)}) custom-call(s32[4]{0:T(128)S(1)} %pad_add_fusion.at.refs_0_, bf16[128,2048]{1,0:T(8,128)(2,1)S(1)} %get-tuple-element.86.keep, bf16[128,2048]{1,0:T(8,128)(2,1)S(1)} %collective-permute-done.17.came, bf16[136,1024]{1,0:T(8,128)(2,1)S(1)} %get-tuple-element.91.a, ...), custom_call_target="tpu_custom_call" | custom-call | flops 4194304 | bytes 4194304 | tf_op jit(solution)/shard_map/pallas_call | solution.py:84
  96.0 6.9 %all-to-all-start = ((bf16[8,16,3200]{2,1,0:T(8,128)(2,1)}), bf16[8,16,3200]{2,1,0:T(8,128)(2,1)S(1)}, u32[]{:S(2)}, u32[]{:S(2)}) async-start(bf16[8,16,3200]{2,1,0:T(8,128)(2,1)} %bitcast.16), calls=%async_computation | async-start | bytes 1638400 | tf_op jit(solution)/shard_map/all_to_all | solution.py:543
  102.9 1.8 %collective-permute-done.9.came = bf16[208,1024]{1,0:T(8,128)(2,1)S(1)} collective-permute-done((bf16[208,1024]{1,0:T(8,128)(2,1)S(1)}, bf16[208,1024]{1,0:T(8,128)(2,1)S(1)}, u32[]{:S(2)}, u32[]{:S(2)}) %collective-permute-start.9) | collective-permute-done | bytes 426016 | tf_op jit(solution)/shard_map/ppermute | solution.py:29
  105.3 1.5 %collective-permute-start.10 = (bf16[208,512]{1,0:T(8,128)(2,1)S(1)}, bf16[208,512]{1,0:T(8,128)(2,1)S(1)}, u32[]{:S(2)}, u32[]{:S(2)}) collective-permute-start(bf16[208,512]{1,0:T(8,128)(2,1)S(1)} %get-tuple-element.68), channel_id=1, source_target_pairs={{0,2},{2,0},{1,3},{3,1},{4,6},{6,4},{5,7},{7,5},{8,10},{10,8},{9,1... | collective-permute-start | bytes 638984 | tf_op jit(solution)/shard_map/ppermute | solution.py:29
  106.8 1.2 collective-permute-done.26
  108.0 2.1 %collective-permute-start.27 = (f32[8,128]{1,0:T(8,128)S(1)}, f32[8,128]{1,0:T(8,128)S(1)}, u32[]{:S(2)}, u32[]{:S(2)}) collective-permute-start(f32[8,128]{1,0:T(8,128)S(1)} %add.41), channel_id=1, source_target_pairs={{0,2},{2,0},{1,3},{3,1},{4,6},{6,4},{5,7},{7,5},{8,10},{10,8},{9,1... | collective-permute-start | bytes 12296 | tf_op jit(solution)/shard_map/ppermute | solution.py:29
  110.1 4.2 %collective-permute-done.27 = f32[8,128]{1,0:T(8,128)S(1)} collective-permute-done((f32[8,128]{1,0:T(8,128)S(1)}, f32[8,128]{1,0:T(8,128)S(1)}, u32[]{:S(2)}, u32[]{:S(2)}) %collective-permute-start.27) | collective-permute-done | bytes 4128 | tf_op jit(solution)/shard_map/ppermute | solution.py:29
  115.0 1.3 %shard_map.202 = (bf16[197,256]{1,0:T(8,128)(2,1)}, bf16[197,256]{1,0:T(8,128)(2,1)}) custom-call(s32[4]{0:T(128)S(1)} %pad_add_fusion.at.refs_0_, f32[208,512]{1,0:T(8,128)S(1)} %get-tuple-element.67.mine, bf16[208,512]{1,0:T(8,128)(2,1)S(1)} %collective-permute-done.10.came, bf16[197,256]{1,0:T(8,128)(2,1)S(1)} %bitcast.26, bf16[197,256]{1,0:T(8,128)(2,1)S(1)} %bitcast.30), custom_call_target="tpu_custom_call" | custom-call | flops 4194304 | bytes 4194304 | tf_op jit(solution)/shard_map/pallas_call | solution.py:84
  116.3 1.6 %collective-permute-done.28 = f32[8,128]{1,0:T(8,128)S(1)} collective-permute-done((f32[8,128]{1,0:T(8,128)S(1)}, f32[8,128]{1,0:T(8,128)S(1)}, u32[]{:S(2)}, u32[]{:S(2)}) %collective-permute-start.28) | collective-permute-done | bytes 4128 | tf_op jit(solution)/shard_map/ppermute | solution.py:29
  117.9 3.4 %all-to-all-done.came = bf16[8,16,3200]{2,1,0:T(8,128)(2,1)S(1)} async-done(((bf16[8,16,3200]{2,1,0:T(8,128)(2,1)}), bf16[8,16,3200]{2,1,0:T(8,128)(2,1)S(1)}, u32[]{:S(2)}, u32[]{:S(2)}) %all-to-all-start) | async-done | bytes 819232 | tf_op jit(solution)/shard_map/all_to_all | solution.py:543
  121.3 1.3 %shard_map.209 = (f32[16,1024]{1,0:T(8,128)}, f32[16,1024]{1,0:T(8,128)}, f32[1,1024]{1,0:T(1,128)}, f32[3,16,256]{2,1,0:T(8,128)}, f32[16,256]{1,0:T(8,128)}, /*index=5*/f32[1,256]{1,0:T(1,128)}, f32[1,256]{1,0:T(1,128)}) custom-call(s32[4]{0:T(128)S(1)} %pad_add_fusion.at.refs_0_, bf16[8,16,3200]{2,1,0:T(8,128)(2,1)S(1)} %all-to-all-done.came, ...), custom_call_target="tpu_custom_call" | custom-call | flops 1048576 | bytes 4194304 | tf_op jit(solution)/shard_map/pallas_call | solution.py:84
  (64 shorter events, 7.3 us)
Async XLA Ops:
  0.6 6.5 %collective-permute-start.1 = (bf16[197,256]{1,0:T(8,128)(2,1)}, bf16[197,256]{1,0:T(8,128)(2,1)S(1)}, u32[]{:S(2)}, u32[]{:S(2)}) collective-permute-start(bf16[197,256]{1,0:T(8,128)(2,1)} %bitcast.23), channel_id=1, source_target_pairs={{0,2},{2,0},{1,3},{3,1},{4,6},{6,4},{5,7},{7,5},{8,10},{10,8},{9,1... | collective-permute-start | bytes 302600 | tf_op jit(solution)/shard_map/ppermute | solution.py:29
  3.0 7.1 %collective-permute-start = (bf16[197,256]{1,0:T(8,128)(2,1)}, bf16[197,256]{1,0:T(8,128)(2,1)S(1)}, u32[]{:S(2)}, u32[]{:S(2)}) collective-permute-start(bf16[197,256]{1,0:T(8,128)(2,1)} %bitcast.24), channel_id=1, source_target_pairs={{0,1},{1,0},{2,3},{3,2},{4,5},{5,4},{6,7},{7,6},{8,9},{9,8},{10,11... | collective-permute-start | bytes 302600 | tf_op jit(solution)/shard_map/ppermute | solution.py:29
  3.0 1.5 %copy-start.10 = (f32[1024]{0:T(1024)S(1)}, f32[1024]{0:T(1024)}, u32[]{:S(2)}) copy-start(f32[1024]{0:T(1024)} %param.20) | copy-start | bytes 12292
  3.0 1.5 %copy-start.11 = (f32[1024]{0:T(1024)S(1)}, f32[1024]{0:T(1024)}, u32[]{:S(2)}) copy-start(f32[1024]{0:T(1024)} %param.16) | copy-start | bytes 12292
  3.0 1.6 %copy-start.5 = (bf16[1024,1024]{1,0:T(8,128)(2,1)S(1)}, bf16[1024,1024]{1,0:T(8,128)(2,1)}, u32[]{:S(2)}) copy-start(bf16[1024,1024]{1,0:T(8,128)(2,1)} %outer.1) | copy-start | bytes 6291460
  3.0 7.0 %collective-permute-start.4 = (bf16[197,256]{1,0:T(8,128)(2,1)}, bf16[197,256]{1,0:T(8,128)(2,1)S(1)}, u32[]{:S(2)}, u32[]{:S(2)}) collective-permute-start(bf16[197,256]{1,0:T(8,128)(2,1)} %bitcast.27), channel_id=1, source_target_pairs={{0,2},{2,0},{1,3},{3,1},{4,6},{6,4},{5,7},{7,5},{8,10},{10,8},{9,1... | collective-permute-start | bytes 302600 | tf_op jit(solution)/shard_map/ppermute | solution.py:29
  4.4 5.8 %collective-permute-start.3 = (bf16[197,256]{1,0:T(8,128)(2,1)}, bf16[197,256]{1,0:T(8,128)(2,1)S(1)}, u32[]{:S(2)}, u32[]{:S(2)}) collective-permute-start(bf16[197,256]{1,0:T(8,128)(2,1)} %bitcast.28), channel_id=1, source_target_pairs={{0,1},{1,0},{2,3},{3,2},{4,5},{5,4},{6,7},{7,6},{8,9},{9,8},{10,11... | collective-permute-start | bytes 302600 | tf_op jit(solution)/shard_map/ppermute | solution.py:29
  4.7 6.7 %copy-start.2 = (bf16[1,197,256]{2,1,0:T(8,128)(2,1)S(1)}, bf16[1,197,256]{2,1,0:T(8,128)(2,1)}, u32[]{:S(2)}) copy-start(bf16[1,197,256]{2,1,0:T(8,128)(2,1)} %param.11) | copy-start | bytes 302596
  4.7 6.7 %copy-start.3 = (bf16[1,197,256]{2,1,0:T(8,128)(2,1)S(1)}, bf16[1,197,256]{2,1,0:T(8,128)(2,1)}, u32[]{:S(2)}) copy-start(bf16[1,197,256]{2,1,0:T(8,128)(2,1)} %param.14) | copy-start | bytes 302596
  4.7 6.7 %copy-start.8 = (bf16[1,197,256]{2,1,0:T(8,128)(2,1)S(1)}, bf16[1,197,256]{2,1,0:T(8,128)(2,1)}, u32[]{:S(2)}) copy-start(bf16[1,197,256]{2,1,0:T(8,128)(2,1)} %param.12) | copy-start | bytes 302596
  4.7 6.7 %copy-start.9 = (bf16[1,197,256]{2,1,0:T(8,128)(2,1)S(1)}, bf16[1,197,256]{2,1,0:T(8,128)(2,1)}, u32[]{:S(2)}) copy-start(bf16[1,197,256]{2,1,0:T(8,128)(2,1)} %param.13) | copy-start | bytes 302596
  7.1 3.0 %collective-permute-start.2 = (bf16[197,256]{1,0:T(8,128)(2,1)S(1)}, bf16[197,256]{1,0:T(8,128)(2,1)S(1)}, u32[]{:S(2)}, u32[]{:S(2)}) collective-permute-start(bf16[197,256]{1,0:T(8,128)(2,1)S(1)} %collective-permute-done.1.f2), channel_id=1, source_target_pairs={{0,1},{1,0},{2,3},{3,2},{4,5},{5,4},{6,7},{7,6},{8,9},{9,8},{10,11... | collective-permute-start | bytes 302600 | tf_op jit(solution)/shard_map/ppermute | solution.py:29
  10.0 1.3 %collective-permute-start.5 = (bf16[197,256]{1,0:T(8,128)(2,1)S(1)}, bf16[197,256]{1,0:T(8,128)(2,1)S(1)}, u32[]{:S(2)}, u32[]{:S(2)}) collective-permute-start(bf16[197,256]{1,0:T(8,128)(2,1)S(1)} %collective-permute-done.4.l2), channel_id=1, source_target_pairs={{0,1},{1,0},{2,3},{3,2},{4,5},{5,4},{6,7},{7,6},{8,9},{9,8},{10,11... | collective-permute-start | bytes 302600 | tf_op jit(solution)/shard_map/ppermute | solution.py:29
  11.4 1.6 %copy-start.6 = (bf16[1024,1024]{1,0:T(8,128)(2,1)S(1)}, bf16[1024,1024]{1,0:T(8,128)(2,1)}, u32[]{:S(2)}) copy-start(bf16[1024,1024]{1,0:T(8,128)(2,1)} %outer.1) | copy-start | bytes 6291460
  13.0 1.6 %copy-start.7 = (bf16[1024,1024]{1,0:T(8,128)(2,1)S(1)}, bf16[1024,1024]{1,0:T(8,128)(2,1)}, u32[]{:S(2)}) copy-start(bf16[1024,1024]{1,0:T(8,128)(2,1)} %inner.1) | copy-start | bytes 6291460
  18.4 3.0 %collective-permute-start.6 = (bf16[208,1024]{1,0:T(8,128)(2,1)S(1)}, bf16[208,1024]{1,0:T(8,128)(2,1)S(1)}, u32[]{:S(2)}, u32[]{:S(2)}) collective-permute-start(bf16[208,1024]{1,0:T(8,128)(2,1)S(1)} %get-tuple-element.58), channel_id=1, source_target_pairs={{0,1},{1,0},{2,3},{3,2},{4,5},{5,4},{6,7},{7,6},{8,9},{9,8},{10,11... | collective-permute-start | bytes 1277960 | tf_op jit(solution)/shard_map/ppermute | solution.py:29
  19.8 16.1 %collective-permute-start.12 = (bf16[256,1024]{1,0:T(8,128)(2,1)S(1)}, bf16[256,1024]{1,0:T(8,128)(2,1)S(1)}, u32[]{:S(2)}, u32[]{:S(2)}) collective-permute-start(bf16[256,1024]{1,0:T(8,128)(2,1)S(1)} %get-tuple-element.81), channel_id=1, source_target_pairs={{0,4},{4,8},{8,12},{12,0},{1,5},{5,9},{9,13},{13,1},{2,6},{6,10},{... | collective-permute-start | bytes 1572872 | tf_op jit(solution)/shard_map/ppermute | solution.py:33
  21.5 15.0 %collective-permute-start.7 = (bf16[208,1024]{1,0:T(8,128)(2,1)S(1)}, bf16[208,1024]{1,0:T(8,128)(2,1)S(1)}, u32[]{:S(2)}, u32[]{:S(2)}) collective-permute-start(bf16[208,1024]{1,0:T(8,128)(2,1)S(1)} %add_convert_fusion.3), channel_id=1, source_target_pairs={{0,2},{2,0},{1,3},{3,1},{4,6},{6,4},{5,7},{7,5},{8,10},{10,8},{9,1... | collective-permute-start | bytes 1277960 | tf_op jit(solution)/shard_map/ppermute | solution.py:29
  23.1 14.8 %collective-permute-start.15 = (bf16[256,1024]{1,0:T(8,128)(2,1)S(1)}, bf16[256,1024]{1,0:T(8,128)(2,1)S(1)}, u32[]{:S(2)}, u32[]{:S(2)}) collective-permute-start(bf16[256,1024]{1,0:T(8,128)(2,1)S(1)} %get-tuple-element.85), channel_id=1, source_target_pairs={{0,12},{4,0},{8,4},{12,8},{1,13},{5,1},{9,5},{13,9},{2,14},{6,2},{... | collective-permute-start | bytes 1572872 | tf_op jit(solution)/shard_map/ppermute | solution.py:33
  26.4 22.7 %collective-permute-start.11 = (bf16[256,1024]{1,0:T(8,128)(2,1)S(1)}, bf16[256,1024]{1,0:T(8,128)(2,1)S(1)}, u32[]{:S(2)}, u32[]{:S(2)}) collective-permute-start(bf16[256,1024]{1,0:T(8,128)(2,1)S(1)} %get-tuple-element.79), channel_id=1, source_target_pairs={{0,12},{4,0},{8,4},{12,8},{1,13},{5,1},{9,5},{13,9},{2,14},{6,2},{... | collective-permute-start | bytes 1572872 | tf_op jit(solution)/shard_map/ppermute | solution.py:33
  28.1 22.4 %collective-permute-start.14 = (bf16[256,1024]{1,0:T(8,128)(2,1)S(1)}, bf16[256,1024]{1,0:T(8,128)(2,1)S(1)}, u32[]{:S(2)}, u32[]{:S(2)}) collective-permute-start(bf16[256,1024]{1,0:T(8,128)(2,1)S(1)} %get-tuple-element.83), channel_id=1, source_target_pairs={{0,4},{4,8},{8,12},{12,0},{1,5},{5,9},{9,13},{13,1},{2,6},{6,10},{... | collective-permute-start | bytes 1572872 | tf_op jit(solution)/shard_map/ppermute | solution.py:33
  35.9 5.3 %copy-start.4 = (f32[1024]{0:T(1024)S(1)}, f32[1024]{0:T(1024)}, u32[]{:S(2)}) copy-start(f32[1024]{0:T(1024)} %param.15) | copy-start | bytes 12292
  36.1 7.1 %copy-start = (bf16[1024,3,256]{2,0,1:T(8,128)(2,1)S(1)}, bf16[1024,3,256]{2,0,1:T(8,128)(2,1)}, u32[]{:S(2)}) copy-start(bf16[1024,3,256]{2,0,1:T(8,128)(2,1)} %param.17) | copy-start | bytes 4718596
  36.1 7.1 %copy-start.1 = (bf16[1024,256]{1,0:T(8,128)(2,1)S(1)}, bf16[1024,256]{1,0:T(8,128)(2,1)}, u32[]{:S(2)}) copy-start(bf16[1024,256]{1,0:T(8,128)(2,1)} %proj.3) | copy-start | bytes 1572868
  36.1 21.6 %collective-permute-start.13 = (bf16[256,1024]{1,0:T(8,128)(2,1)S(1)}, bf16[256,1024]{1,0:T(8,128)(2,1)S(1)}, u32[]{:S(2)}, u32[]{:S(2)}) collective-permute-start(bf16[256,1024]{1,0:T(8,128)(2,1)S(1)} %add_convert_fusion.1), channel_id=1, source_target_pairs={{0,4},{4,8},{8,12},{12,0},{1,5},{5,9},{9,13},{13,1},{2,6},{6,10},{... | collective-permute-start | bytes 1572872 | tf_op jit(solution)/shard_map/ppermute | solution.py:33
  36.6 4.5 %collective-permute-start.8 = (bf16[208,1024]{1,0:T(8,128)(2,1)S(1)}, bf16[208,1024]{1,0:T(8,128)(2,1)S(1)}, u32[]{:S(2)}, u32[]{:S(2)}) collective-permute-start(bf16[208,1024]{1,0:T(8,128)(2,1)S(1)} %add_convert_fusion.2.done), channel_id=1, source_target_pairs={{0,1},{1,0},{2,3},{3,2},{4,5},{5,4},{6,7},{7,6},{8,9},{9,8},{10,11... | collective-permute-start | bytes 1277960 | tf_op jit(solution)/shard_map/ppermute | solution.py:29
  38.1 21.1 %collective-permute-start.16 = (bf16[256,1024]{1,0:T(8,128)(2,1)S(1)}, bf16[256,1024]{1,0:T(8,128)(2,1)S(1)}, u32[]{:S(2)}, u32[]{:S(2)}) collective-permute-start(bf16[256,1024]{1,0:T(8,128)(2,1)S(1)} %add_convert_fusion), channel_id=1, source_target_pairs={{0,12},{4,0},{8,4},{12,8},{1,13},{5,1},{9,5},{13,9},{2,14},{6,2},{... | collective-permute-start | bytes 1572872 | tf_op jit(solution)/shard_map/ppermute | solution.py:33
  46.4 33.9 %collective-permute-start.19 = (bf16[208,1024]{1,0:T(8,128)(2,1)S(1)}, bf16[208,1024]{1,0:T(8,128)(2,1)S(1)}, u32[]{:S(2)}, u32[]{:S(2)}) collective-permute-start(bf16[208,1024]{1,0:T(8,128)(2,1)S(1)} %shard_map.199.rows.refs_3_), channel_id=1, source_target_pairs={{0,16},{16,0},{1,17},{17,1},{2,18},{18,2},{3,19},{19,3},{4,20},{20... | collective-permute-start | bytes 1277960 | tf_op jit(solution)/shard_map/ppermute | solution.py:29
  49.2 31.1 %collective-permute-start.18 = (bf16[1024,208]{1,0:T(8,128)(2,1)S(1)}, bf16[1024,208]{1,0:T(8,128)(2,1)S(1)}, u32[]{:S(2)}, u32[]{:S(2)}) collective-permute-start(bf16[1024,208]{1,0:T(8,128)(2,1)S(1)} %get-tuple-element.89), channel_id=1, source_target_pairs={{0,16},{16,0},{1,17},{17,1},{2,18},{18,2},{3,19},{19,3},{4,20},{20... | collective-permute-start | bytes 1277960 | tf_op jit(solution)/shard_map/ppermute | solution.py:29
  60.3 26.9 %collective-permute-start.17 = (bf16[128,2048]{1,0:T(8,128)(2,1)S(1)}, bf16[128,2048]{1,0:T(8,128)(2,1)S(1)}, u32[]{:S(2)}, u32[]{:S(2)}) collective-permute-start(bf16[128,2048]{1,0:T(8,128)(2,1)S(1)} %get-tuple-element.87), channel_id=1, source_target_pairs={{0,16},{16,0},{1,17},{17,1},{2,18},{18,2},{3,19},{19,3},{4,20},{20... | collective-permute-start | bytes 1572872 | tf_op jit(solution)/shard_map/ppermute | solution.py:29
  63.3 8.9 %collective-permute-start.20 = (f32[8,128]{1,0:T(8,128)S(1)}, f32[8,128]{1,0:T(8,128)S(1)}, u32[]{:S(2)}, u32[]{:S(2)}) collective-permute-start(f32[8,128]{1,0:T(8,128)S(1)} %get-tuple-element.90), channel_id=1, source_target_pairs={{0,128},{32,160},{64,192},{96,224},{128,0},{160,32},{192,64},{224,... | collective-permute-start | bytes 12296 | tf_op jit(solution)/shard_map/ppermute | solution.py:268
  72.2 4.5 %collective-permute-start.21 = (f32[8,128]{1,0:T(8,128)S(1)}, f32[8,128]{1,0:T(8,128)S(1)}, u32[]{:S(2)}, u32[]{:S(2)}) collective-permute-start(f32[8,128]{1,0:T(8,128)S(1)} %add.38), channel_id=1, source_target_pairs={{0,64},{32,96},{64,0},{96,32},{128,192},{160,224},{192,128},{224,1... | collective-permute-start | bytes 12296 | tf_op jit(solution)/shard_map/ppermute | solution.py:268
  76.7 3.6 %collective-permute-start.22 = (f32[8,128]{1,0:T(8,128)S(1)}, f32[8,128]{1,0:T(8,128)S(1)}, u32[]{:S(2)}, u32[]{:S(2)}) collective-permute-start(f32[8,128]{1,0:T(8,128)S(1)} %add.39), channel_id=1, source_target_pairs={{0,32},{32,0},{64,96},{96,64},{128,160},{160,128},{192,224},{224,1... | collective-permute-start | bytes 12296 | tf_op jit(solution)/shard_map/ppermute | solution.py:268
  81.4 9.8 %collective-permute-start.24 = (bf16[136,1024]{1,0:T(8,128)(2,1)S(1)}, bf16[136,1024]{1,0:T(8,128)(2,1)S(1)}, u32[]{:S(2)}, u32[]{:S(2)}) collective-permute-start(bf16[136,1024]{1,0:T(8,128)(2,1)S(1)} %get-tuple-element.92), channel_id=1, source_target_pairs={{0,4},{4,8},{8,12},{12,0},{1,5},{5,9},{9,13},{13,1},{2,6},{6,10},{... | collective-permute-start | bytes 835592 | tf_op jit(solution)/shard_map/ppermute | solution.py:33
  83.0 9.6 %collective-permute-start.25 = (bf16[136,1024]{1,0:T(8,128)(2,1)S(1)}, bf16[136,1024]{1,0:T(8,128)(2,1)S(1)}, u32[]{:S(2)}, u32[]{:S(2)}) collective-permute-start(bf16[136,1024]{1,0:T(8,128)(2,1)S(1)} %get-tuple-element.93), channel_id=1, source_target_pairs={{0,12},{4,0},{8,4},{12,8},{1,13},{5,1},{9,5},{13,9},{2,14},{6,2},{... | collective-permute-start | bytes 835592 | tf_op jit(solution)/shard_map/ppermute | solution.py:33
  85.6 8.7 %collective-permute-start.23 = (bf16[136,1024]{1,0:T(8,128)(2,1)S(1)}, bf16[136,1024]{1,0:T(8,128)(2,1)S(1)}, u32[]{:S(2)}, u32[]{:S(2)}) collective-permute-start(bf16[136,1024]{1,0:T(8,128)(2,1)S(1)} %shard_map.207), channel_id=1, source_target_pairs={{0,8},{4,12},{8,0},{12,4},{1,9},{5,13},{9,1},{13,5},{2,10},{6,14},... | collective-permute-start | bytes 835592 | tf_op jit(solution)/shard_map/ppermute | solution.py:33
  96.0 25.4 %all-to-all-start = ((bf16[8,16,3200]{2,1,0:T(8,128)(2,1)}), bf16[8,16,3200]{2,1,0:T(8,128)(2,1)S(1)}, u32[]{:S(2)}, u32[]{:S(2)}) async-start(bf16[8,16,3200]{2,1,0:T(8,128)(2,1)} %bitcast.16), calls=%async_computation | async-start | bytes 1638400 | tf_op jit(solution)/shard_map/all_to_all | solution.py:543
  102.9 1.8 %collective-permute-start.9 = (bf16[208,1024]{1,0:T(8,128)(2,1)S(1)}, bf16[208,1024]{1,0:T(8,128)(2,1)S(1)}, u32[]{:S(2)}, u32[]{:S(2)}) collective-permute-start(bf16[208,1024]{1,0:T(8,128)(2,1)S(1)} %get-tuple-element.66), channel_id=1, source_target_pairs={{0,1},{1,0},{2,3},{3,2},{4,5},{5,4},{6,7},{7,6},{8,9},{9,8},{10,11... | collective-permute-start | bytes 1277960 | tf_op jit(solution)/shard_map/ppermute | solution.py:29
  105.3 9.7 %collective-permute-start.10 = (bf16[208,512]{1,0:T(8,128)(2,1)S(1)}, bf16[208,512]{1,0:T(8,128)(2,1)S(1)}, u32[]{:S(2)}, u32[]{:S(2)}) collective-permute-start(bf16[208,512]{1,0:T(8,128)(2,1)S(1)} %get-tuple-element.68), channel_id=1, source_target_pairs={{0,2},{2,0},{1,3},{3,1},{4,6},{6,4},{5,7},{7,5},{8,10},{10,8},{9,1... | collective-permute-start | bytes 638984 | tf_op jit(solution)/shard_map/ppermute | solution.py:29
  106.8 1.2 collective-permute-start.26
  108.0 6.3 %collective-permute-start.27 = (f32[8,128]{1,0:T(8,128)S(1)}, f32[8,128]{1,0:T(8,128)S(1)}, u32[]{:S(2)}, u32[]{:S(2)}) collective-permute-start(f32[8,128]{1,0:T(8,128)S(1)} %add.41), channel_id=1, source_target_pairs={{0,2},{2,0},{1,3},{3,1},{4,6},{6,4},{5,7},{7,5},{8,10},{10,8},{9,1... | collective-permute-start | bytes 12296 | tf_op jit(solution)/shard_map/ppermute | solution.py:29
  114.3 3.6 %collective-permute-start.28 = (f32[8,128]{1,0:T(8,128)S(1)}, f32[8,128]{1,0:T(8,128)S(1)}, u32[]{:S(2)}, u32[]{:S(2)}) collective-permute-start(f32[8,128]{1,0:T(8,128)S(1)} %add.42), channel_id=1, source_target_pairs={{0,16},{16,0},{1,17},{17,1},{2,18},{18,2},{3,19},{19,3},{4,20},{20... | collective-permute-start | bytes 12296 | tf_op jit(solution)/shard_map/ppermute | solution.py:29
